TPU v7x, 32 devices: a whole 2x2x4 slice. The times are simulated.
32 devices in a mesh: ctx: 8 (over z, x), uly: 4 (over y, core).
Axes of the slice: x: 2, y: 2, z: 4, core: 2. Of those that a mesh axis runs over, the one named last changes fastest.
Arguments:
- tokens: bfloat16 [4096, 2304], P(('ctx', 'uly')), may hold values from -6 to 6
- cotangent: bfloat16 [4096, 2304], P(('ctx', 'uly')), may hold values from -6 to 6
- span_order: int32 [16], replicated, may hold values from 0 to 15, as said below
- segments: int32 [4096], replicated, may hold values from 0 to 1, as said below
- w_query: bfloat16 [2304, 2048], P(('ctx', 'uly')), may hold values from -0.125 to 0.125
- w_key: bfloat16 [2304, 1024], P(('ctx', 'uly')), may hold values from -0.125 to 0.125
- w_value: bfloat16 [2304, 1024], P(('ctx', 'uly')), may hold values from -0.125 to 0.125
- w_out: bfloat16 [2304, 2048], P('ctx', 'uly'), may hold values from -0.125 to 0.125
- w_gate: bfloat16 [2304, 9216], P('ctx', 'uly'), may hold values from -0.125 to 0.125
- w_up: bfloat16 [2304, 9216], P('ctx', 'uly'), may hold values from -0.125 to 0.125
- w_down: bfloat16 [2304, 9216], P('ctx', 'uly'), may hold values from -0.0625 to 0.0625
- gain_attn_in: bfloat16 [2304], P(('ctx', 'uly')), may hold values from 0.099609375 to 1.8984375
- gain_attn_out: bfloat16 [2304], P(('ctx', 'uly')), may hold values from 0.099609375 to 1.8984375
- gain_ffn_in: bfloat16 [2304], P(('ctx', 'uly')), may hold values from 0.099609375 to 1.8984375
- gain_ffn_out: bfloat16 [2304], P(('ctx', 'uly')), may hold values from 0.099609375 to 1.8984375
Outputs:
- block_out: bfloat16 [4096, 2304], P(('ctx', 'uly'))
- grad_tokens: float32 [4096, 2304], P(('ctx', 'uly'))
- grad_query: float32 [2304, 2048], P(('ctx', 'uly'))
- grad_key: float32 [2304, 1024], P(('ctx', 'uly'))
- grad_value: float32 [2304, 1024], P(('ctx', 'uly'))
- grad_outproj: float32 [2304, 2048], P('ctx', 'uly')
- grad_gate: float32 [2304, 9216], P('ctx', 'uly')
- grad_up: float32 [2304, 9216], P('ctx', 'uly')
- grad_down: float32 [2304, 9216], P('ctx', 'uly')
- grad_gain_attn_in: float32 [2304], P(('ctx', 'uly'))
- grad_gain_attn_out: float32 [2304], P(('ctx', 'uly'))
- grad_gain_ffn_in: float32 [2304], P(('ctx', 'uly'))
- grad_gain_ffn_out: float32 [2304], P(('ctx', 'uly'))
Inputs may be any that keep to these rules, and one draw needn't show every extreme that they name: `span_order`: A permutation; entries 2c and 2c + 1 are two blocks of positions that sum to 15. `segments`: never falls along the stream; 2 sequences, each of at least 1024 positions.
All inputs are finite; a program needn't handle non-finite values.
Results may differ from a plain program's by a relative error of at most 0.029.
Values may be sent and summed in bfloat16 or wider, within the bound.
A program may use at most 448 MiB of HBM per device.

v0:
```python
import functools

import jax
import jax.numpy as jnp
from jax import lax
from jax.experimental import pallas as pl
from jax.experimental.pallas import tpu as pltpu
from jax.sharding import PartitionSpec as P


HEAD_DIM = 256
AXES = ("ctx", "uly")

norm_eps = 1e-06
soft_cap = 50.0
rotary_base = 10000.0
gelu_coef = 0.7978845608028654
cubic_coef = 0.044715


BURST, LAG = 1, 1

bf16 = jnp.bfloat16
f32 = jnp.float32


def rms_scale(values):
    return lax.rsqrt(jnp.mean(values * values, axis=-1, keepdims=True) + norm_eps)


def norm_apply(values, weight):
    return values * rms_scale(values) * weight


def norm_grad(values, weight, grad):
    scale = rms_scale(values)
    inner = jnp.mean(grad * weight * values, axis=-1, keepdims=True)
    return scale * weight * grad - values * (scale * scale * scale) * inner


def gain_part(values, grad):
    return jnp.sum(grad * values * rms_scale(values), axis=0)


def gelu_parts(values):
    inner = gelu_coef * (values + cubic_coef * values * values * values)
    tanh_part = jnp.tanh(inner)
    value = 0.5 * values * (1.0 + tanh_part)
    slope = 0.5 * (1.0 + tanh_part) + 0.5 * values * (1.0 - tanh_part * tanh_part) * gelu_coef * (
        1.0 + 3.0 * cubic_coef * values * values
    )
    return value, slope


def rotary(values, cosines, sines, sign):
    half = HEAD_DIM // 2
    parts = []
    for start in range(0, values.shape[1], HEAD_DIM):
        first = values[:, start : start + half]
        second = values[:, start + half : start + HEAD_DIM]
        parts.append(first * cosines - sign * second * sines)
        parts.append(second * cosines + sign * first * sines)
    return jnp.concatenate(parts, axis=1)


def dot(left, right, left_dim=1, right_dim=0):
    return lax.dot_general(
        left, right, (((left_dim,), (right_dim,)), ((), ())), preferred_element_type=f32
    )


class Plan:
    def __init__(self, mesh):
        grid = mesh.devices
        self.contexts, self.ulysses = mesh.shape["ctx"], mesh.shape["uly"]
        self.cores = sum(tuple(d.coords) == tuple(grid[0, 0].coords) for d in grid[0])
        self.layers = len({d.coords[2] for d in grid[:, 0]})
        self.sides = self.contexts // self.layers
        self.rows = self.ulysses // self.cores
        self.halves = self.layers // self.cores

    def split(self, device):
        ctx, uly = divmod(device, self.ulysses)
        return (*divmod(ctx, self.sides), *divmod(uly, self.cores))

    def join(self, layer, side, row, core):
        return (layer * self.sides + side) * self.ulysses + row * self.cores + core

    def perm(self, target):
        count = self.contexts * self.ulysses
        return [(d, self.join(*target(*self.split(d)))) for d in range(count)]

    def here(self):
        layer, side = jnp.divmod(lax.axis_index("ctx"), self.sides)
        row, core = jnp.divmod(lax.axis_index("uly"), self.cores)
        return layer, side, row, core


class Ring:
    def __init__(self, plan, outer, inner, place, locate):
        self.size = outer * inner
        self.inner = inner

        def cell(index):
            out, rest = divmod(index % self.size, inner)
            return out, (rest if out % 2 == 0 else inner - 1 - rest)

        def index_of(out, inn):
            return out * inner + (inn if out % 2 == 0 else inner - 1 - inn)

        self.cells = [cell(i) for i in range(self.size)]

        def shifted(step):
            def target(*where):
                return place(where, *cell(index_of(*locate(where)) + step))

            return plan.perm(target)

        self.ahead, self.behind = shifted(1), shifted(-1)

    def position(self, out, inn):
        rest = jnp.where(out % 2 == 0, inn, self.inner - 1 - inn)
        return out * self.inner + rest


def move(values, perm):
    return lax.ppermute(values, AXES, perm)


def both(*values):
    return lax.optimization_barrier(values)


def after(values, *earlier):
    return lax.optimization_barrier((values, *earlier))[0]


def ring_gather(block, ring):
    size = ring.size
    found = {0: block}
    if size == 2:
        found[1] = move(block, ring.ahead)
        return [found[0], found[1]]
    forth = back = block
    middle = size // 2
    for step in range(1, middle):
        forth = move(forth, ring.ahead)
        back = move(back, ring.behind)
        forth, back = both(forth, back)
        found[size - step], found[step] = forth, back
    cut = block.shape[0] // 2
    forth = move(forth[:cut], ring.ahead)
    back = move(back[cut:], ring.behind)
    found[middle] = jnp.concatenate([forth, back], axis=0)
    return [found[k] for k in range(size)]


def ring_scatter(parts, ring, kind=bf16, landed=None):
    size = ring.size
    if size == 2:
        return parts[0].astype(f32) + move(parts[1].astype(kind), ring.ahead).astype(f32)
    middle = size // 2
    cut = parts[0].shape[0] // 2
    forth = move(parts[middle][:cut].astype(kind), ring.ahead)
    back = move(parts[middle][cut:].astype(kind), ring.behind)
    forth, back = both(forth, back)
    landed = [] if landed is None else landed
    for left in range(middle - 1, 0, -1):
        landed.append(forth)
        fore, aft = parts[left].astype(f32), parts[size - left].astype(f32)
        if left == middle - 1:
            fore = jnp.concatenate([fore[:cut] + forth.astype(f32), fore[cut:]], axis=0)
            aft = jnp.concatenate([aft[:cut], aft[cut:] + back.astype(f32)], axis=0)
        else:
            fore, aft = fore + forth.astype(f32), aft + back.astype(f32)
        forth = move(fore.astype(kind), ring.ahead)
        back = move(aft.astype(kind), ring.behind)
        forth, back = both(forth, back)
    return parts[0].astype(f32) + forth.astype(f32) + back.astype(f32)


def place_rows(blocks, indices, count):
    first = blocks[0]
    out = jnp.zeros((count, *first.shape), first.dtype)
    for block, index in zip(blocks, indices, strict=True):
        out = lax.dynamic_update_slice(out, block[None], (index, *(0,) * first.ndim))
    return out


def take_block(values, index, size):
    return lax.dynamic_slice_in_dim(values, index * size, size, 0)


class Sender:
    def __init__(self, plan, send, recv):
        self.plan, self.send, self.recv, self.sent = plan, send, recv, []
        self.ctx, self.uly = lax.axis_index("ctx"), lax.axis_index("uly")
        self.layer, self.side = self.ctx // plan.sides, self.ctx % plan.sides
        self.row, self.core = self.uly // plan.cores, self.uly % plan.cores
        flip = self.side % 2
        self.here = self.side * plan.layers + (
            self.layer * (1 - flip) + (plan.layers - 1 - self.layer) * flip
        )

    def at(self, layer, side, row, core):
        plan = self.plan
        return {"ctx": layer * plan.sides + side, "uly": row * plan.cores + core}

    def group(self):
        plan = self.plan
        for dr in range(plan.rows - 1, -1, -1):
            for dc in range(plan.cores):
                if (dr, dc) != (0, 0):
                    row, core = (self.row + dr) % plan.rows, (self.core + dc) % plan.cores
                    yield self.at(self.layer, self.side, row, core), row * plan.cores + core

    def meet(self):
        plan = self.plan
        friends = [friend for friend, _ in self.group()]
        for dl in range(1, plan.layers):
            for dc in range(plan.cores):
                layer, core = (self.layer + dl) % plan.layers, (self.core + dc) % plan.cores
                friends.append(self.at(layer, self.side, self.row, core))
        for ds in sorted({1 % plan.sides, plan.sides - 1} - {0}):
            side = (self.side + ds) % plan.sides
            friends.append(self.at(self.layer, side, self.row, self.core))
        barrier = pltpu.get_barrier_semaphore()
        for friend in friends:
            pl.semaphore_signal(
                barrier, inc=1, device_id=friend, device_id_type=pl.DeviceIdType.MESH
            )
        pl.semaphore_wait(barrier, len(friends))

    def push(self, source, target, device):
        k = len(self.sent)
        copy = pltpu.make_async_remote_copy(
            source,
            target,
            self.send.at[k],
            self.recv.at[k],
            device_id=device,
            device_id_type=pl.DeviceIdType.MESH,
        )
        copy.start()
        self.sent.append(copy)
        return copy

    def finish(self):
        for copy in self.sent:
            copy.wait_send()

    def spot(self, index):
        plan = self.plan
        out, low = index // plan.layers, index % plan.layers
        flip = out % 2
        return (low * (1 - flip) + (plan.layers - 1 - low) * flip) * plan.sides + out

    def ring(self, piece, cut, own=None):
        count = self.plan.contexts
        middle = count // 2
        ahead = {"ctx": self.spot((self.here + 1) % count), "uly": self.uly}
        behind = {"ctx": self.spot((self.here + count - 1) % count), "uly": self.uly}
        last = ()
        for step in range(middle):
            for copy in last:
                copy.wait_recv()
            fore = piece(self.spot((self.here + count - step) % count))
            aft = piece(self.spot((self.here + step) % count))
            first, second = (fore, aft) if step or own is None else (own, own)
            if step == middle - 1:
                fore, first = fore.at[:cut], first.at[:cut]
                aft, second = aft.at[cut:], second.at[cut:]
            last = (self.push(first, fore, ahead), self.push(second, aft, behind))
            yield
        for copy in last:
            copy.wait_recv()

    def slice_send(self, matrix, result, p):
        plan = self.plan
        h = (self.layer + p) % plan.halves
        target = self.at(
            self.core * plan.halves + h,
            self.side,
            self.row,
            plan.cores - 1 - self.layer // plan.halves,
        )
        width = matrix.shape[1] // plan.halves
        cols = pl.ds(pl.multiple_of(h * width, 128), width)
        return self.push(matrix.at[:, cols], result.at[self.ctx], target)

    def slice_pass(self, result, p, held):
        plan = self.plan
        origin = (plan.cores - 1 - self.core) * plan.halves
        origin = origin + (self.layer - p + plan.halves) % plan.halves
        passed = []
        for step in range(plan.sides):
            held.wait_recv()
            slot = result.at[origin * plan.sides + (self.side - step + plan.sides) % plan.sides]
            for dc in range(1, plan.cores):
                core = (self.core + dc) % plan.cores
                passed.append(self.push(slot, slot, self.at(self.layer, self.side, self.row, core)))
            if step < plan.sides - 1:
                side = (self.side + 1) % plan.sides
                held = self.push(slot, slot, self.at(self.layer, side, self.row, self.core))
            yield
        for copy in passed:
            copy.wait_recv()

    def run(self, rings, slices):
        going, queue, flying, moving, turn = [], list(rings), [], [], 0
        tasks = [(m, r, p) for m, r in slices for p in range(self.plan.halves)]

        def drive(generators):
            return [g for g in generators if next(g, "end") != "end"]

        while going or queue or tasks or flying or moving:
            going = drive(going)
            if not going and queue:
                going = drive(queue.pop(0))
            for _ in range(BURST):
                if tasks:
                    matrix, result, p = tasks.pop(0)
                    flying.append((result, p, self.slice_send(matrix, result, p)))
            turn += 1
            if flying and turn > LAG:
                moving.append(self.slice_pass(*flying.pop(0)))
            moving = drive(moving)


def copies_of(plan, slices):
    return slices * plan.halves * (1 + plan.sides - 1 + plan.sides * (plan.cores - 1))


def weights_kernel(plan, *refs):
    tok_in, wq, wk, wv, out_in, gain_in, gate_in = refs[:7]
    tok_all, qkv, out_all, gain_all, gate_all = refs[7:12]
    tok_tmp, qkv_tmp, out_tmp, gain_tmp, local, send, recv = refs[12:]
    link = Sender(plan, send, recv)
    link.meet()
    ulysses, ctx, uly = plan.ulysses, link.ctx, link.uly
    q_cols, k_cols = wq.shape[1] // ulysses, wk.shape[1] // ulysses

    def parts(u):
        yield wq.at[:, pl.ds(pl.multiple_of(u * q_cols, 128), q_cols)], pl.ds(0, q_cols)
        for k, matrix in enumerate((wk, wv)):
            cols = pl.ds(pl.multiple_of(u * k_cols, 128), k_cols)
            yield matrix.at[:, cols], pl.ds(q_cols + k * k_cols, k_cols)

    pairs = [(src, qkv_tmp.at[:, cols]) for src, cols in parts(uly)]
    pairs += [(gain_in, gain_tmp), (out_in, out_tmp), (tok_in, tok_tmp)]
    pulls = [pltpu.make_async_copy(*pair, local.at[k]) for k, pair in enumerate(pairs)]
    for pull in pulls:
        pull.start()
    place = ctx * ulysses + uly
    first = []
    for friend, u in link.group():
        for source, cols in parts(u):
            first.append(link.push(source, qkv.at[place, :, cols], friend))
        first.append(link.push(gain_in, gain_all.at[place], friend))
    for pull in pulls:
        pull.wait()
    pairs = [
        (qkv_tmp, qkv.at[place]),
        (gain_tmp, gain_all.at[place]),
        (out_tmp, out_all.at[ctx]),
        (tok_tmp, tok_all.at[uly]),
    ]
    puts = [pltpu.make_async_copy(*pair, local.at[6 + k]) for k, pair in enumerate(pairs)]
    for put in puts:
        put.start()
    for put in puts:
        put.wait()
    for copy in first:
        copy.wait_recv()
    tokens = [link.push(tok_in, tok_all.at[uly], friend) for friend, _ in link.group()]

    def block(array):
        return lambda c: array.at[pl.ds(c * ulysses, ulysses)]

    rings = [
        [link.ring(block(qkv), ulysses // 2), link.ring(block(gain_all), ulysses // 2)],
        [link.ring(lambda c: out_all.at[c], out_all.shape[1] // 16 * 8)],
    ]
    link.run(rings, [(gate_in, gate_all)])
    for copy in tokens:
        copy.wait_recv()
    link.finish()


anywhere = pl.BlockSpec(memory_space=pl.ANY)


def sliced(plan, weights):
    shape = (plan.contexts, weights.shape[0], weights.shape[1] // plan.halves)
    return jax.ShapeDtypeStruct(shape, weights.dtype)


def fetch_weights(plan, tokens, wq, wk, wv, w_out, gains, w_gate):
    shard, contexts, ulysses = wq.shape[0], plan.contexts, plan.ulysses
    cols = (wq.shape[1] + wk.shape[1] + wv.shape[1]) // ulysses
    results = [
        jax.ShapeDtypeStruct((ulysses, *tokens.shape), tokens.dtype),
        jax.ShapeDtypeStruct((contexts * ulysses, shard, cols), wq.dtype),
        jax.ShapeDtypeStruct((contexts, *w_out.shape), w_out.dtype),
        jax.ShapeDtypeStruct((contexts * ulysses, *gains.shape), gains.dtype),
        sliced(plan, w_gate),
    ]
    copies = 5 * (ulysses - 1) + 3 * contexts + copies_of(plan, 1)
    return pl.pallas_call(
        functools.partial(weights_kernel, plan),
        out_shape=results,
        in_specs=[anywhere] * 7,
        out_specs=[anywhere] * len(results),
        scratch_shapes=[
            pltpu.VMEM(tokens.shape, tokens.dtype),
            pltpu.VMEM((shard, cols), wq.dtype),
            pltpu.VMEM(w_out.shape, w_out.dtype),
            pltpu.VMEM(gains.shape, gains.dtype),
            pltpu.SemaphoreType.DMA((10,)),
            pltpu.SemaphoreType.DMA((copies,)),
            pltpu.SemaphoreType.DMA((copies,)),
        ],
        compiler_params=pltpu.CompilerParams(collective_id=1, has_side_effects=True),
    )(tokens, wq, wk, wv, w_out, gains, w_gate)


def keys_kernel(plan, kv_in, up_in, down_in, kv_all, up_all, down_all, tmp, local, send, recv):
    link = Sender(plan, send, recv)
    link.meet()
    pull = pltpu.make_async_copy(kv_in, tmp, local.at[0])
    put = pltpu.make_async_copy(tmp, kv_all.at[link.ctx], local.at[1])
    pull.start()
    pull.wait()
    put.start()
    ring = link.ring(lambda c: kv_all.at[c], kv_in.shape[0] // 2, kv_in)
    link.run([[ring]], [(up_in, up_all), (down_in, down_all)])
    put.wait()
    link.finish()


def fetch_keys(plan, kv, w_up, w_down):
    copies = plan.contexts + copies_of(plan, 2)
    return pl.pallas_call(
        functools.partial(keys_kernel, plan),
        out_shape=[
            jax.ShapeDtypeStruct((plan.contexts, *kv.shape), kv.dtype),
            sliced(plan, w_up),
            sliced(plan, w_down),
        ],
        in_specs=[anywhere] * 3,
        out_specs=[anywhere] * 3,
        scratch_shapes=[
            pltpu.VMEM(kv.shape, kv.dtype),
            pltpu.SemaphoreType.DMA((2,)),
            pltpu.SemaphoreType.DMA((copies,)),
            pltpu.SemaphoreType.DMA((copies,)),
        ],
        compiler_params=pltpu.CompilerParams(collective_id=2, has_side_effects=True),
    )(kv, w_up, w_down)


def visible(q_first, k_first, boundary, span):
    q_pos = q_first + lax.broadcasted_iota(jnp.int32, (span, span), 0)
    k_pos = k_first + lax.broadcasted_iota(jnp.int32, (span, span), 1)
    low = jnp.where(q_pos >= boundary, boundary, 0)
    return (k_pos <= q_pos) & (k_pos >= low)


def active(q_first, k_first, boundary, span):
    split = (q_first >= boundary) & (k_first + span <= boundary)
    return (k_first <= q_first) & jnp.logical_not(split)


def attend_kernel(span, repeat, count, qp, kp, bd, q_ref, kv_ref, o_ref, lse_ref, acc, den):
    i, j = pl.program_id(0), pl.program_id(1)

    @pl.when(j == 0)
    def _():
        acc[...] = jnp.zeros_like(acc)
        den[...] = jnp.zeros_like(den)

    q_first, k_first, boundary = qp[i], kp[j], bd[0]

    @pl.when(active(q_first, k_first, boundary, span))
    def _():
        allowed = visible(q_first, k_first, boundary, span)
        keys, values = kv_ref[:, :HEAD_DIM], kv_ref[:, HEAD_DIM:]
        for r in range(repeat):
            cols = slice(r * HEAD_DIM, (r + 1) * HEAD_DIM)
            scores = dot(q_ref[:, cols], keys, 1, 1)
            weights = jnp.where(
                allowed, jnp.exp(soft_cap * jnp.tanh(scores * (1.0 / soft_cap))), 0.0
            )
            den[r] += jnp.sum(weights, axis=1, keepdims=True)
            acc[:, cols] += dot(weights.astype(bf16), values)

    @pl.when(j == count - 1)
    def _():
        for r in range(repeat):
            cols = slice(r * HEAD_DIM, (r + 1) * HEAD_DIM)
            total = den[r][:, :1]
            o_ref[:, cols] = (acc[:, cols] / total).astype(bf16)
            lse_ref[:, r * 128 : (r + 1) * 128] = jnp.broadcast_to(jnp.log(total), (span, 128))


def attend(q, kv, q_pos, k_pos, boundary, span):
    rows, width = q.shape
    repeat = width // HEAD_DIM
    count = kv.shape[0] // span
    spec = pltpu.PrefetchScalarGridSpec(
        num_scalar_prefetch=3,
        grid=(rows // span, count),
        in_specs=[
            pl.BlockSpec((span, width), lambda i, j, *_: (i, 0)),
            pl.BlockSpec((span, kv.shape[1]), lambda i, j, *_: (j, 0)),
        ],
        out_specs=[
            pl.BlockSpec((span, width), lambda i, j, *_: (i, 0)),
            pl.BlockSpec((span, 128 * repeat), lambda i, j, *_: (i, 0)),
        ],
        scratch_shapes=[
            pltpu.VMEM((span, width), f32),
            pltpu.VMEM((repeat, span, 128), f32),
        ],
    )
    flops = 2 * rows * kv.shape[0] * width
    return pl.pallas_call(
        functools.partial(attend_kernel, span, repeat, count),
        out_shape=[
            jax.ShapeDtypeStruct((rows, width), bf16),
            jax.ShapeDtypeStruct((rows, 128 * repeat), f32),
        ],
        grid_spec=spec,
        compiler_params=pltpu.CompilerParams(dimension_semantics=("arbitrary", "arbitrary")),
        cost_estimate=pl.CostEstimate(
            flops=flops, bytes_accessed=2 * kv.size * 2, transcendentals=rows * kv.shape[0] * repeat
        ),
    )(q_pos, k_pos, boundary, q, kv)


def attend_back_kernel(
    span, repeat, count, blocks, qp, kp, bd, q_ref, g_ref, lse_ref, ds_ref, kv_ref, dq_ref, dkv_ref, acc, dk, dv
):
    j, i = pl.program_id(0), pl.program_id(1)

    @pl.when((j == 0) & (i == 0))
    def _():
        acc[...] = jnp.zeros_like(acc)

    @pl.when(i == 0)
    def _():
        dk[...] = jnp.zeros_like(dk)
        dv[...] = jnp.zeros_like(dv)

    q_first, k_first, boundary = qp[i], kp[j], bd[0]

    @pl.when(active(q_first, k_first, boundary, span))
    def _():
        allowed = visible(q_first, k_first, boundary, span)
        keys, values = kv_ref[:, :HEAD_DIM], kv_ref[:, HEAD_DIM:]
        rows = pl.ds(pl.multiple_of(i * span, span), span)
        for r in range(repeat):
            cols = slice(r * HEAD_DIM, (r + 1) * HEAD_DIM)
            query, grad = q_ref[rows, cols], g_ref[rows, cols]
            lse = lse_ref[rows, r * 128 : r * 128 + 1]
            dsum = ds_ref[rows, r * 128 : r * 128 + 1]
            bent = jnp.tanh(dot(query, keys, 1, 1) * (1.0 / soft_cap))
            probs = jnp.where(allowed, jnp.exp(soft_cap * bent - lse), 0.0)
            dprob = dot(grad, values, 1, 1)
            dscore = (probs * (dprob - dsum) * (1.0 - bent * bent)).astype(bf16)
            acc[rows, cols] += dot(dscore, keys)
            dk[...] += dot(dscore, query, 0, 0)
            dv[...] += dot(probs.astype(bf16), grad, 0, 0)

    @pl.when(i == blocks - 1)
    def _():
        dkv_ref[:, :HEAD_DIM] = dk[...].astype(dkv_ref.dtype)
        dkv_ref[:, HEAD_DIM:] = dv[...].astype(dkv_ref.dtype)

    @pl.when((j == count - 1) & (i == blocks - 1))
    def _():
        dq_ref[...] = acc[...]


def attend_back(q, grad, lse, dsum, kv, q_pos, k_pos, boundary, span):
    rows, width = q.shape
    repeat = width // HEAD_DIM
    count, blocks = kv.shape[0] // span, rows // span
    whole = lambda w: pl.BlockSpec((rows, w), lambda j, i, *_: (0, 0))
    spec = pltpu.PrefetchScalarGridSpec(
        num_scalar_prefetch=3,
        grid=(count, blocks),
        in_specs=[
            whole(width),
            whole(width),
            whole(128 * repeat),
            whole(128 * repeat),
            pl.BlockSpec((span, kv.shape[1]), lambda j, i, *_: (j, 0)),
        ],
        out_specs=[
            whole(width),
            pl.BlockSpec((span, kv.shape[1]), lambda j, i, *_: (j, 0)),
        ],
        scratch_shapes=[
            pltpu.VMEM((rows, width), f32),
            pltpu.VMEM((span, HEAD_DIM), f32),
            pltpu.VMEM((span, HEAD_DIM), f32),
        ],
    )
    return pl.pallas_call(
        functools.partial(attend_back_kernel, span, repeat, count, blocks),
        out_shape=[
            jax.ShapeDtypeStruct((rows, width), f32),
            jax.ShapeDtypeStruct(kv.shape, bf16),
        ],
        grid_spec=spec,
        compiler_params=pltpu.CompilerParams(dimension_semantics=("arbitrary", "arbitrary")),
        cost_estimate=pl.CostEstimate(
            flops=5 * rows * kv.shape[0] * width,
            bytes_accessed=2 * kv.size * 2,
            transcendentals=rows * kv.shape[0] * repeat,
        ),
    )(q_pos, k_pos, boundary, q, grad, lse, dsum, kv)


def on_device(
    plan,
    tokens,
    cotangent,
    span_order,
    segments,
    w_query,
    w_key,
    w_value,
    w_out,
    w_gate,
    w_up,
    w_down,
    gain_attn_in,
    gain_attn_out,
    gain_ffn_in,
    gain_ffn_out,
):
    rows, width = tokens.shape
    contexts, ulysses = plan.contexts, plan.ulysses
    layers, sides, cores, halves = plan.layers, plan.sides, plan.cores, plan.halves
    group_rows = rows * ulysses
    span = group_rows // 2
    q_scale = float(HEAD_DIM) ** (-0.5)
    ctx = lax.axis_index("ctx")
    layer, side, row, core = plan.here()

    ctx_ring = Ring(
        plan, sides, layers, lambda w, out, inn: (inn, out, w[2], w[3]), lambda w: (w[1], w[0])
    )
    ffn_ring = Ring(
        plan, plan.rows, layers, lambda w, out, inn: (inn, w[1], out, w[3]), lambda w: (w[2], w[0])
    )
    side_ring = Ring(
        plan, 1, sides, lambda w, out, inn: (w[0], inn, w[2], w[3]), lambda w: (0, w[1])
    )
    row_ring = Ring(
        plan, 1, plan.rows, lambda w, out, inn: (w[0], w[1], inn, w[3]), lambda w: (0, w[2])
    )
    core_ring = Ring(
        plan, 1, cores, lambda w, out, inn: (w[0], w[1], w[2], inn), lambda w: (0, w[3])
    )
    ctx_cells = jnp.array([inn * sides + out for out, inn in ctx_ring.cells], jnp.int32)
    ctx_place = ctx_ring.position(side, layer)
    ring_ctx = [ctx_cells[(ctx_place + k) % contexts] for k in range(contexts)]

    def group_gather(values):
        mine = ring_gather(values, row_ring)
        blocks, where = [], []
        for k, block in enumerate(mine):
            for m, found in enumerate(ring_gather(block, core_ring)):
                blocks.append(found)
                where.append((row + k) % plan.rows * cores + (core + m) % cores)
        return place_rows(blocks, where, ulysses).reshape(group_rows, values.shape[1])

    def group_scatter(values):
        parts = values.reshape(plan.rows, cores, rows, values.shape[1])

        def part(k, m):
            at = ((row + k) % plan.rows, (core + m) % cores, 0, 0)
            return lax.dynamic_slice(parts, at, (1, 1, *parts.shape[2:]))[0, 0]

        summed = [
            ring_scatter([part(k, m) for m in range(cores)], core_ring) for k in range(plan.rows)
        ]
        return ring_scatter(summed, row_ring)

    def ctx_scatter(arrays):
        size = arrays[0].shape[0] // contexts

        def part(k):
            blocks = [take_block(array, ring_ctx[k], size) for array in arrays]
            return jnp.concatenate(blocks, axis=1) if len(blocks) > 1 else blocks[0]

        return ring_scatter([part(k) for k in range(contexts)], ctx_ring, bf16)

    shard = gain_attn_in.shape[0]
    places = (ctx_place, row, core)
    tiny_rings = (ctx_ring, row_ring, core_ring)
    ring_order = [inn * sides + out for out, inn in ctx_ring.cells]

    def turn(values, axis, back):
        count, place = values.shape[axis], places[axis]
        start = place if back else (count - place) % count
        twice = jnp.concatenate([values, values], axis=axis)
        return lax.dynamic_slice_in_dim(twice, start, count, axis)

    def sum_gains(parts):
        count = parts.shape[0]
        found = jnp.transpose(parts.reshape(count, contexts * ulysses, shard), (1, 0, 2))
        found = jnp.pad(found, ((0, 0), (0, -count % 8), (0, -shard % 128)))
        found = found.reshape(contexts, plan.rows, cores, *found.shape[1:])
        found = jnp.stack([found[c] for c in ring_order])
        for axis in range(3):
            found = turn(found, axis, True)
        for axis in (2, 1, 0):
            entries = [lax.index_in_dim(found, k, axis, False) for k in range(found.shape[axis])]
            found = ring_scatter(entries, tiny_rings[axis], f32)
        return found[:count, :shard]

    packed = jnp.stack([gain_attn_in, gain_attn_out, gain_ffn_in, gain_ffn_out])
    packed = jnp.pad(packed, ((0, 4), (0, -shard % 128)))
    tok_group, col_qkv, col_out, gains, ffn_gate = fetch_weights(
        plan, tokens, w_query, w_key, w_value, w_out, packed.astype(f32), w_gate
    )
    tok_group = tok_group.reshape(group_rows, width)
    col_qkv = col_qkv.reshape(width, -1)
    col_out = col_out.reshape(width, -1)
    gains = jnp.transpose(gains[:, :4, :shard], (1, 0, 2)).reshape(4, width)
    weight_one, weight_two, weight_three, weight_four = (1.0 + gains[k][None] for k in range(4))

    own_spans = lax.dynamic_slice_in_dim(span_order, 2 * ctx, 2, 0) * span
    boundary = jnp.sum((segments == 0).astype(jnp.int32)).reshape(1)
    key_spans = span_order * span
    group_pos = (own_spans[:, None] + jnp.arange(span, dtype=jnp.int32)[None, :]).reshape(-1)
    half = HEAD_DIM // 2
    freqs = rotary_base ** (-jnp.arange(half).astype(f32) / half)
    angles = group_pos.astype(f32)[:, None] * freqs[None, :]
    cosines, sines = jnp.cos(angles), jnp.sin(angles)

    q_cols, k_cols = w_query.shape[1] // ulysses, w_key.shape[1] // ulysses
    tok_rows = tok_group.astype(f32)
    normed_in = norm_apply(tok_rows, weight_one).astype(bf16)
    qkv = dot(normed_in, col_qkv)
    queries = (rotary(qkv[:, :q_cols], cosines, sines, 1.0) * q_scale).astype(bf16)
    keys = rotary(qkv[:, q_cols : q_cols + k_cols], cosines, sines, 1.0).astype(bf16)
    values = qkv[:, q_cols + k_cols :].astype(bf16)
    kv, ffn_up, ffn_down = fetch_keys(
        plan, jnp.concatenate([keys, values], axis=1), w_up, w_down
    )
    kv = kv.reshape(contexts * group_rows, -1)
    ffn_gate, ffn_up, ffn_down = (w.reshape(width, -1) for w in (ffn_gate, ffn_up, ffn_down))

    slice_cols = w_gate.shape[1] // halves

    def slice_perm(p):
        return plan.perm(lambda l, s, r, c: (c * halves + (l + p) % halves, s, r, l // halves))

    def slice_back(p):
        return [(b, a) for a, b in slice_perm(p)]

    def pick(options, index):
        out = options[0]
        for k in range(1, len(options)):
            out = jnp.where(index == k, options[k], out)
        return out

    def slice_start(grad):
        parts = grad.reshape(cores, halves, sides, -1, slice_cols)
        size = parts.shape[3]
        others = []
        for m in range(1, cores):
            at = ((core + m) % cores, 0, 0, 0, 0)
            piece = lax.dynamic_slice(parts, at, (1, *parts.shape[1:]))[0]
            perm = plan.perm(lambda l, s, r, c, m=m: (l, s, r, (c + m) % cores))
            others.append(move(piece, perm))

        def side_part(k):
            here = (side + k) % sides
            shape = (halves, 1, size, slice_cols)
            found = lax.dynamic_slice(parts, (core, 0, here, 0, 0), (1, *shape))[0].astype(f32)
            for other in others:
                found = found + lax.dynamic_slice(other, (0, here, 0, 0), shape).astype(f32)
            return found.reshape(halves * size, slice_cols)

        summed = ring_scatter([side_part(k) for k in range(sides)], side_ring, bf16)
        return summed.astype(bf16).reshape(halves, size, slice_cols)

    def slice_end(summed):
        got = []
        for p in range(halves):
            piece = lax.dynamic_index_in_dim(summed, (layer - p) % halves, 0, keepdims=False)
            got.append(move(piece, slice_back(p)))
        cuts = [pick(got, (h - layer) % halves) for h in range(halves)]
        return jnp.concatenate(cuts, axis=1).astype(f32)

    head_o, lse = attend(queries, kv, own_spans, key_spans, boundary, span)
    attn_out = group_scatter(dot(head_o, col_out, 1, 1))
    tok_own = tokens.astype(f32)
    hidden_in = tok_own + norm_apply(attn_out, weight_two)
    normed_own = norm_apply(hidden_in, weight_three).astype(bf16)

    size = ffn_ring.size
    order = [0]
    for k in range(1, size // 2):
        order += [k, size - k]
    order.append(size // 2)
    near = max(size - 3, 1)

    def ffn_gather(values):
        found = ring_gather(values, ffn_ring)
        return [
            jnp.concatenate([found[k] for k in ks], axis=0) for ks in (order[:near], order[near:])
        ]

    def ffn_scatter(chunk):
        parts = [None] * size
        far = chunk(1, None)
        for values, ks in ((far, order[near:]), (chunk(0, far), order[:near])):
            for n, k in enumerate(ks):
                parts[k] = values[n * rows : (n + 1) * rows]
        landed = []
        return ring_scatter(parts, ffn_ring, bf16, landed), landed

    normed_mid = ffn_gather(normed_own)
    gate = [dot(x, ffn_gate) for x in normed_mid]
    upper = [dot(x, ffn_up) for x in normed_mid]
    hidden = [(gelu_parts(g)[0] * u).astype(bf16) for g, u in zip(gate, upper, strict=True)]

    def down_part(n, far):
        rows_in = hidden[n] if far is None else after(hidden[n], far)
        return dot(rows_in, ffn_down, 1, 1)

    ffn_out, _ = ffn_scatter(down_part)
    block_out = (hidden_in + norm_apply(ffn_out, weight_four)).astype(bf16)
    cot_own = cotangent.astype(f32)
    d_ffn = ffn_gather(norm_grad(ffn_out, weight_four, cot_own).astype(bf16))
    d_gate, d_upper = [], []
    for n in range(2):
        d_hidden = dot(d_ffn[n], ffn_down)
        gate_value, gate_slope = gelu_parts(gate[n])
        d_gate.append((d_hidden * upper[n] * gate_slope).astype(bf16))
        d_upper.append((d_hidden * gate_value).astype(bf16))

    def mid_part(n, far):
        left, right = d_gate[n], d_upper[n]
        if far is not None:
            left, right = after(left, far), after(right, far)
        return dot(left, ffn_gate, 1, 1) + dot(right, ffn_up, 1, 1)

    d_mid, landed = ffn_scatter(mid_part)
    grad_hidden = cot_own + norm_grad(hidden_in, weight_three, d_mid)
    joined = [jnp.concatenate(x, axis=0) for x in (d_ffn, hidden, normed_mid, d_gate, d_upper)]

    def weight_grad(left, right, step):
        left = after(left, landed[min(step, len(landed) - 1)])
        grad = dot(left, right, 0, 0).astype(bf16)
        return slice_start(grad)

    sum_down = weight_grad(joined[0], joined[1], 0)
    sum_gate = weight_grad(joined[2], joined[3], 1)
    sum_up = weight_grad(joined[2], joined[4], 2)
    grad_down = slice_end(after(sum_down, d_mid))
    grad_gate = slice_end(after(sum_gate, d_mid))

    d_attn = group_gather(norm_grad(attn_out, weight_two, grad_hidden).astype(bf16))
    out_part = dot(d_attn, head_o, 0, 0).astype(bf16)
    grad_o = dot(d_attn, col_out).astype(bf16)
    products = grad_o.astype(f32) * head_o.astype(f32)
    dsum = jnp.concatenate(
        [
            jnp.broadcast_to(
                jnp.sum(products[:, s : s + HEAD_DIM], axis=1, keepdims=True), (group_rows, 128)
            )
            for s in range(0, q_cols, HEAD_DIM)
        ],
        axis=1,
    )
    grad_q, grad_kv = attend_back(
        queries, grad_o, lse, dsum, kv, own_spans, key_spans, boundary, span
    )
    grad_kv = ctx_scatter([grad_kv])
    grad_up = slice_end(after(sum_up, grad_kv))
    grad_q = (rotary(grad_q, cosines, sines, -1.0) * q_scale).astype(bf16)
    grad_k = rotary(grad_kv[:, :k_cols], cosines, sines, -1.0).astype(bf16)
    grad_v = grad_kv[:, k_cols:].astype(bf16)
    grad_qkv = jnp.concatenate([grad_q, grad_k, grad_v], axis=1)
    d_in_part = dot(grad_qkv, col_qkv, 1, 1)
    d_in = group_scatter(d_in_part)
    grad_tokens = grad_hidden + norm_grad(tok_own, weight_one, d_in)
    qkv_part = dot(normed_in, grad_qkv, 0, 0).astype(bf16)
    mixed_grad = ctx_scatter([qkv_part, out_part])
    grad_outproj = mixed_grad[:, qkv_part.shape[1] :]
    mixed_grad = mixed_grad[:, : qkv_part.shape[1]].astype(bf16)
    mixed_grad = lax.all_to_all(
        mixed_grad.reshape(ulysses, -1, mixed_grad.shape[1]),
        "uly",
        split_axis=0,
        concat_axis=0,
        tiled=True,
    )
    mixed_grad = jnp.transpose(mixed_grad, (1, 0, 2)).astype(f32)
    grad_query = mixed_grad[:, :, :q_cols].reshape(w_query.shape)
    grad_key = mixed_grad[:, :, q_cols : q_cols + k_cols].reshape(w_key.shape)
    grad_value = mixed_grad[:, :, q_cols + k_cols :].reshape(w_value.shape)

    gain_grads = sum_gains(
        jnp.stack(
            [
                gain_part(attn_out, after(grad_hidden, grad_q)),
                gain_part(hidden_in, after(d_mid, grad_q)),
                gain_part(ffn_out, after(cot_own, grad_q)),
            ]
        )
    )
    products = [
        jnp.sum(w.astype(f32) * g, axis=1)
        for w, g in ((w_query, grad_query), (w_key, grad_key), (w_value, grad_value))
    ]
    gain_first = (products[0] + products[1] + products[2]) / (1.0 + gain_attn_in.astype(f32))
    return (
        block_out,
        grad_tokens,
        grad_query,
        grad_key,
        grad_value,
        grad_outproj,
        grad_gate,
        grad_up,
        grad_down,
        gain_first,
        gain_grads[0],
        gain_grads[1],
        gain_grads[2],
    )


def solution(mesh):
    flat, cut, line = P(AXES, None), P("ctx", "uly"), P(AXES)
    in_specs = (flat, flat, P(), P(), flat, flat, flat, cut, cut, cut, cut, line, line, line, line)
    out_specs = (flat, flat, flat, flat, flat, cut, cut, cut, cut, line, line, line, line)
    plan = Plan(mesh)

    def body(*args):
        return on_device(plan, *args)

    return jax.shard_map(
        body, mesh=mesh, in_specs=in_specs, out_specs=out_specs, check_vma=False
    )
```

profile of v0, /device:TPU:0, one launch (start us, length us, event | category | flops | bytes accessed | tf_op | source)
XLA Modules:
  0.0 892.5 jit_solution(9759543140012084876)
XLA Ops:
  2.1 121.4 %shard_map.255 = (bf16[4,128,2304]{2,1,0:T(8,128)(2,1)}, bf16[32,72,1024]{2,1,0:T(8,128)(2,1)}, bf16[8,288,512]{2,1,0:T(8,128)(2,1)}, f32[32,8,128]{2,1,0:T(8,128)}, bf16[8,288,1152]{2,1,0:T(8,128)(2,1)}) custom-call(bf16[128,2304]{1,0:T(8,128)(2,1)} %refs_0_.1, bf16[72,2048]{1,0:T(8,128)(2,1)} %refs_1_.1, bf16[72,1024]{1,0:T(8,128)(2,1)} %refs_2_.1, ...), custom_call_target="tpu_custom_call" | custom-call | tf_op jit(solution)/shard_map/pallas_call | solution.py:409
  131.9 2.6 fusion.157
  136.7 122.7 %shard_map.256 = (bf16[8,512,512]{2,1,0:T(8,128)(2,1)}, bf16[8,288,1152]{2,1,0:T(8,128)(2,1)}, bf16[8,288,1152]{2,1,0:T(8,128)(2,1)}) custom-call(bf16[512,512]{1,0:T(8,128)(2,1)} %pad_maximum_fusion.6.kv_in, bf16[288,2304]{1,0:T(8,128)(2,1)} %up_in.1, bf16[288,2304]{1,0:T(8,128)(2,1)} %down_in.1), custom_call_target="tpu_custom_call" | custom-call | tf_op jit(solution)/shard_map/pallas_call | solution.py:443
  260.3 27.9 %shard_map.257 = (bf16[512,512]{1,0:T(8,128)(2,1)}, f32[512,256]{1,0:T(8,128)}) custom-call(s32[2]{0:T(128)} %copy-done.75, s32[16]{0:T(128)} %broadcast_multiply_fusion.4.kp, s32[1]{0:T(128)} %bitcast.bd, bf16[512,512]{1,0:T(8,128)(2,1)} %fusion.60.q_ref, bf16[4096,512]{1,0:T(8,128)(2,1)} %bitcast.349), custom_call_target="tpu_custom_call" | custom-call | flops 2147483648 | bytes 8388608 | tf_op jit(solution)/shard_map/pallas_call | solution.py:527
  288.1 4.6 fusion.158
  300.8 12.8 %collective-permute-done.2 = bf16[128,2304]{1,0:T(8,128)(2,1)S(1)} collective-permute-done((bf16[128,2304]{1,0:T(8,128)(2,1)S(1)}, bf16[128,2304]{1,0:T(8,128)(2,1)S(1)}, u32[]{:S(2)}, u32[]{:S(2)}) %collective-permute-start.2) | collective-permute-done | bytes 589856 | tf_op jit(solution)/shard_map/ppermute | solution.py:127
  319.6 12.7 %collective-permute-done.3 = bf16[128,2304]{1,0:T(8,128)(2,1)S(1)} collective-permute-done((bf16[128,2304]{1,0:T(8,128)(2,1)S(1)}, bf16[128,2304]{1,0:T(8,128)(2,1)S(1)}, u32[]{:S(2)}, u32[]{:S(2)}) %collective-permute-start.3) | collective-permute-done | bytes 589856 | tf_op jit(solution)/shard_map/ppermute | solution.py:127
  334.4 11.7 %collective-permute-done.5 = bf16[128,2304]{1,0:T(8,128)(2,1)S(1)} collective-permute-done((bf16[128,2304]{1,0:T(8,128)(2,1)S(1)}, bf16[128,2304]{1,0:T(8,128)(2,1)S(1)}, u32[]{:S(2)}, u32[]{:S(2)}) %collective-permute-start.5) | collective-permute-done | bytes 589856 | tf_op jit(solution)/shard_map/ppermute | solution.py:127
  348.8 6.7 fusion.159
  355.5 4.0 collective-permute-done.7
  362.2 4.6 collective-permute-done.9
  367.8 2.4 fusion.160
  370.3 2.6 slice-done.11
  372.9 3.7 multiply_convert_fusion.4
  376.6 2.5 fusion.155
  381.3 5.8 multiply_convert_fusion.2
  387.4 2.8 collective-permute-start.13
  390.3 4.0 fusion.161
  394.3 6.5 collective-permute-done.13
  402.8 3.3 collective-permute-start.15
  406.1 10.8 %collective-permute-done.15 = bf16[128,2304]{1,0:T(8,128)(2,1)S(1)} collective-permute-done((bf16[128,2304]{1,0:T(8,128)(2,1)S(1)}, bf16[128,2304]{1,0:T(8,128)(2,1)S(1)}, u32[]{:S(2)}, u32[]{:S(2)}) %collective-permute-start.15) | collective-permute-done | bytes 589856 | tf_op jit(solution)/shard_map/ppermute | solution.py:127
  416.9 3.2 collective-permute-done.16
  421.2 2.3 collective-permute-start.17
  424.9 6.9 collective-permute-done.17
  434.2 2.3 multiply_reduce_fusion.6
  436.5 3.3 constant_dynamic-update-slice_fusion.31
  462.2 10.0 %collective-permute-done.21 = bf16[128,2304]{1,0:T(8,128)(2,1)S(1)} collective-permute-done((bf16[128,2304]{1,0:T(8,128)(2,1)}, bf16[128,2304]{1,0:T(8,128)(2,1)S(1)}, u32[]{:S(2)}, u32[]{:S(2)}) %collective-permute-start.21) | collective-permute-done | bytes 589856 | tf_op jit(solution)/shard_map/ppermute | solution.py:127
  476.0 9.2 %multiply_convert_fusion.1 = (bf16[640,1152]{1,0:T(8,128)(2,1)}, bf16[640,1152]{1,0:T(8,128)(2,1)}) fusion(f32[640,1152]{1,0:T(8,128)S(1)} %copy-done.89, f32[640,1152]{1,0:T(8,128)S(1)} %copy-done.90, bf16[640,2304]{1,0:T(8,128)(2,1)S(1)} %get-tuple-element.291, bf16[2304,1152]{1,0:T(8,128)(2,1)} %bitcast.339), kind=kOutput, calls=%fused_computation.21 | convolution fusion | flops 3414343680 | bytes 17104896 | tf_op jit(solution)/shard_map/dot_general | solution.py:67
  488.0 4.1 collective-permute-done.26
  494.4 4.5 multiply_convert_fusion.3
  499.0 4.3 fusion.162
  503.3 4.6 fusion.156
  507.9 5.9 fusion.163
  516.0 7.1 convolution_add_fusion
  526.1 12.9 %collective-permute-done.29 = bf16[128,2304]{1,0:T(8,128)(2,1)S(1)} collective-permute-done((bf16[128,2304]{1,0:T(8,128)(2,1)S(1)}, bf16[128,2304]{1,0:T(8,128)(2,1)S(1)}, u32[]{:S(2)}, u32[]{:S(2)}) %collective-permute-start.29) | collective-permute-done | bytes 589856 | tf_op jit(solution)/shard_map/ppermute | solution.py:127
  541.5 6.6 convolution_convert_fusion
  552.3 7.9 convolution_convert_fusion.2
  568.9 6.6 convolution_convert_fusion.1
  578.8 4.2 collective-permute-done.36
  583.2 2.6 fusion.9
  589.4 34.3 %shard_map.258 = (f32[512,512]{1,0:T(8,128)}, bf16[4096,512]{1,0:T(8,128)(2,1)}) custom-call(s32[2]{0:T(128)} %copy-done.75, s32[16]{0:T(128)} %broadcast_multiply_fusion.4.kp, s32[1]{0:T(128)} %bitcast.bd, bf16[512,512]{1,0:T(8,128)(2,1)} %fusion.60.q_ref, bf16[512,512]{1,0:T(8,128)(2,1)} %get-tuple-element.364.g_ref, ...), custom_call_target="tpu_custom_call" | custom-call | flops 5368709120 | bytes 8388608 | tf_op jit(solution)/shard_map/pallas_call | solution.py:610
  627.5 3.2 convolution_convert_fusion.4
  630.6 3.3 collective-permute-done.38
  638.1 3.0 fusion.11
  642.8 6.5 collective-permute-done.40
  651.8 4.2 fusion.10
  660.3 28.7 %collective-permute-done.42 = bf16[512,512]{1,0:T(8,128)(2,1)S(1)} collective-permute-done((bf16[512,512]{1,0:T(8,128)(2,1)S(1)}, bf16[512,512]{1,0:T(8,128)(2,1)S(1)}, u32[]{:S(2)}, u32[]{:S(2)}) %collective-permute-start.42) | collective-permute-done | bytes 524320 | tf_op jit(solution)/shard_map/ppermute | solution.py:127
  693.6 6.7 collective-permute-start.60
  702.0 25.3 %collective-permute-done.44 = bf16[512,512]{1,0:T(8,128)(2,1)S(1)} collective-permute-done((bf16[512,512]{1,0:T(8,128)(2,1)S(1)}, bf16[512,512]{1,0:T(8,128)(2,1)S(1)}, u32[]{:S(2)}, u32[]{:S(2)}) %collective-permute-start.44) | collective-permute-done | bytes 524320 | tf_op jit(solution)/shard_map/ppermute | solution.py:127
  735.8 5.1 fusion.164
  742.6 3.2 convolution_convert_fusion.3
  745.8 2.3 collective-permute-start.71
  769.4 6.2 collective-permute-done.49
  775.6 2.3 collective-permute-done.50
  785.5 28.4 %collective-permute-done.51 = bf16[288,1536]{1,0:T(8,128)(2,1)S(1)} collective-permute-done((bf16[288,1536]{1,0:T(8,128)(2,1)S(1)}, bf16[288,1536]{1,0:T(8,128)(2,1)S(1)}, u32[]{:S(2)}, u32[]{:S(2)}) %collective-permute-start.51) | collective-permute-done | bytes 884768 | tf_op jit(solution)/shard_map/ppermute | solution.py:127
  814.9 2.5 collective-permute-start.53
  818.7 18.7 %collective-permute-done.53 = bf16[288,1536]{1,0:T(8,128)(2,1)S(1)} collective-permute-done((bf16[288,1536]{1,0:T(8,128)(2,1)S(1)}, bf16[288,1536]{1,0:T(8,128)(2,1)S(1)}, u32[]{:S(2)}, u32[]{:S(2)}) %collective-permute-start.53) | collective-permute-done | bytes 884768 | tf_op jit(solution)/shard_map/ppermute | solution.py:127
  837.4 9.1 %collective-permute-done.54 = bf16[288,1536]{1,0:T(8,128)(2,1)S(1)} collective-permute-done((bf16[288,1536]{1,0:T(8,128)(2,1)S(1)}, bf16[288,1536]{1,0:T(8,128)(2,1)S(1)}, u32[]{:S(2)}, u32[]{:S(2)}) %collective-permute-start.54) | collective-permute-done | bytes 884768 | tf_op jit(solution)/shard_map/ppermute | solution.py:127
  846.7 7.8 collective-permute-start.55
  857.7 13.3 %collective-permute-done.55 = bf16[288,1536]{1,0:T(8,128)(2,1)S(1)} collective-permute-done((bf16[288,1536]{1,0:T(8,128)(2,1)S(1)}, bf16[288,1536]{1,0:T(8,128)(2,1)S(1)}, u32[]{:S(2)}, u32[]{:S(2)}) %collective-permute-start.55) | collective-permute-done | bytes 884768 | tf_op jit(solution)/shard_map/ppermute | solution.py:127
  871.0 3.0 collective-permute-done.56
  875.3 4.2 all-to-all-start
  879.5 3.2 fusion.44
  883.5 5.5 all-to-all-done
  (525 shorter events, 164.5 us)
Async XLA Ops:
  298.0 15.7 %collective-permute-start.2 = (bf16[128,2304]{1,0:T(8,128)(2,1)S(1)}, bf16[128,2304]{1,0:T(8,128)(2,1)S(1)}, u32[]{:S(2)}, u32[]{:S(2)}) collective-permute-start(bf16[128,2304]{1,0:T(8,128)(2,1)S(1)} %fusion.58), channel_id=1, source_target_pairs={{0,2},{1,3},{2,0},{3,1},{4,6},{5,7},{6,4},{7,5},{8,10},{9,11},{10,... | collective-permute-start | bytes 1769480 | tf_op jit(solution)/shard_map/ppermute | solution.py:127
  317.5 14.8 %collective-permute-start.3 = (bf16[128,2304]{1,0:T(8,128)(2,1)S(1)}, bf16[128,2304]{1,0:T(8,128)(2,1)S(1)}, u32[]{:S(2)}, u32[]{:S(2)}) collective-permute-start(bf16[128,2304]{1,0:T(8,128)(2,1)S(1)} %get-tuple-element.186), channel_id=1, source_target_pairs={{0,8},{1,9},{2,0},{3,1},{4,12},{5,13},{6,4},{7,5},{8,16},{9,17},{1... | collective-permute-start | bytes 1769480 | tf_op jit(solution)/shard_map/ppermute | solution.py:127
  317.5 14.8 %collective-permute-start.4 = (bf16[128,2304]{1,0:T(8,128)(2,1)S(1)}, bf16[128,2304]{1,0:T(8,128)(2,1)S(1)}, u32[]{:S(2)}, u32[]{:S(2)}) collective-permute-start(bf16[128,2304]{1,0:T(8,128)(2,1)S(1)} %get-tuple-element.186), channel_id=1, source_target_pairs={{0,2},{1,3},{2,10},{3,11},{4,6},{5,7},{6,14},{7,15},{8,0},{9,1},{1... | collective-permute-start | bytes 1769480 | tf_op jit(solution)/shard_map/ppermute | solution.py:127
  332.3 13.9 %collective-permute-start.5 = (bf16[128,2304]{1,0:T(8,128)(2,1)S(1)}, bf16[128,2304]{1,0:T(8,128)(2,1)S(1)}, u32[]{:S(2)}, u32[]{:S(2)}) collective-permute-start(bf16[128,2304]{1,0:T(8,128)(2,1)S(1)} %collective-permute-done.3), channel_id=1, source_target_pairs={{0,8},{1,9},{2,0},{3,1},{4,12},{5,13},{6,4},{7,5},{8,16},{9,17},{1... | collective-permute-start | bytes 1769480 | tf_op jit(solution)/shard_map/ppermute | solution.py:127
  332.5 13.9 %collective-permute-start.6 = (bf16[128,2304]{1,0:T(8,128)(2,1)S(1)}, bf16[128,2304]{1,0:T(8,128)(2,1)S(1)}, u32[]{:S(2)}, u32[]{:S(2)}) collective-permute-start(bf16[128,2304]{1,0:T(8,128)(2,1)S(1)} %collective-permute-done.4), channel_id=1, source_target_pairs={{0,2},{1,3},{2,10},{3,11},{4,6},{5,7},{6,14},{7,15},{8,0},{9,1},{1... | collective-permute-start | bytes 1769480 | tf_op jit(solution)/shard_map/ppermute | solution.py:127
  346.4 13.0 %collective-permute-start.7 = (bf16[128,2304]{1,0:T(8,128)(2,1)S(1)}, bf16[128,2304]{1,0:T(8,128)(2,1)S(1)}, u32[]{:S(2)}, u32[]{:S(2)}) collective-permute-start(bf16[128,2304]{1,0:T(8,128)(2,1)S(1)} %collective-permute-done.5), channel_id=1, source_target_pairs={{0,8},{1,9},{2,0},{3,1},{4,12},{5,13},{6,4},{7,5},{8,16},{9,17},{1... | collective-permute-start | bytes 1769480 | tf_op jit(solution)/shard_map/ppermute | solution.py:127
  346.7 13.2 %collective-permute-start.8 = (bf16[128,2304]{1,0:T(8,128)(2,1)S(1)}, bf16[128,2304]{1,0:T(8,128)(2,1)S(1)}, u32[]{:S(2)}, u32[]{:S(2)}) collective-permute-start(bf16[128,2304]{1,0:T(8,128)(2,1)S(1)} %collective-permute-done.6), channel_id=1, source_target_pairs={{0,2},{1,3},{2,10},{3,11},{4,6},{5,7},{6,14},{7,15},{8,0},{9,1},{1... | collective-permute-start | bytes 1769480 | tf_op jit(solution)/shard_map/ppermute | solution.py:127
  360.0 6.8 collective-permute-start.9
  379.3 7.9 collective-permute-start.11
  380.0 7.2 collective-permute-start.12
  387.4 13.5 %collective-permute-start.13 = (bf16[128,2304]{1,0:T(8,128)(2,1)S(1)}, bf16[128,2304]{1,0:T(8,128)(2,1)S(1)}, u32[]{:S(2)}, u32[]{:S(2)}) collective-permute-start(bf16[128,2304]{1,0:T(8,128)(2,1)S(1)} %pad_maximum_fusion.2), channel_id=1, source_target_pairs={{0,8},{1,9},{2,0},{3,1},{4,12},{5,13},{6,4},{7,5},{8,16},{9,17},{1... | collective-permute-start | bytes 1769480 | tf_op jit(solution)/shard_map/ppermute | solution.py:127
  390.2 12.3 %collective-permute-start.14 = (bf16[128,2304]{1,0:T(8,128)(2,1)S(1)}, bf16[128,2304]{1,0:T(8,128)(2,1)S(1)}, u32[]{:S(2)}, u32[]{:S(2)}) collective-permute-start(bf16[128,2304]{1,0:T(8,128)(2,1)S(1)} %pad_maximum_fusion.3), channel_id=1, source_target_pairs={{0,2},{1,3},{2,10},{3,11},{4,6},{5,7},{6,14},{7,15},{8,0},{9,1},{1... | collective-permute-start | bytes 1769480 | tf_op jit(solution)/shard_map/ppermute | solution.py:127
  402.8 14.1 %collective-permute-start.15 = (bf16[128,2304]{1,0:T(8,128)(2,1)S(1)}, bf16[128,2304]{1,0:T(8,128)(2,1)S(1)}, u32[]{:S(2)}, u32[]{:S(2)}) collective-permute-start(bf16[128,2304]{1,0:T(8,128)(2,1)S(1)} %get-tuple-element.213), channel_id=1, source_target_pairs={{0,8},{1,9},{2,0},{3,1},{4,12},{5,13},{6,4},{7,5},{8,16},{9,17},{1... | collective-permute-start | bytes 1769480 | tf_op jit(solution)/shard_map/ppermute | solution.py:127
  406.1 14.0 %collective-permute-start.16 = (bf16[128,2304]{1,0:T(8,128)(2,1)S(1)}, bf16[128,2304]{1,0:T(8,128)(2,1)S(1)}, u32[]{:S(2)}, u32[]{:S(2)}) collective-permute-start(bf16[128,2304]{1,0:T(8,128)(2,1)S(1)} %get-tuple-element.212), channel_id=1, source_target_pairs={{0,2},{1,3},{2,10},{3,11},{4,6},{5,7},{6,14},{7,15},{8,0},{9,1},{1... | collective-permute-start | bytes 1769480 | tf_op jit(solution)/shard_map/ppermute | solution.py:127
  421.2 10.6 %collective-permute-start.17 = (bf16[128,2304]{1,0:T(8,128)(2,1)}, bf16[128,2304]{1,0:T(8,128)(2,1)S(1)}, u32[]{:S(2)}, u32[]{:S(2)}) collective-permute-start(bf16[128,2304]{1,0:T(8,128)(2,1)} %get-tuple-element.211), channel_id=1, source_target_pairs={{0,8},{1,9},{2,0},{3,1},{4,12},{5,13},{6,4},{7,5},{8,16},{9,17},{1... | collective-permute-start | bytes 1769480 | tf_op jit(solution)/shard_map/ppermute | solution.py:127
  423.5 10.7 %collective-permute-start.18 = (bf16[128,2304]{1,0:T(8,128)(2,1)S(1)}, bf16[128,2304]{1,0:T(8,128)(2,1)}, u32[]{:S(2)}, u32[]{:S(2)}) collective-permute-start(bf16[128,2304]{1,0:T(8,128)(2,1)S(1)} %get-tuple-element.210), channel_id=1, source_target_pairs={{0,2},{1,3},{2,10},{3,11},{4,6},{5,7},{6,14},{7,15},{8,0},{9,1},{1... | collective-permute-start | bytes 1769480 | tf_op jit(solution)/shard_map/ppermute | solution.py:127
  439.8 16.0 %collective-permute-start.19 = (bf16[128,2304]{1,0:T(8,128)(2,1)}, bf16[128,2304]{1,0:T(8,128)(2,1)}, u32[]{:S(2)}, u32[]{:S(2)}) collective-permute-start(bf16[128,2304]{1,0:T(8,128)(2,1)} %get-tuple-element.184), channel_id=1, source_target_pairs={{0,8},{1,9},{2,0},{3,1},{4,12},{5,13},{6,4},{7,5},{8,16},{9,17},{1... | collective-permute-start | bytes 1769480 | tf_op jit(solution)/shard_map/ppermute | solution.py:127
  440.7 15.2 %collective-permute-start.20 = (bf16[128,2304]{1,0:T(8,128)(2,1)}, bf16[128,2304]{1,0:T(8,128)(2,1)}, u32[]{:S(2)}, u32[]{:S(2)}) collective-permute-start(bf16[128,2304]{1,0:T(8,128)(2,1)} %get-tuple-element.184), channel_id=1, source_target_pairs={{0,2},{1,3},{2,10},{3,11},{4,6},{5,7},{6,14},{7,15},{8,0},{9,1},{1... | collective-permute-start | bytes 1769480 | tf_op jit(solution)/shard_map/ppermute | solution.py:127
  455.9 16.3 %collective-permute-start.21 = (bf16[128,2304]{1,0:T(8,128)(2,1)}, bf16[128,2304]{1,0:T(8,128)(2,1)S(1)}, u32[]{:S(2)}, u32[]{:S(2)}) collective-permute-start(bf16[128,2304]{1,0:T(8,128)(2,1)} %collective-permute-done.19), channel_id=1, source_target_pairs={{0,8},{1,9},{2,0},{3,1},{4,12},{5,13},{6,4},{7,5},{8,16},{9,17},{1... | collective-permute-start | bytes 1769480 | tf_op jit(solution)/shard_map/ppermute | solution.py:127
  456.8 15.4 %collective-permute-start.22 = (bf16[128,2304]{1,0:T(8,128)(2,1)}, bf16[128,2304]{1,0:T(8,128)(2,1)S(1)}, u32[]{:S(2)}, u32[]{:S(2)}) collective-permute-start(bf16[128,2304]{1,0:T(8,128)(2,1)} %collective-permute-done.20), channel_id=1, source_target_pairs={{0,2},{1,3},{2,10},{3,11},{4,6},{5,7},{6,14},{7,15},{8,0},{9,1},{1... | collective-permute-start | bytes 1769480 | tf_op jit(solution)/shard_map/ppermute | solution.py:127
  472.2 13.1 %collective-permute-start.23 = (bf16[128,2304]{1,0:T(8,128)(2,1)S(1)}, bf16[128,2304]{1,0:T(8,128)(2,1)S(1)}, u32[]{:S(2)}, u32[]{:S(2)}) collective-permute-start(bf16[128,2304]{1,0:T(8,128)(2,1)S(1)} %collective-permute-done.21), channel_id=1, source_target_pairs={{0,8},{1,9},{2,0},{3,1},{4,12},{5,13},{6,4},{7,5},{8,16},{9,17},{1... | collective-permute-start | bytes 1769480 | tf_op jit(solution)/shard_map/ppermute | solution.py:127
  472.4 12.9 %collective-permute-start.24 = (bf16[128,2304]{1,0:T(8,128)(2,1)S(1)}, bf16[128,2304]{1,0:T(8,128)(2,1)S(1)}, u32[]{:S(2)}, u32[]{:S(2)}) collective-permute-start(bf16[128,2304]{1,0:T(8,128)(2,1)S(1)} %collective-permute-done.22), channel_id=1, source_target_pairs={{0,2},{1,3},{2,10},{3,11},{4,6},{5,7},{6,14},{7,15},{8,0},{9,1},{1... | collective-permute-start | bytes 1769480 | tf_op jit(solution)/shard_map/ppermute | solution.py:127
  485.4 6.8 collective-permute-start.26
  487.2 7.2 collective-permute-start.25
  513.9 9.5 %collective-permute-start.27 = (bf16[64,2304]{1,0:T(8,128)(2,1)S(1)}, bf16[64,2304]{1,0:T(8,128)(2,1)S(1)}, u32[]{:S(2)}, u32[]{:S(2)}) collective-permute-start(bf16[64,2304]{1,0:T(8,128)(2,1)S(1)} %get-tuple-element.259), channel_id=1, source_target_pairs={{0,8},{1,9},{2,0},{3,1},{4,12},{5,13},{6,4},{7,5},{8,16},{9,17},{1... | collective-permute-start | bytes 884744 | tf_op jit(solution)/shard_map/ppermute | solution.py:127
  514.2 9.5 %collective-permute-start.28 = (bf16[64,2304]{1,0:T(8,128)(2,1)S(1)}, bf16[64,2304]{1,0:T(8,128)(2,1)S(1)}, u32[]{:S(2)}, u32[]{:S(2)}) collective-permute-start(bf16[64,2304]{1,0:T(8,128)(2,1)S(1)} %get-tuple-element.258), channel_id=1, source_target_pairs={{0,2},{1,3},{2,10},{3,11},{4,6},{5,7},{6,14},{7,15},{8,0},{9,1},{1... | collective-permute-start | bytes 884744 | tf_op jit(solution)/shard_map/ppermute | solution.py:127
  523.9 15.1 %collective-permute-start.29 = (bf16[128,2304]{1,0:T(8,128)(2,1)S(1)}, bf16[128,2304]{1,0:T(8,128)(2,1)S(1)}, u32[]{:S(2)}, u32[]{:S(2)}) collective-permute-start(bf16[128,2304]{1,0:T(8,128)(2,1)S(1)} %pad_maximum_fusion.4), channel_id=1, source_target_pairs={{0,8},{1,9},{2,0},{3,1},{4,12},{5,13},{6,4},{7,5},{8,16},{9,17},{1... | collective-permute-start | bytes 1769480 | tf_op jit(solution)/shard_map/ppermute | solution.py:127
  524.3 14.8 %collective-permute-start.30 = (bf16[128,2304]{1,0:T(8,128)(2,1)S(1)}, bf16[128,2304]{1,0:T(8,128)(2,1)S(1)}, u32[]{:S(2)}, u32[]{:S(2)}) collective-permute-start(bf16[128,2304]{1,0:T(8,128)(2,1)S(1)} %pad_maximum_fusion.5), channel_id=1, source_target_pairs={{0,2},{1,3},{2,10},{3,11},{4,6},{5,7},{6,14},{7,15},{8,0},{9,1},{1... | collective-permute-start | bytes 1769480 | tf_op jit(solution)/shard_map/ppermute | solution.py:127
  539.4 9.9 %collective-permute-start.31 = (bf16[128,2304]{1,0:T(8,128)(2,1)S(1)}, bf16[128,2304]{1,0:T(8,128)(2,1)S(1)}, u32[]{:S(2)}, u32[]{:S(2)}) collective-permute-start(bf16[128,2304]{1,0:T(8,128)(2,1)S(1)} %get-tuple-element.207), channel_id=1, source_target_pairs={{0,8},{1,9},{2,0},{3,1},{4,12},{5,13},{6,4},{7,5},{8,16},{9,17},{1... | collective-permute-start | bytes 1769480 | tf_op jit(solution)/shard_map/ppermute | solution.py:127
  540.0 9.9 %collective-permute-start.32 = (bf16[128,2304]{1,0:T(8,128)(2,1)S(1)}, bf16[128,2304]{1,0:T(8,128)(2,1)S(1)}, u32[]{:S(2)}, u32[]{:S(2)}) collective-permute-start(bf16[128,2304]{1,0:T(8,128)(2,1)S(1)} %get-tuple-element.206), channel_id=1, source_target_pairs={{0,2},{1,3},{2,10},{3,11},{4,6},{5,7},{6,14},{7,15},{8,0},{9,1},{1... | collective-permute-start | bytes 1769480 | tf_op jit(solution)/shard_map/ppermute | solution.py:127
  548.3 34.9 %collective-permute-start.65 = (bf16[2,2,288,1152]{3,2,0,1:T(8,128)(2,1)S(1)}, bf16[2,2,288,1152]{3,2,0,1:T(8,128)(2,1)S(1)}, u32[]{:S(2)}, u32[]{:S(2)}) collective-permute-start(bf16[2,2,288,1152]{3,2,0,1:T(8,128)(2,1)S(1)} %copy_bitcast_fusion), channel_id=1, source_target_pairs={{0,1},{1,0},{2,3},{3,2},{4,5},{5,4},{6,7},{7,6},{8,9},{9,8},{10,11... | collective-permute-start | bytes 7962632 | tf_op jit(solution)/shard_map/ppermute | solution.py:127
  550.1 14.3 %collective-permute-start.33 = (bf16[128,2304]{1,0:T(8,128)(2,1)S(1)}, bf16[128,2304]{1,0:T(8,128)(2,1)S(1)}, u32[]{:S(2)}, u32[]{:S(2)}) collective-permute-start(bf16[128,2304]{1,0:T(8,128)(2,1)S(1)} %get-tuple-element.205), channel_id=1, source_target_pairs={{0,8},{1,9},{2,0},{3,1},{4,12},{5,13},{6,4},{7,5},{8,16},{9,17},{1... | collective-permute-start | bytes 1769480 | tf_op jit(solution)/shard_map/ppermute | solution.py:127
  550.5 14.3 %collective-permute-start.34 = (bf16[128,2304]{1,0:T(8,128)(2,1)S(1)}, bf16[128,2304]{1,0:T(8,128)(2,1)S(1)}, u32[]{:S(2)}, u32[]{:S(2)}) collective-permute-start(bf16[128,2304]{1,0:T(8,128)(2,1)S(1)} %get-tuple-element.204), channel_id=1, source_target_pairs={{0,2},{1,3},{2,10},{3,11},{4,6},{5,7},{6,14},{7,15},{8,0},{9,1},{1... | collective-permute-start | bytes 1769480 | tf_op jit(solution)/shard_map/ppermute | solution.py:127
  563.5 74.6 %collective-permute-start.57 = (bf16[2,2,288,1152]{3,2,0,1:T(8,128)(2,1)}, bf16[2,2,288,1152]{3,2,0,1:T(8,128)(2,1)}, u32[]{:S(2)}, u32[]{:S(2)}) collective-permute-start(bf16[2,2,288,1152]{3,2,0,1:T(8,128)(2,1)} %copy_bitcast_fusion.2), channel_id=1, source_target_pairs={{0,1},{1,0},{2,3},{3,2},{4,5},{5,4},{6,7},{7,6},{8,9},{9,8},{10,11... | collective-permute-start | bytes 7962632 | tf_op jit(solution)/shard_map/ppermute | solution.py:127
  567.2 15.8 %collective-permute-start.35 = (bf16[128,2304]{1,0:T(8,128)(2,1)S(1)}, bf16[128,2304]{1,0:T(8,128)(2,1)S(1)}, u32[]{:S(2)}, u32[]{:S(2)}) collective-permute-start(bf16[128,2304]{1,0:T(8,128)(2,1)S(1)} %get-tuple-element.188), channel_id=1, source_target_pairs={{0,1},{1,0},{2,3},{3,2},{4,5},{5,4},{6,7},{7,6},{8,9},{9,8},{10,11... | collective-permute-start | bytes 1769480 | tf_op jit(solution)/shard_map/ppermute | solution.py:127
  567.3 15.7 %collective-permute-start.36 = (bf16[128,2304]{1,0:T(8,128)(2,1)S(1)}, bf16[128,2304]{1,0:T(8,128)(2,1)S(1)}, u32[]{:S(2)}, u32[]{:S(2)}) collective-permute-start(bf16[128,2304]{1,0:T(8,128)(2,1)S(1)} %get-tuple-element.188), channel_id=1, source_target_pairs={{0,2},{1,3},{2,0},{3,1},{4,6},{5,7},{6,4},{7,5},{8,10},{9,11},{10,... | collective-permute-start | bytes 1769480 | tf_op jit(solution)/shard_map/ppermute | solution.py:127
  578.7 73.2 %collective-permute-start.61 = (bf16[2,2,288,1152]{3,2,0,1:T(8,128)(2,1)}, bf16[2,2,288,1152]{3,2,0,1:T(8,128)(2,1)}, u32[]{:S(2)}, u32[]{:S(2)}) collective-permute-start(bf16[2,2,288,1152]{3,2,0,1:T(8,128)(2,1)} %copy_bitcast_fusion.1), channel_id=1, source_target_pairs={{0,1},{1,0},{2,3},{3,2},{4,5},{5,4},{6,7},{7,6},{8,9},{9,8},{10,11... | collective-permute-start | bytes 7962632 | tf_op jit(solution)/shard_map/ppermute | solution.py:127
  585.8 72.2 %collective-permute-start.66 = (bf16[576,1152]{1,0:T(8,128)(2,1)}, bf16[576,1152]{1,0:T(8,128)(2,1)}, u32[]{:S(2)}, u32[]{:S(2)}) collective-permute-start(bf16[576,1152]{1,0:T(8,128)(2,1)} %bitcast.75), channel_id=1, source_target_pairs={{0,4},{1,5},{2,6},{3,7},{4,0},{5,1},{6,2},{7,3},{8,12},{9,13},{10,... | collective-permute-start | bytes 3981320 | tf_op jit(solution)/shard_map/ppermute | solution.py:127
  625.2 8.8 collective-permute-start.38
  625.3 9.0 %collective-permute-start.39 = (bf16[256,512]{1,0:T(8,128)(2,1)S(1)}, bf16[256,512]{1,0:T(8,128)(2,1)S(1)}, u32[]{:S(2)}, u32[]{:S(2)}) collective-permute-start(bf16[256,512]{1,0:T(8,128)(2,1)S(1)} %get-tuple-element.232), channel_id=1, source_target_pairs={{0,4},{1,5},{2,6},{3,7},{4,12},{5,13},{6,14},{7,15},{8,0},{9,1},{1... | collective-permute-start | bytes 786440 | tf_op jit(solution)/shard_map/ppermute | solution.py:127
  634.4 14.8 %collective-permute-start.40 = (bf16[512,512]{1,0:T(8,128)(2,1)S(1)}, bf16[512,512]{1,0:T(8,128)(2,1)S(1)}, u32[]{:S(2)}, u32[]{:S(2)}) collective-permute-start(bf16[512,512]{1,0:T(8,128)(2,1)S(1)} %pad_maximum_fusion.8), channel_id=1, source_target_pairs={{0,8},{1,9},{2,10},{3,11},{4,0},{5,1},{6,2},{7,3},{8,16},{9,17},{1... | collective-permute-start | bytes 1572872 | tf_op jit(solution)/shard_map/ppermute | solution.py:127
  634.5 14.7 %collective-permute-start.41 = (bf16[512,512]{1,0:T(8,128)(2,1)S(1)}, bf16[512,512]{1,0:T(8,128)(2,1)S(1)}, u32[]{:S(2)}, u32[]{:S(2)}) collective-permute-start(bf16[512,512]{1,0:T(8,128)(2,1)S(1)} %pad_maximum_fusion.9), channel_id=1, source_target_pairs={{0,4},{1,5},{2,6},{3,7},{4,12},{5,13},{6,14},{7,15},{8,0},{9,1},{1... | collective-permute-start | bytes 1572872 | tf_op jit(solution)/shard_map/ppermute | solution.py:127
  641.1 49.0 %collective-permute-start.58 = (bf16[576,1152]{1,0:T(8,128)(2,1)S(1)}, bf16[576,1152]{1,0:T(8,128)(2,1)S(1)}, u32[]{:S(2)}, u32[]{:S(2)}) collective-permute-start(bf16[576,1152]{1,0:T(8,128)(2,1)S(1)} %bitcast.292), channel_id=1, source_target_pairs={{0,4},{1,5},{2,6},{3,7},{4,0},{5,1},{6,2},{7,3},{8,12},{9,13},{10,... | collective-permute-start | bytes 3981320 | tf_op jit(solution)/shard_map/ppermute | solution.py:127
  649.6 39.4 %collective-permute-start.42 = (bf16[512,512]{1,0:T(8,128)(2,1)S(1)}, bf16[512,512]{1,0:T(8,128)(2,1)S(1)}, u32[]{:S(2)}, u32[]{:S(2)}) collective-permute-start(bf16[512,512]{1,0:T(8,128)(2,1)S(1)} %get-tuple-element.229), channel_id=1, source_target_pairs={{0,8},{1,9},{2,10},{3,11},{4,0},{5,1},{6,2},{7,3},{8,16},{9,17},{1... | collective-permute-start | bytes 1572872 | tf_op jit(solution)/shard_map/ppermute | solution.py:127
  649.7 40.0 %collective-permute-start.43 = (bf16[512,512]{1,0:T(8,128)(2,1)S(1)}, bf16[512,512]{1,0:T(8,128)(2,1)S(1)}, u32[]{:S(2)}, u32[]{:S(2)}) collective-permute-start(bf16[512,512]{1,0:T(8,128)(2,1)S(1)} %get-tuple-element.228), channel_id=1, source_target_pairs={{0,4},{1,5},{2,6},{3,7},{4,12},{5,13},{6,14},{7,15},{8,0},{9,1},{1... | collective-permute-start | bytes 1572872 | tf_op jit(solution)/shard_map/ppermute | solution.py:127
  656.1 111.3 %collective-permute-start.62 = (bf16[576,1152]{1,0:T(8,128)(2,1)}, bf16[576,1152]{1,0:T(8,128)(2,1)}, u32[]{:S(2)}, u32[]{:S(2)}) collective-permute-start(bf16[576,1152]{1,0:T(8,128)(2,1)} %bitcast.66), channel_id=1, source_target_pairs={{0,4},{1,5},{2,6},{3,7},{4,0},{5,1},{6,2},{7,3},{8,12},{9,13},{10,... | collective-permute-start | bytes 3981320 | tf_op jit(solution)/shard_map/ppermute | solution.py:127
  660.0 33.4 %collective-permute-start.67 = (bf16[288,1152]{1,0:T(8,128)(2,1)S(1)}, bf16[288,1152]{1,0:T(8,128)(2,1)S(1)}, u32[]{:S(2)}, u32[]{:S(2)}) collective-permute-start(bf16[288,1152]{1,0:T(8,128)(2,1)S(1)} %get-tuple-element.267), channel_id=1, source_target_pairs={{8,0},{24,1},{10,2},{26,3},{12,4},{28,5},{14,6},{30,7},{0,8},{16,9... | collective-permute-start | bytes 1990664 | tf_op jit(solution)/shard_map/ppermute | solution.py:127
  690.0 37.4 %collective-permute-start.44 = (bf16[512,512]{1,0:T(8,128)(2,1)S(1)}, bf16[512,512]{1,0:T(8,128)(2,1)S(1)}, u32[]{:S(2)}, u32[]{:S(2)}) collective-permute-start(bf16[512,512]{1,0:T(8,128)(2,1)S(1)} %get-tuple-element.227), channel_id=1, source_target_pairs={{0,8},{1,9},{2,10},{3,11},{4,0},{5,1},{6,2},{7,3},{8,16},{9,17},{1... | collective-permute-start | bytes 1572872 | tf_op jit(solution)/shard_map/ppermute | solution.py:127
  690.0 37.3 %collective-permute-start.45 = (bf16[512,512]{1,0:T(8,128)(2,1)S(1)}, bf16[512,512]{1,0:T(8,128)(2,1)S(1)}, u32[]{:S(2)}, u32[]{:S(2)}) collective-permute-start(bf16[512,512]{1,0:T(8,128)(2,1)S(1)} %get-tuple-element.226), channel_id=1, source_target_pairs={{0,4},{1,5},{2,6},{3,7},{4,12},{5,13},{6,14},{7,15},{8,0},{9,1},{1... | collective-permute-start | bytes 1572872 | tf_op jit(solution)/shard_map/ppermute | solution.py:127
  693.5 86.8 %collective-permute-start.59 = (bf16[288,1152]{1,0:T(8,128)(2,1)}, bf16[288,1152]{1,0:T(8,128)(2,1)}, u32[]{:S(2)}, u32[]{:S(2)}) collective-permute-start(bf16[288,1152]{1,0:T(8,128)(2,1)} %get-tuple-element.275), channel_id=1, source_target_pairs={{8,0},{24,1},{10,2},{26,3},{12,4},{28,5},{14,6},{30,7},{0,8},{16,9... | collective-permute-start | bytes 1990664 | tf_op jit(solution)/shard_map/ppermute | solution.py:127
  693.6 86.8 %collective-permute-start.60 = (bf16[288,1152]{1,0:T(8,128)(2,1)}, bf16[288,1152]{1,0:T(8,128)(2,1)}, u32[]{:S(2)}, u32[]{:S(2)}) collective-permute-start(bf16[288,1152]{1,0:T(8,128)(2,1)} %get-tuple-element.274), channel_id=1, source_target_pairs={{0,0},{16,1},{2,2},{18,3},{4,4},{20,5},{6,6},{22,7},{8,8},{24,9},{... | collective-permute-start | bytes 1990664 | tf_op jit(solution)/shard_map/ppermute | solution.py:127
  762.8 54.9 %collective-permute-start.47 = (bf16[128,2304]{1,0:T(8,128)(2,1)S(1)}, bf16[128,2304]{1,0:T(8,128)(2,1)S(1)}, u32[]{:S(2)}, u32[]{:S(2)}) collective-permute-start(bf16[128,2304]{1,0:T(8,128)(2,1)S(1)} %get-tuple-element.223), channel_id=1, source_target_pairs={{0,1},{1,0},{2,3},{3,2},{4,5},{5,4},{6,7},{7,6},{8,9},{9,8},{10,11... | collective-permute-start | bytes 1769480 | tf_op jit(solution)/shard_map/ppermute | solution.py:127
  764.8 10.8 %collective-permute-start.49 = (bf16[144,1536]{1,0:T(8,128)(2,1)S(1)}, bf16[144,1536]{1,0:T(8,128)(2,1)S(1)}, u32[]{:S(2)}, u32[]{:S(2)}) collective-permute-start(bf16[144,1536]{1,0:T(8,128)(2,1)S(1)} %get-tuple-element.288), channel_id=1, source_target_pairs={{0,8},{1,9},{2,10},{3,11},{4,0},{5,1},{6,2},{7,3},{8,16},{9,17},{1... | collective-permute-start | bytes 1327112 | tf_op jit(solution)/shard_map/ppermute | solution.py:127
  767.3 10.6 %collective-permute-start.50 = (bf16[144,1536]{1,0:T(8,128)(2,1)S(1)}, bf16[144,1536]{1,0:T(8,128)(2,1)S(1)}, u32[]{:S(2)}, u32[]{:S(2)}) collective-permute-start(bf16[144,1536]{1,0:T(8,128)(2,1)S(1)} %get-tuple-element.287), channel_id=1, source_target_pairs={{0,4},{1,5},{2,6},{3,7},{4,12},{5,13},{6,14},{7,15},{8,0},{9,1},{1... | collective-permute-start | bytes 1327112 | tf_op jit(solution)/shard_map/ppermute | solution.py:127
  775.6 81.0 %collective-permute-start.46 = (bf16[128,2304]{1,0:T(8,128)(2,1)S(1)}, bf16[128,2304]{1,0:T(8,128)(2,1)S(1)}, u32[]{:S(2)}, u32[]{:S(2)}) collective-permute-start(bf16[128,2304]{1,0:T(8,128)(2,1)S(1)} %get-tuple-element.222), channel_id=1, source_target_pairs={{0,1},{1,0},{2,3},{3,2},{4,5},{5,4},{6,7},{7,6},{8,9},{9,8},{10,11... | collective-permute-start | bytes 1769480 | tf_op jit(solution)/shard_map/ppermute | solution.py:127
  777.9 39.9 %collective-permute-start.63 = (bf16[288,1152]{1,0:T(8,128)(2,1)S(1)}, bf16[288,1152]{1,0:T(8,128)(2,1)S(1)}, u32[]{:S(2)}, u32[]{:S(2)}) collective-permute-start(bf16[288,1152]{1,0:T(8,128)(2,1)S(1)} %get-tuple-element.271), channel_id=1, source_target_pairs={{8,0},{24,1},{10,2},{26,3},{12,4},{28,5},{14,6},{30,7},{0,8},{16,9... | collective-permute-start | bytes 1990664 | tf_op jit(solution)/shard_map/ppermute | solution.py:127
  780.3 33.6 %collective-permute-start.51 = (bf16[288,1536]{1,0:T(8,128)(2,1)S(1)}, bf16[288,1536]{1,0:T(8,128)(2,1)S(1)}, u32[]{:S(2)}, u32[]{:S(2)}) collective-permute-start(bf16[288,1536]{1,0:T(8,128)(2,1)S(1)} %fusion.63), channel_id=1, source_target_pairs={{0,8},{1,9},{2,10},{3,11},{4,0},{5,1},{6,2},{7,3},{8,16},{9,17},{1... | collective-permute-start | bytes 2654216 | tf_op jit(solution)/shard_map/ppermute | solution.py:127
  780.4 34.3 %collective-permute-start.52 = (bf16[288,1536]{1,0:T(8,128)(2,1)S(1)}, bf16[288,1536]{1,0:T(8,128)(2,1)S(1)}, u32[]{:S(2)}, u32[]{:S(2)}) collective-permute-start(bf16[288,1536]{1,0:T(8,128)(2,1)S(1)} %pad_maximum_fusion.1), channel_id=1, source_target_pairs={{0,4},{1,5},{2,6},{3,7},{4,12},{5,13},{6,14},{7,15},{8,0},{9,1},{1... | collective-permute-start | bytes 2654216 | tf_op jit(solution)/shard_map/ppermute | solution.py:127
  814.9 22.5 %collective-permute-start.53 = (bf16[288,1536]{1,0:T(8,128)(2,1)S(1)}, bf16[288,1536]{1,0:T(8,128)(2,1)S(1)}, u32[]{:S(2)}, u32[]{:S(2)}) collective-permute-start(bf16[288,1536]{1,0:T(8,128)(2,1)S(1)} %add_convert_fusion.3), channel_id=1, source_target_pairs={{0,8},{1,9},{2,10},{3,11},{4,0},{5,1},{6,2},{7,3},{8,16},{9,17},{1... | collective-permute-start | bytes 2654216 | tf_op jit(solution)/shard_map/ppermute | solution.py:127
  817.6 28.8 %collective-permute-start.54 = (bf16[288,1536]{1,0:T(8,128)(2,1)S(1)}, bf16[288,1536]{1,0:T(8,128)(2,1)S(1)}, u32[]{:S(2)}, u32[]{:S(2)}) collective-permute-start(bf16[288,1536]{1,0:T(8,128)(2,1)S(1)} %add_convert_fusion.2), channel_id=1, source_target_pairs={{0,4},{1,5},{2,6},{3,7},{4,12},{5,13},{6,14},{7,15},{8,0},{9,1},{1... | collective-permute-start | bytes 2654216 | tf_op jit(solution)/shard_map/ppermute | solution.py:127
  817.8 38.7 %collective-permute-start.48 = (bf16[128,2304]{1,0:T(8,128)(2,1)S(1)}, bf16[128,2304]{1,0:T(8,128)(2,1)S(1)}, u32[]{:S(2)}, u32[]{:S(2)}) collective-permute-start(bf16[128,2304]{1,0:T(8,128)(2,1)S(1)} %fusion.56), channel_id=1, source_target_pairs={{0,2},{1,3},{2,0},{3,1},{4,6},{5,7},{6,4},{7,5},{8,10},{9,11},{10,... | collective-permute-start | bytes 1769480 | tf_op jit(solution)/shard_map/ppermute | solution.py:127
  846.7 24.3 %collective-permute-start.55 = (bf16[288,1536]{1,0:T(8,128)(2,1)S(1)}, bf16[288,1536]{1,0:T(8,128)(2,1)S(1)}, u32[]{:S(2)}, u32[]{:S(2)}) collective-permute-start(bf16[288,1536]{1,0:T(8,128)(2,1)S(1)} %add_convert_fusion.1), channel_id=1, source_target_pairs={{0,8},{1,9},{2,10},{3,11},{4,0},{5,1},{6,2},{7,3},{8,16},{9,17},{1... | collective-permute-start | bytes 2654216 | tf_op jit(solution)/shard_map/ppermute | solution.py:127
  854.8 19.1 %collective-permute-start.56 = (bf16[288,1536]{1,0:T(8,128)(2,1)S(1)}, bf16[288,1536]{1,0:T(8,128)(2,1)S(1)}, u32[]{:S(2)}, u32[]{:S(2)}) collective-permute-start(bf16[288,1536]{1,0:T(8,128)(2,1)S(1)} %add_convert_fusion), channel_id=1, source_target_pairs={{0,4},{1,5},{2,6},{3,7},{4,12},{5,13},{6,14},{7,15},{8,0},{9,1},{1... | collective-permute-start | bytes 2654216 | tf_op jit(solution)/shard_map/ppermute | solution.py:127
  875.3 13.8 %all-to-all-start = ((bf16[4,72,1024]{2,1,0:T(8,128)(2,1)}), bf16[4,72,1024]{2,1,0:T(8,128)(2,1)}, u32[]{:S(2)}, u32[]{:S(2)}) async-start(bf16[4,72,1024]{2,1,0:T(8,128)(2,1)} %bitcast.289), calls=%async_computation | async-start | bytes 1179648 | tf_op jit(solution)/shard_map/all_to_all | solution.py:900
  (125 other events, 1826.8 us)
where the time goes:
time: 902 us; the launch traced here: 893 us
  Pallas kernels  306 us (34%)
  waiting for transfers between devices  277 us (31%)
  matrix products  103 us (11%)
  starting transfers between devices  92.2 us (10%)
  other arithmetic  62.4 us (7%)
  local copies, waits for them, and re-layouts  38.8 us (4%)
  between operations  13.3 us (1%)
    ppermute x79, waiting for transfers between devices, move(): return lax.ppermute(values, AXES, perm)  271 us
    pallas_call x1, Pallas kernels, fetch_keys(): pl.pallas_call(functools.partial(keys_kernel, plan), out_shape=[jax.Shape...  123 us
    pallas_call x1, Pallas kernels, fetch_weights(): pl.pallas_call(functools.partial(weights_kernel, plan), out_shape=results...  121 us
    dot_general x21, matrix products, dot(): lax.dot_general(left, right, (((left_dim,), (right_dim,)), ((), ())), pre...  103 us
    ppermute x79, starting transfers between devices, move(): return lax.ppermute(values, AXES, perm)  88 us
    pallas_call x1, Pallas kernels, attend_back(): pl.pallas_call(functools.partial(attend_back_kernel, span, repeat, count,...  34.3 us
    pallas_call x1, Pallas kernels, attend(): pl.pallas_call(functools.partial(attend_kernel, span, repeat, count), out...  27.9 us
    unnamed x252, local copies, waits for them, and re-layouts  18.3 us
  transfers between devices with their start and end apart: 80, of which 49 were waited for; matrix products, arithmetic and copies ran while one was open for 15% of the time, Pallas kernels for 4%

commit v1 on v0

--- a/solution.py
+++ b/solution.py
@@ -17,8 +17,6 @@
 gelu_coef = 0.7978845608028654
 cubic_coef = 0.044715
 
-
-BURST, LAG = 1, 1
 
 bf16 = jnp.bfloat16
 f32 = jnp.float32
@@ -307,23 +305,19 @@
             copy.wait_recv()
 
     def run(self, rings, slices):
-        going, queue, flying, moving, turn = [], list(rings), [], [], 0
+        flying, moving = [], []
         tasks = [(m, r, p) for m, r in slices for p in range(self.plan.halves)]
 
         def drive(generators):
             return [g for g in generators if next(g, "end") != "end"]
 
-        while going or queue or tasks or flying or moving:
-            going = drive(going)
-            if not going and queue:
-                going = drive(queue.pop(0))
-            for _ in range(BURST):
-                if tasks:
-                    matrix, result, p = tasks.pop(0)
-                    flying.append((result, p, self.slice_send(matrix, result, p)))
-            turn += 1
-            if flying and turn > LAG:
+        while rings or tasks or flying or moving:
+            rings = drive(rings)
+            if flying:
                 moving.append(self.slice_pass(*flying.pop(0)))
+            if tasks:
+                matrix, result, p = tasks.pop(0)
+                flying.append((result, p, self.slice_send(matrix, result, p)))
             moving = drive(moving)
 
 
@@ -378,8 +372,9 @@
         return lambda c: array.at[pl.ds(c * ulysses, ulysses)]
 
     rings = [
-        [link.ring(block(qkv), ulysses // 2), link.ring(block(gain_all), ulysses // 2)],
-        [link.ring(lambda c: out_all.at[c], out_all.shape[1] // 16 * 8)],
+        link.ring(block(qkv), ulysses // 2),
+        link.ring(block(gain_all), ulysses // 2),
+        link.ring(lambda c: out_all.at[c], out_all.shape[1] // 16 * 8),
     ]
     link.run(rings, [(gate_in, gate_all)])
     for copy in tokens:
@@ -424,7 +419,7 @@
     )(tokens, wq, wk, wv, w_out, gains, w_gate)
 
 
-def keys_kernel(plan, kv_in, up_in, down_in, kv_all, up_all, down_all, tmp, local, send, recv):
+def keys_kernel(plan, kv_in, up_in, kv_all, up_all, tmp, local, send, recv):
     link = Sender(plan, send, recv)
     link.meet()
     pull = pltpu.make_async_copy(kv_in, tmp, local.at[0])
@@ -433,22 +428,21 @@
     pull.wait()
     put.start()
     ring = link.ring(lambda c: kv_all.at[c], kv_in.shape[0] // 2, kv_in)
-    link.run([[ring]], [(up_in, up_all), (down_in, down_all)])
+    link.run([ring], [(up_in, up_all)])
     put.wait()
     link.finish()
 
 
-def fetch_keys(plan, kv, w_up, w_down):
-    copies = plan.contexts + copies_of(plan, 2)
+def fetch_keys(plan, kv, w_up):
+    copies = plan.contexts + copies_of(plan, 1)
     return pl.pallas_call(
         functools.partial(keys_kernel, plan),
         out_shape=[
             jax.ShapeDtypeStruct((plan.contexts, *kv.shape), kv.dtype),
             sliced(plan, w_up),
-            sliced(plan, w_down),
         ],
-        in_specs=[anywhere] * 3,
-        out_specs=[anywhere] * 3,
+        in_specs=[anywhere] * 2,
+        out_specs=[anywhere] * 2,
         scratch_shapes=[
             pltpu.VMEM(kv.shape, kv.dtype),
             pltpu.SemaphoreType.DMA((2,)),
@@ -456,7 +450,7 @@
             pltpu.SemaphoreType.DMA((copies,)),
         ],
         compiler_params=pltpu.CompilerParams(collective_id=2, has_side_effects=True),
-    )(kv, w_up, w_down)
+    )(kv, w_up)
 
 
 def visible(q_first, k_first, boundary, span):
@@ -471,150 +465,162 @@
     return (k_first <= q_first) & jnp.logical_not(split)
 
 
-def attend_kernel(span, repeat, count, qp, kp, bd, q_ref, kv_ref, o_ref, lse_ref, acc, den):
-    i, j = pl.program_id(0), pl.program_id(1)
-
-    @pl.when(j == 0)
+def whole(q_first, k_first, boundary, span):
+    same = (k_first >= boundary) | (q_first + span <= boundary)
+    return (k_first + span <= q_first) & same
+
+
+def over_pairs(span, blocks, chunk, qp, kp, bd, work):
+    start = pl.program_id(0) * chunk
+
+    def pair(t, carry):
+        i, j = t % blocks, t // blocks
+        q_first, k_first, boundary = qp[i], kp[start + j], bd[0]
+        q_rows = pl.ds(pl.multiple_of(i * span, span), span)
+        k_rows = pl.ds(pl.multiple_of(j * span, span), span)
+        full = whole(q_first, k_first, boundary, span)
+
+        @pl.when(full)
+        def _():
+            work(q_rows, k_rows, None)
+
+        @pl.when(active(q_first, k_first, boundary, span) & jnp.logical_not(full))
+        def _():
+            work(q_rows, k_rows, visible(q_first, k_first, boundary, span))
+
+        return carry
+
+    lax.fori_loop(0, blocks * chunk, pair, 0)
+
+
+def attend_kernel(span, repeat, steps, chunk, qp, kp, bd, q_ref, kv_ref, o_ref, lse_ref, acc, den):
+    step = pl.program_id(0)
+
+    @pl.when(step == 0)
     def _():
         acc[...] = jnp.zeros_like(acc)
         den[...] = jnp.zeros_like(den)
 
-    q_first, k_first, boundary = qp[i], kp[j], bd[0]
-
-    @pl.when(active(q_first, k_first, boundary, span))
-    def _():
-        allowed = visible(q_first, k_first, boundary, span)
-        keys, values = kv_ref[:, :HEAD_DIM], kv_ref[:, HEAD_DIM:]
+    def work(q_rows, k_rows, allowed):
+        keys, values = kv_ref[k_rows, :HEAD_DIM], kv_ref[k_rows, HEAD_DIM:]
         for r in range(repeat):
             cols = slice(r * HEAD_DIM, (r + 1) * HEAD_DIM)
-            scores = dot(q_ref[:, cols], keys, 1, 1)
-            weights = jnp.where(
-                allowed, jnp.exp(soft_cap * jnp.tanh(scores * (1.0 / soft_cap))), 0.0
-            )
-            den[r] += jnp.sum(weights, axis=1, keepdims=True)
-            acc[:, cols] += dot(weights.astype(bf16), values)
-
-    @pl.when(j == count - 1)
+            scores = dot(q_ref[q_rows, cols], keys, 1, 1)
+            weights = jnp.exp(soft_cap * jnp.tanh(scores * (1.0 / soft_cap)))
+            if allowed is not None:
+                weights = jnp.where(allowed, weights, 0.0)
+            folded = weights[:, :128]
+            for k in range(128, span, 128):
+                folded = folded + weights[:, k : k + 128]
+            den[q_rows, r * 128 : (r + 1) * 128] += folded
+            acc[q_rows, cols] += dot(weights.astype(bf16), values)
+
+    over_pairs(span, q_ref.shape[0] // span, chunk, qp, kp, bd, work)
+
+    @pl.when(step == steps - 1)
     def _():
         for r in range(repeat):
-            cols = slice(r * HEAD_DIM, (r + 1) * HEAD_DIM)
-            total = den[r][:, :1]
+            cols, lanes = slice(r * HEAD_DIM, (r + 1) * HEAD_DIM), slice(r * 128, (r + 1) * 128)
+            total = jnp.sum(den[:, lanes], axis=1, keepdims=True)
             o_ref[:, cols] = (acc[:, cols] / total).astype(bf16)
-            lse_ref[:, r * 128 : (r + 1) * 128] = jnp.broadcast_to(jnp.log(total), (span, 128))
+            lse_ref[:, lanes] = jnp.broadcast_to(jnp.log(total), den[:, lanes].shape)
+
+
+def key_chunk(count):
+    return next(c for c in (4, 2, 1) if count % c == 0)
 
 
 def attend(q, kv, q_pos, k_pos, boundary, span):
     rows, width = q.shape
     repeat = width // HEAD_DIM
     count = kv.shape[0] // span
+    chunk = key_chunk(count)
     spec = pltpu.PrefetchScalarGridSpec(
         num_scalar_prefetch=3,
-        grid=(rows // span, count),
+        grid=(count // chunk,),
         in_specs=[
-            pl.BlockSpec((span, width), lambda i, j, *_: (i, 0)),
-            pl.BlockSpec((span, kv.shape[1]), lambda i, j, *_: (j, 0)),
+            pl.BlockSpec((rows, width), lambda j, *_: (0, 0)),
+            pl.BlockSpec((chunk * span, kv.shape[1]), lambda j, *_: (j, 0)),
         ],
         out_specs=[
-            pl.BlockSpec((span, width), lambda i, j, *_: (i, 0)),
-            pl.BlockSpec((span, 128 * repeat), lambda i, j, *_: (i, 0)),
+            pl.BlockSpec((rows, width), lambda j, *_: (0, 0)),
+            pl.BlockSpec((rows, 128 * repeat), lambda j, *_: (0, 0)),
         ],
         scratch_shapes=[
-            pltpu.VMEM((span, width), f32),
-            pltpu.VMEM((repeat, span, 128), f32),
+            pltpu.VMEM((rows, width), f32),
+            pltpu.VMEM((rows, 128 * repeat), f32),
         ],
     )
-    flops = 2 * rows * kv.shape[0] * width
     return pl.pallas_call(
-        functools.partial(attend_kernel, span, repeat, count),
+        functools.partial(attend_kernel, span, repeat, count // chunk, chunk),
         out_shape=[
             jax.ShapeDtypeStruct((rows, width), bf16),
             jax.ShapeDtypeStruct((rows, 128 * repeat), f32),
         ],
         grid_spec=spec,
-        compiler_params=pltpu.CompilerParams(dimension_semantics=("arbitrary", "arbitrary")),
+        compiler_params=pltpu.CompilerParams(dimension_semantics=("arbitrary",)),
         cost_estimate=pl.CostEstimate(
-            flops=flops, bytes_accessed=2 * kv.size * 2, transcendentals=rows * kv.shape[0] * repeat
+            flops=2 * rows * kv.shape[0] * width,
+            bytes_accessed=2 * kv.size * 2,
+            transcendentals=rows * kv.shape[0] * repeat,
         ),
     )(q_pos, k_pos, boundary, q, kv)
 
 
 def attend_back_kernel(
-    span, repeat, count, blocks, qp, kp, bd, q_ref, g_ref, lse_ref, ds_ref, kv_ref, dq_ref, dkv_ref, acc, dk, dv
+    span, repeat, chunk, qp, kp, bd, q_ref, g_ref, lse_ref, ds_ref, kv_ref, dq_ref, dkv_ref, acc
 ):
-    j, i = pl.program_id(0), pl.program_id(1)
-
-    @pl.when((j == 0) & (i == 0))
+    step = pl.program_id(0)
+
+    @pl.when(step == 0)
     def _():
-        acc[...] = jnp.zeros_like(acc)
-
-    @pl.when(i == 0)
-    def _():
-        dk[...] = jnp.zeros_like(dk)
-        dv[...] = jnp.zeros_like(dv)
-
-    q_first, k_first, boundary = qp[i], kp[j], bd[0]
-
-    @pl.when(active(q_first, k_first, boundary, span))
-    def _():
-        allowed = visible(q_first, k_first, boundary, span)
-        keys, values = kv_ref[:, :HEAD_DIM], kv_ref[:, HEAD_DIM:]
-        rows = pl.ds(pl.multiple_of(i * span, span), span)
+        dq_ref[...] = jnp.zeros_like(dq_ref)
+
+    acc[...] = jnp.zeros_like(acc)
+
+    def work(q_rows, k_rows, allowed):
+        keys, values = kv_ref[k_rows, :HEAD_DIM], kv_ref[k_rows, HEAD_DIM:]
         for r in range(repeat):
             cols = slice(r * HEAD_DIM, (r + 1) * HEAD_DIM)
-            query, grad = q_ref[rows, cols], g_ref[rows, cols]
-            lse = lse_ref[rows, r * 128 : r * 128 + 1]
-            dsum = ds_ref[rows, r * 128 : r * 128 + 1]
+            query, grad = q_ref[q_rows, cols], g_ref[q_rows, cols]
+            lse = lse_ref[q_rows, r * 128 : r * 128 + 1]
+            dsum = ds_ref[q_rows, r * 128 : r * 128 + 1]
             bent = jnp.tanh(dot(query, keys, 1, 1) * (1.0 / soft_cap))
-            probs = jnp.where(allowed, jnp.exp(soft_cap * bent - lse), 0.0)
+            probs = jnp.exp(soft_cap * bent - lse)
+            if allowed is not None:
+                probs = jnp.where(allowed, probs, 0.0)
             dprob = dot(grad, values, 1, 1)
             dscore = (probs * (dprob - dsum) * (1.0 - bent * bent)).astype(bf16)
-            acc[rows, cols] += dot(dscore, keys)
-            dk[...] += dot(dscore, query, 0, 0)
-            dv[...] += dot(probs.astype(bf16), grad, 0, 0)
-
-    @pl.when(i == blocks - 1)
-    def _():
-        dkv_ref[:, :HEAD_DIM] = dk[...].astype(dkv_ref.dtype)
-        dkv_ref[:, HEAD_DIM:] = dv[...].astype(dkv_ref.dtype)
-
-    @pl.when((j == count - 1) & (i == blocks - 1))
-    def _():
-        dq_ref[...] = acc[...]
+            dq_ref[q_rows, cols] += dot(dscore, keys)
+            acc[k_rows, :HEAD_DIM] += dot(dscore, query, 0, 0)
+            acc[k_rows, HEAD_DIM:] += dot(probs.astype(bf16), grad, 0, 0)
+
+    over_pairs(span, q_ref.shape[0] // span, chunk, qp, kp, bd, work)
+    dkv_ref[...] = acc[...].astype(dkv_ref.dtype)
 
 
 def attend_back(q, grad, lse, dsum, kv, q_pos, k_pos, boundary, span):
     rows, width = q.shape
     repeat = width // HEAD_DIM
-    count, blocks = kv.shape[0] // span, rows // span
-    whole = lambda w: pl.BlockSpec((rows, w), lambda j, i, *_: (0, 0))
+    count = kv.shape[0] // span
+    chunk = key_chunk(count)
+    fixed = lambda w: pl.BlockSpec((rows, w), lambda j, *_: (0, 0))
+    moving = pl.BlockSpec((chunk * span, kv.shape[1]), lambda j, *_: (j, 0))
     spec = pltpu.PrefetchScalarGridSpec(
         num_scalar_prefetch=3,
-        grid=(count, blocks),
-        in_specs=[
-            whole(width),
-            whole(width),
-            whole(128 * repeat),
-            whole(128 * repeat),
-            pl.BlockSpec((span, kv.shape[1]), lambda j, i, *_: (j, 0)),
-        ],
-        out_specs=[
-            whole(width),
-            pl.BlockSpec((span, kv.shape[1]), lambda j, i, *_: (j, 0)),
-        ],
-        scratch_shapes=[
-            pltpu.VMEM((rows, width), f32),
-            pltpu.VMEM((span, HEAD_DIM), f32),
-            pltpu.VMEM((span, HEAD_DIM), f32),
-        ],
+        grid=(count // chunk,),
+        in_specs=[fixed(width), fixed(width), fixed(128 * repeat), fixed(128 * repeat), moving],
+        out_specs=[fixed(width), moving],
+        scratch_shapes=[pltpu.VMEM((chunk * span, kv.shape[1]), f32)],
     )
     return pl.pallas_call(
-        functools.partial(attend_back_kernel, span, repeat, count, blocks),
+        functools.partial(attend_back_kernel, span, repeat, chunk),
         out_shape=[
             jax.ShapeDtypeStruct((rows, width), f32),
             jax.ShapeDtypeStruct(kv.shape, bf16),
         ],
         grid_spec=spec,
-        compiler_params=pltpu.CompilerParams(dimension_semantics=("arbitrary", "arbitrary")),
+        compiler_params=pltpu.CompilerParams(dimension_semantics=("arbitrary",)),
         cost_estimate=pl.CostEstimate(
             flops=5 * rows * kv.shape[0] * width,
             bytes_accessed=2 * kv.size * 2,
@@ -750,11 +756,9 @@
     queries = (rotary(qkv[:, :q_cols], cosines, sines, 1.0) * q_scale).astype(bf16)
     keys = rotary(qkv[:, q_cols : q_cols + k_cols], cosines, sines, 1.0).astype(bf16)
     values = qkv[:, q_cols + k_cols :].astype(bf16)
-    kv, ffn_up, ffn_down = fetch_keys(
-        plan, jnp.concatenate([keys, values], axis=1), w_up, w_down
-    )
+    kv, ffn_up = fetch_keys(plan, jnp.concatenate([keys, values], axis=1), w_up)
     kv = kv.reshape(contexts * group_rows, -1)
-    ffn_gate, ffn_up, ffn_down = (w.reshape(width, -1) for w in (ffn_gate, ffn_up, ffn_down))
+    ffn_gate, ffn_up = ffn_gate.reshape(width, -1), ffn_up.reshape(width, -1)
 
     slice_cols = w_gate.shape[1] // halves
 
@@ -769,6 +773,22 @@
         for k in range(1, len(options)):
             out = jnp.where(index == k, options[k], out)
         return out
+
+    def slice_fetch(weights):
+        cuts = [weights[:, h * slice_cols : (h + 1) * slice_cols] for h in range(halves)]
+        size = weights.shape[0]
+        got = [move(pick(cuts, (layer + p) % halves), slice_perm(p)) for p in range(halves)]
+        sided = ring_gather(jnp.concatenate(got, axis=0), side_ring)
+        cored = ring_gather(jnp.concatenate(sided, axis=0), core_ring)
+        blocks, where = [], []
+        for m, found in enumerate(cored):
+            for k in range(sides):
+                for p in range(halves):
+                    n = k * halves + p
+                    blocks.append(found[n * size : (n + 1) * size])
+                    origin = (core + m) % cores * halves + (layer - p) % halves
+                    where.append(origin * sides + (side + k) % sides)
+        return place_rows(blocks, where, contexts).reshape(width, slice_cols)
 
     def slice_start(grad):
         parts = grad.reshape(cores, halves, sides, -1, slice_cols)
@@ -788,7 +808,8 @@
                 found = found + lax.dynamic_slice(other, (0, here, 0, 0), shape).astype(f32)
             return found.reshape(halves * size, slice_cols)
 
-        summed = ring_scatter([side_part(k) for k in range(sides)], side_ring, bf16)
+        sent = [side_part(k).astype(bf16) for k in range(1, sides)]
+        summed = ring_scatter([side_part(0), *sent], side_ring, bf16)
         return summed.astype(bf16).reshape(halves, size, slice_cols)
 
     def slice_end(summed):
@@ -799,6 +820,7 @@
         cuts = [pick(got, (h - layer) % halves) for h in range(halves)]
         return jnp.concatenate(cuts, axis=1).astype(f32)
 
+    ffn_down = slice_fetch(after(w_down, kv))
     head_o, lse = attend(queries, kv, own_spans, key_spans, boundary, span)
     attn_out = group_scatter(dot(head_o, col_out, 1, 1))
     tok_own = tokens.astype(f32)
@@ -857,14 +879,14 @@
     grad_hidden = cot_own + norm_grad(hidden_in, weight_three, d_mid)
     joined = [jnp.concatenate(x, axis=0) for x in (d_ffn, hidden, normed_mid, d_gate, d_upper)]
 
-    def weight_grad(left, right, step):
-        left = after(left, landed[min(step, len(landed) - 1)])
+    def weight_grad(left, right, earlier):
+        left = after(left, earlier)
         grad = dot(left, right, 0, 0).astype(bf16)
         return slice_start(grad)
 
-    sum_down = weight_grad(joined[0], joined[1], 0)
-    sum_gate = weight_grad(joined[2], joined[3], 1)
-    sum_up = weight_grad(joined[2], joined[4], 2)
+    sum_down = weight_grad(joined[0], joined[1], landed[0])
+    sum_gate = weight_grad(joined[2], joined[3], landed[min(1, len(landed) - 1)])
+    sum_up = weight_grad(joined[2], joined[4], d_mid)
     grad_down = slice_end(after(sum_down, d_mid))
     grad_gate = slice_end(after(sum_gate, d_mid))
 
@@ -885,18 +907,20 @@
         queries, grad_o, lse, dsum, kv, own_spans, key_spans, boundary, span
     )
     grad_kv = ctx_scatter([grad_kv])
-    grad_up = slice_end(after(sum_up, grad_kv))
+    grad_up = slice_end(after(sum_up, grad_q))
     grad_q = (rotary(grad_q, cosines, sines, -1.0) * q_scale).astype(bf16)
     grad_k = rotary(grad_kv[:, :k_cols], cosines, sines, -1.0).astype(bf16)
     grad_v = grad_kv[:, k_cols:].astype(bf16)
-    grad_qkv = jnp.concatenate([grad_q, grad_k, grad_v], axis=1)
-    d_in_part = dot(grad_qkv, col_qkv, 1, 1)
+    grad_kv = jnp.concatenate([grad_k, grad_v], axis=1)
+    q_part = dot(normed_in, grad_q, 0, 0).astype(bf16)
+    kv_part = dot(normed_in, grad_kv, 0, 0).astype(bf16)
+    d_in_part = dot(grad_q, col_qkv[:, :q_cols], 1, 1) + dot(grad_kv, col_qkv[:, q_cols:], 1, 1)
     d_in = group_scatter(d_in_part)
     grad_tokens = grad_hidden + norm_grad(tok_own, weight_one, d_in)
-    qkv_part = dot(normed_in, grad_qkv, 0, 0).astype(bf16)
-    mixed_grad = ctx_scatter([qkv_part, out_part])
-    grad_outproj = mixed_grad[:, qkv_part.shape[1] :]
-    mixed_grad = mixed_grad[:, : qkv_part.shape[1]].astype(bf16)
+    first_grad = ctx_scatter([q_part, out_part])
+    second_grad = ctx_scatter([kv_part])
+    grad_outproj = first_grad[:, q_cols:]
+    mixed_grad = jnp.concatenate([first_grad[:, :q_cols], second_grad], axis=1).astype(bf16)
     mixed_grad = lax.all_to_all(
         mixed_grad.reshape(ulysses, -1, mixed_grad.shape[1]),
         "uly",

time: 902 us -> 835 us (0.926)
  the two profiles are of different devices: /device:TPU:0 before, /device:TPU:8 now
where the time goes in v1:
time: 835 us; the launch traced here: 824 us
  waiting for transfers between devices  252 us (30%)
  Pallas kernels  211 us (25%)
  starting transfers between devices  148 us (18%)
  matrix products  102 us (12%)
  other arithmetic  59.3 us (7%)
  local copies, waits for them, and re-layouts  37.9 us (5%)
  between operations  14.1 us (2%)
    ppermute x91, waiting for transfers between devices, move(): return lax.ppermute(values, AXES, perm)  247 us
    ppermute x91, starting transfers between devices, move(): return lax.ppermute(values, AXES, perm)  145 us
    pallas_call x1, Pallas kernels, fetch_weights(): pl.pallas_call(functools.partial(weights_kernel, plan), out_shape=results...  111 us
    dot_general x23, matrix products, dot(): lax.dot_general(left, right, (((left_dim,), (right_dim,)), ((), ())), pre...  102 us
    pallas_call x1, Pallas kernels, fetch_keys(): pl.pallas_call(functools.partial(keys_kernel, plan), out_shape=[jax.Shape...  74.5 us
  transfers between devices with their start and end apart: 92, of which 55 were waited for; matrix products, arithmetic and copies ran while one was open for 17% of the time, Pallas kernels for 2%

profile of v1, /device:TPU:8, one launch (start us, length us, event | category | flops | bytes accessed | tf_op | source)
XLA Modules:
  0.0 824.4 jit_solution(9164893369745008411)
XLA Ops:
  2.1 110.5 %shard_map.255 = (bf16[4,128,2304]{2,1,0:T(8,128)(2,1)}, bf16[32,72,1024]{2,1,0:T(8,128)(2,1)}, bf16[8,288,512]{2,1,0:T(8,128)(2,1)}, f32[32,8,128]{2,1,0:T(8,128)}, bf16[8,288,1152]{2,1,0:T(8,128)(2,1)}) custom-call(bf16[128,2304]{1,0:T(8,128)(2,1)} %refs_0_.1, bf16[72,2048]{1,0:T(8,128)(2,1)} %refs_1_.1, bf16[72,1024]{1,0:T(8,128)(2,1)} %refs_2_.1, ...), custom_call_target="tpu_custom_call" | custom-call | tf_op jit(solution)/shard_map/pallas_call | solution.py:404
  120.9 2.6 fusion.168
  125.7 74.5 %shard_map.256 = (bf16[8,512,512]{2,1,0:T(8,128)(2,1)}, bf16[8,288,1152]{2,1,0:T(8,128)(2,1)}) custom-call(bf16[512,512]{1,0:T(8,128)(2,1)} %pad_maximum_fusion.8.kv_in, bf16[288,2304]{1,0:T(8,128)(2,1)} %up_in.1), custom_call_target="tpu_custom_call" | custom-call | tf_op jit(solution)/shard_map/pallas_call | solution.py:438
  201.1 10.6 %shard_map.257 = (bf16[512,512]{1,0:T(8,128)(2,1)}, f32[512,256]{1,0:T(8,128)}) custom-call(s32[2]{0:T(128)} %copy-done.75, s32[16]{0:T(128)} %broadcast_multiply_fusion.4.kp, s32[1]{0:T(128)} %bitcast.bd, bf16[512,512]{1,0:T(8,128)(2,1)} %fusion.63.q_ref, bf16[4096,512]{1,0:T(8,128)(2,1)} %bitcast.384), custom_call_target="tpu_custom_call" | custom-call | flops 2147483648 | bytes 8388608 | tf_op jit(solution)/shard_map/pallas_call | solution.py:554
  211.6 4.6 fusion.169
  216.2 2.9 fusion.71
  222.3 6.5 collective-permute-start.12
  232.1 19.0 %collective-permute-done.12 = bf16[288,1152]{1,0:T(8,128)(2,1)S(1)} collective-permute-done((bf16[288,1152]{1,0:T(8,128)(2,1)S(1)}, bf16[288,1152]{1,0:T(8,128)(2,1)S(1)}, u32[]{:S(2)}, u32[]{:S(2)}) %collective-permute-start.12) | collective-permute-done | bytes 663584 | tf_op jit(solution)/shard_map/ppermute | solution.py:125
  255.7 6.7 collective-permute-start.3
  262.6 13.4 %collective-permute-done.3 = bf16[128,2304]{1,0:T(8,128)(2,1)S(1)} collective-permute-done((bf16[128,2304]{1,0:T(8,128)(2,1)S(1)}, bf16[128,2304]{1,0:T(8,128)(2,1)S(1)}, u32[]{:S(2)}, u32[]{:S(2)}) %collective-permute-start.3) | collective-permute-done | bytes 589856 | tf_op jit(solution)/shard_map/ppermute | solution.py:125
  280.7 3.1 collective-permute-start.14
  283.9 9.3 %collective-permute-done.5 = bf16[128,2304]{1,0:T(8,128)(2,1)S(1)} collective-permute-done((bf16[128,2304]{1,0:T(8,128)(2,1)S(1)}, bf16[128,2304]{1,0:T(8,128)(2,1)S(1)}, u32[]{:S(2)}, u32[]{:S(2)}) %collective-permute-start.5) | collective-permute-done | bytes 589856 | tf_op jit(solution)/shard_map/ppermute | solution.py:125
  295.7 5.6 fusion.170
  301.3 6.1 collective-permute-done.7
  310.4 4.6 collective-permute-done.9
  316.7 2.5 fusion.171
  319.3 3.7 multiply_convert_fusion.4
  323.9 2.5 fusion.166
  328.8 5.8 multiply_convert_fusion.2
  335.3 2.4 collective-permute-start.17
  337.8 4.0 fusion.172
  341.8 5.8 collective-permute-done.17
  352.2 9.3 %collective-permute-done.19 = bf16[128,2304]{1,0:T(8,128)(2,1)S(1)} collective-permute-done((bf16[128,2304]{1,0:T(8,128)(2,1)S(1)}, bf16[128,2304]{1,0:T(8,128)(2,1)S(1)}, u32[]{:S(2)}, u32[]{:S(2)}) %collective-permute-start.19) | collective-permute-done | bytes 589856 | tf_op jit(solution)/shard_map/ppermute | solution.py:125
  367.4 7.3 collective-permute-done.21
  401.1 8.1 collective-permute-done.25
  409.2 2.5 collective-permute-done.26
  415.6 9.3 %multiply_convert_fusion.1 = (bf16[640,1152]{1,0:T(8,128)(2,1)}, bf16[640,1152]{1,0:T(8,128)(2,1)}) fusion(f32[640,1152]{1,0:T(8,128)S(1)} %copy-done.89, f32[640,1152]{1,0:T(8,128)S(1)} %copy-done.90, bf16[640,2304]{1,0:T(8,128)(2,1)S(1)} %get-tuple-element.317, bf16[2304,1152]{1,0:T(8,128)(2,1)} %bitcast.315), kind=kOutput, calls=%fused_computation.23 | convolution fusion | flops 3414343680 | bytes 17104896 | tf_op jit(solution)/shard_map/dot_general | solution.py:65
  428.7 4.1 collective-permute-done.30
  433.8 4.5 multiply_convert_fusion.3
  438.3 4.3 fusion.173
  442.6 4.6 fusion.167
  447.3 6.0 fusion.174
  455.5 7.7 convolution_add_fusion
  467.3 13.8 %collective-permute-done.33 = bf16[128,2304]{1,0:T(8,128)(2,1)S(1)} collective-permute-done((bf16[128,2304]{1,0:T(8,128)(2,1)S(1)}, bf16[128,2304]{1,0:T(8,128)(2,1)S(1)}, u32[]{:S(2)}, u32[]{:S(2)}) %collective-permute-start.33) | collective-permute-done | bytes 589856 | tf_op jit(solution)/shard_map/ppermute | solution.py:125
  484.7 6.6 convolution_convert_fusion
  495.3 8.0 convolution_convert_fusion.2
  512.2 6.6 convolution_convert_fusion.1
  522.1 4.6 collective-permute-done.40
  526.9 2.6 fusion.9
  529.6 2.4 collective-permute-start.78
  535.6 15.3 %shard_map.258 = (f32[512,512]{1,0:T(8,128)}, bf16[4096,512]{1,0:T(8,128)(2,1)}) custom-call(s32[2]{0:T(128)} %copy-done.75, s32[16]{0:T(128)} %broadcast_multiply_fusion.4.kp, s32[1]{0:T(128)} %bitcast.bd, bf16[512,512]{1,0:T(8,128)(2,1)} %fusion.63.q_ref, bf16[512,512]{1,0:T(8,128)(2,1)} %get-tuple-element.394.g_ref, ...), custom_call_target="tpu_custom_call" | custom-call | flops 5368709120 | bytes 8388608 | tf_op jit(solution)/shard_map/pallas_call | solution.py:616
  552.8 8.3 %collective-permute-start.43 = (bf16[256,512]{1,0:T(8,128)(2,1)S(1)}, bf16[256,512]{1,0:T(8,128)(2,1)S(1)}, u32[]{:S(2)}, u32[]{:S(2)}) collective-permute-start(bf16[256,512]{1,0:T(8,128)(2,1)S(1)} %get-tuple-element.240), channel_id=1, source_target_pairs={{0,4},{1,5},{2,6},{3,7},{4,12},{5,13},{6,14},{7,15},{8,0},{9,1},{1... | collective-permute-start | bytes 786440 | tf_op jit(solution)/shard_map/ppermute | solution.py:125
  561.1 3.2 convolution_convert_fusion.4
  564.3 3.4 collective-permute-done.42
  575.6 5.8 collective-permute-done.44
  582.6 2.4 collective-permute-start.47
  589.3 9.3 %collective-permute-done.46 = bf16[512,512]{1,0:T(8,128)(2,1)S(1)} collective-permute-done((bf16[512,512]{1,0:T(8,128)(2,1)S(1)}, bf16[512,512]{1,0:T(8,128)(2,1)S(1)}, u32[]{:S(2)}, u32[]{:S(2)}) %collective-permute-start.46) | collective-permute-done | bytes 524320 | tf_op jit(solution)/shard_map/ppermute | solution.py:125
  599.6 24.9 %collective-permute-start.48 = (bf16[512,512]{1,0:T(8,128)(2,1)S(1)}, bf16[512,512]{1,0:T(8,128)(2,1)S(1)}, u32[]{:S(2)}, u32[]{:S(2)}) collective-permute-start(bf16[512,512]{1,0:T(8,128)(2,1)S(1)} %get-tuple-element.235), channel_id=1, source_target_pairs={{0,8},{1,9},{2,10},{3,11},{4,0},{5,1},{6,2},{7,3},{8,16},{9,17},{1... | collective-permute-start | bytes 1572872 | tf_op jit(solution)/shard_map/ppermute | solution.py:125
  624.5 4.3 fusion.10
  632.6 6.7 collective-permute-start.72
  641.9 22.6 %collective-permute-done.49 = bf16[512,512]{1,0:T(8,128)(2,1)S(1)} collective-permute-done((bf16[512,512]{1,0:T(8,128)(2,1)S(1)}, bf16[512,512]{1,0:T(8,128)(2,1)S(1)}, u32[]{:S(2)}, u32[]{:S(2)}) %collective-permute-start.49) | collective-permute-done | bytes 524320 | tf_op jit(solution)/shard_map/ppermute | solution.py:125
  677.1 3.3 convolution_convert_fusion.3
  702.0 3.1 collective-permute-done.61
  707.3 5.8 collective-permute-done.53
  715.3 4.4 collective-permute-done.63
  728.7 13.1 %collective-permute-done.65 = bf16[288,512]{1,0:T(8,128)(2,1)S(1)} collective-permute-done((bf16[288,512]{1,0:T(8,128)(2,1)S(1)}, bf16[288,512]{1,0:T(8,128)(2,1)S(1)}, u32[]{:S(2)}, u32[]{:S(2)}) %collective-permute-start.65) | collective-permute-done | bytes 294944 | tf_op jit(solution)/shard_map/ppermute | solution.py:125
  752.1 2.8 collective-permute-done.67
  756.6 6.8 collective-permute-start.76
  763.9 5.9 collective-permute-done.57
  770.0 3.0 collective-permute-start.59
  774.9 20.1 %collective-permute-done.59 = bf16[288,1024]{1,0:T(8,128)(2,1)S(1)} collective-permute-done((bf16[288,1024]{1,0:T(8,128)(2,1)S(1)}, bf16[288,1024]{1,0:T(8,128)(2,1)S(1)}, u32[]{:S(2)}, u32[]{:S(2)}) %collective-permute-start.59) | collective-permute-done | bytes 589856 | tf_op jit(solution)/shard_map/ppermute | solution.py:125
  795.1 12.6 %collective-permute-done.60 = bf16[288,1024]{1,0:T(8,128)(2,1)S(1)} collective-permute-done((bf16[288,1024]{1,0:T(8,128)(2,1)S(1)}, bf16[288,1024]{1,0:T(8,128)(2,1)S(1)}, u32[]{:S(2)}, u32[]{:S(2)}) %collective-permute-start.60) | collective-permute-done | bytes 589856 | tf_op jit(solution)/shard_map/ppermute | solution.py:125
  808.9 3.5 all-to-all-start
  816.3 5.5 all-to-all-done
  (580 shorter events, 195.3 us)
Async XLA Ops:
  219.5 32.6 %collective-permute-start = (bf16[128,2304]{1,0:T(8,128)(2,1)}, bf16[128,2304]{1,0:T(8,128)(2,1)}, u32[]{:S(2)}, u32[]{:S(2)}) collective-permute-start(bf16[128,2304]{1,0:T(8,128)(2,1)} %get-tuple-element.232), channel_id=1, source_target_pairs={{0,1},{1,0},{2,3},{3,2},{4,5},{5,4},{6,7},{7,6},{8,9},{9,8},{10,11... | collective-permute-start | bytes 1769480 | tf_op jit(solution)/shard_map/ppermute | solution.py:125
  220.6 11.6 %collective-permute-start.11 = (bf16[288,1152]{1,0:T(8,128)(2,1)}, bf16[288,1152]{1,0:T(8,128)(2,1)S(1)}, u32[]{:S(2)}, u32[]{:S(2)}) collective-permute-start(bf16[288,1152]{1,0:T(8,128)(2,1)} %get-tuple-element.303), channel_id=1, source_target_pairs={{0,0},{1,16},{2,2},{3,18},{4,4},{5,20},{6,6},{7,22},{8,8},{9,24},{... | collective-permute-start | bytes 1990664 | tf_op jit(solution)/shard_map/ppermute | solution.py:125
  222.3 28.9 %collective-permute-start.12 = (bf16[288,1152]{1,0:T(8,128)(2,1)S(1)}, bf16[288,1152]{1,0:T(8,128)(2,1)S(1)}, u32[]{:S(2)}, u32[]{:S(2)}) collective-permute-start(bf16[288,1152]{1,0:T(8,128)(2,1)S(1)} %get-tuple-element.302), channel_id=1, source_target_pairs={{0,8},{1,24},{2,10},{3,26},{4,12},{5,28},{6,14},{7,30},{8,0},{9,16... | collective-permute-start | bytes 1990664 | tf_op jit(solution)/shard_map/ppermute | solution.py:125
  230.6 21.5 %collective-permute-start.2 = (bf16[128,2304]{1,0:T(8,128)(2,1)S(1)}, bf16[128,2304]{1,0:T(8,128)(2,1)S(1)}, u32[]{:S(2)}, u32[]{:S(2)}) collective-permute-start(bf16[128,2304]{1,0:T(8,128)(2,1)S(1)} %fusion.61), channel_id=1, source_target_pairs={{0,2},{1,3},{2,0},{3,1},{4,6},{5,7},{6,4},{7,5},{8,10},{9,11},{10,... | collective-permute-start | bytes 1769480 | tf_op jit(solution)/shard_map/ppermute | solution.py:125
  251.3 29.2 %collective-permute-start.13 = (bf16[576,1152]{1,0:T(8,128)(2,1)S(1)}, bf16[576,1152]{1,0:T(8,128)(2,1)S(1)}, u32[]{:S(2)}, u32[]{:S(2)}) collective-permute-start(bf16[576,1152]{1,0:T(8,128)(2,1)S(1)} %pad_maximum_fusion.1), channel_id=1, source_target_pairs={{0,4},{1,5},{2,6},{3,7},{4,0},{5,1},{6,2},{7,3},{8,12},{9,13},{10,... | collective-permute-start | bytes 3981320 | tf_op jit(solution)/shard_map/ppermute | solution.py:125
  255.7 20.3 %collective-permute-start.3 = (bf16[128,2304]{1,0:T(8,128)(2,1)S(1)}, bf16[128,2304]{1,0:T(8,128)(2,1)S(1)}, u32[]{:S(2)}, u32[]{:S(2)}) collective-permute-start(bf16[128,2304]{1,0:T(8,128)(2,1)S(1)} %get-tuple-element.202), channel_id=1, source_target_pairs={{0,8},{1,9},{2,0},{3,1},{4,12},{5,13},{6,4},{7,5},{8,16},{9,17},{1... | collective-permute-start | bytes 1769480 | tf_op jit(solution)/shard_map/ppermute | solution.py:125
  262.4 15.8 %collective-permute-start.4 = (bf16[128,2304]{1,0:T(8,128)(2,1)S(1)}, bf16[128,2304]{1,0:T(8,128)(2,1)S(1)}, u32[]{:S(2)}, u32[]{:S(2)}) collective-permute-start(bf16[128,2304]{1,0:T(8,128)(2,1)S(1)} %get-tuple-element.202), channel_id=1, source_target_pairs={{0,2},{1,3},{2,10},{3,11},{4,6},{5,7},{6,14},{7,15},{8,0},{9,1},{1... | collective-permute-start | bytes 1769480 | tf_op jit(solution)/shard_map/ppermute | solution.py:125
  278.2 15.0 %collective-permute-start.5 = (bf16[128,2304]{1,0:T(8,128)(2,1)S(1)}, bf16[128,2304]{1,0:T(8,128)(2,1)S(1)}, u32[]{:S(2)}, u32[]{:S(2)}) collective-permute-start(bf16[128,2304]{1,0:T(8,128)(2,1)S(1)} %collective-permute-done.3), channel_id=1, source_target_pairs={{0,8},{1,9},{2,0},{3,1},{4,12},{5,13},{6,4},{7,5},{8,16},{9,17},{1... | collective-permute-start | bytes 1769480 | tf_op jit(solution)/shard_map/ppermute | solution.py:125
  278.5 14.9 %collective-permute-start.6 = (bf16[128,2304]{1,0:T(8,128)(2,1)S(1)}, bf16[128,2304]{1,0:T(8,128)(2,1)S(1)}, u32[]{:S(2)}, u32[]{:S(2)}) collective-permute-start(bf16[128,2304]{1,0:T(8,128)(2,1)S(1)} %collective-permute-done.4), channel_id=1, source_target_pairs={{0,2},{1,3},{2,10},{3,11},{4,6},{5,7},{6,14},{7,15},{8,0},{9,1},{1... | collective-permute-start | bytes 1769480 | tf_op jit(solution)/shard_map/ppermute | solution.py:125
  280.7 42.3 %collective-permute-start.14 = (bf16[1152,1152]{1,0:T(8,128)(2,1)S(1)}, bf16[1152,1152]{1,0:T(8,128)(2,1)S(1)}, u32[]{:S(2)}, u32[]{:S(2)}) collective-permute-start(bf16[1152,1152]{1,0:T(8,128)(2,1)S(1)} %pad_maximum_fusion), channel_id=1, source_target_pairs={{0,1},{1,0},{2,3},{3,2},{4,5},{5,4},{6,7},{7,6},{8,9},{9,8},{10,11... | collective-permute-start | bytes 7962632 | tf_op jit(solution)/shard_map/ppermute | solution.py:125
  293.4 14.1 %collective-permute-start.7 = (bf16[128,2304]{1,0:T(8,128)(2,1)S(1)}, bf16[128,2304]{1,0:T(8,128)(2,1)S(1)}, u32[]{:S(2)}, u32[]{:S(2)}) collective-permute-start(bf16[128,2304]{1,0:T(8,128)(2,1)S(1)} %collective-permute-done.5), channel_id=1, source_target_pairs={{0,8},{1,9},{2,0},{3,1},{4,12},{5,13},{6,4},{7,5},{8,16},{9,17},{1... | collective-permute-start | bytes 1769480 | tf_op jit(solution)/shard_map/ppermute | solution.py:125
  294.1 14.0 %collective-permute-start.8 = (bf16[128,2304]{1,0:T(8,128)(2,1)S(1)}, bf16[128,2304]{1,0:T(8,128)(2,1)S(1)}, u32[]{:S(2)}, u32[]{:S(2)}) collective-permute-start(bf16[128,2304]{1,0:T(8,128)(2,1)S(1)} %collective-permute-done.6), channel_id=1, source_target_pairs={{0,2},{1,3},{2,10},{3,11},{4,6},{5,7},{6,14},{7,15},{8,0},{9,1},{1... | collective-permute-start | bytes 1769480 | tf_op jit(solution)/shard_map/ppermute | solution.py:125
  335.3 12.3 %collective-permute-start.17 = (bf16[128,2304]{1,0:T(8,128)(2,1)S(1)}, bf16[128,2304]{1,0:T(8,128)(2,1)S(1)}, u32[]{:S(2)}, u32[]{:S(2)}) collective-permute-start(bf16[128,2304]{1,0:T(8,128)(2,1)S(1)} %pad_maximum_fusion.2), channel_id=1, source_target_pairs={{0,8},{1,9},{2,0},{3,1},{4,12},{5,13},{6,4},{7,5},{8,16},{9,17},{1... | collective-permute-start | bytes 1769480 | tf_op jit(solution)/shard_map/ppermute | solution.py:125
  337.7 12.2 %collective-permute-start.18 = (bf16[128,2304]{1,0:T(8,128)(2,1)S(1)}, bf16[128,2304]{1,0:T(8,128)(2,1)S(1)}, u32[]{:S(2)}, u32[]{:S(2)}) collective-permute-start(bf16[128,2304]{1,0:T(8,128)(2,1)S(1)} %pad_maximum_fusion.3), channel_id=1, source_target_pairs={{0,2},{1,3},{2,10},{3,11},{4,6},{5,7},{6,14},{7,15},{8,0},{9,1},{1... | collective-permute-start | bytes 1769480 | tf_op jit(solution)/shard_map/ppermute | solution.py:125
  350.2 11.4 %collective-permute-start.19 = (bf16[128,2304]{1,0:T(8,128)(2,1)S(1)}, bf16[128,2304]{1,0:T(8,128)(2,1)S(1)}, u32[]{:S(2)}, u32[]{:S(2)}) collective-permute-start(bf16[128,2304]{1,0:T(8,128)(2,1)S(1)} %get-tuple-element.229), channel_id=1, source_target_pairs={{0,8},{1,9},{2,0},{3,1},{4,12},{5,13},{6,4},{7,5},{8,16},{9,17},{1... | collective-permute-start | bytes 1769480 | tf_op jit(solution)/shard_map/ppermute | solution.py:125
  351.7 11.3 %collective-permute-start.20 = (bf16[128,2304]{1,0:T(8,128)(2,1)S(1)}, bf16[128,2304]{1,0:T(8,128)(2,1)S(1)}, u32[]{:S(2)}, u32[]{:S(2)}) collective-permute-start(bf16[128,2304]{1,0:T(8,128)(2,1)S(1)} %get-tuple-element.228), channel_id=1, source_target_pairs={{0,2},{1,3},{2,10},{3,11},{4,6},{5,7},{6,14},{7,15},{8,0},{9,1},{1... | collective-permute-start | bytes 1769480 | tf_op jit(solution)/shard_map/ppermute | solution.py:125
  364.0 10.7 %collective-permute-start.21 = (bf16[128,2304]{1,0:T(8,128)(2,1)}, bf16[128,2304]{1,0:T(8,128)(2,1)}, u32[]{:S(2)}, u32[]{:S(2)}) collective-permute-start(bf16[128,2304]{1,0:T(8,128)(2,1)} %get-tuple-element.227), channel_id=1, source_target_pairs={{0,8},{1,9},{2,0},{3,1},{4,12},{5,13},{6,4},{7,5},{8,16},{9,17},{1... | collective-permute-start | bytes 1769480 | tf_op jit(solution)/shard_map/ppermute | solution.py:125
  365.9 10.0 %collective-permute-start.22 = (bf16[128,2304]{1,0:T(8,128)(2,1)S(1)}, bf16[128,2304]{1,0:T(8,128)(2,1)}, u32[]{:S(2)}, u32[]{:S(2)}) collective-permute-start(bf16[128,2304]{1,0:T(8,128)(2,1)S(1)} %get-tuple-element.226), channel_id=1, source_target_pairs={{0,2},{1,3},{2,10},{3,11},{4,6},{5,7},{6,14},{7,15},{8,0},{9,1},{1... | collective-permute-start | bytes 1769480 | tf_op jit(solution)/shard_map/ppermute | solution.py:125
  380.6 15.4 %collective-permute-start.23 = (bf16[128,2304]{1,0:T(8,128)(2,1)S(1)}, bf16[128,2304]{1,0:T(8,128)(2,1)S(1)}, u32[]{:S(2)}, u32[]{:S(2)}) collective-permute-start(bf16[128,2304]{1,0:T(8,128)(2,1)S(1)} %get-tuple-element.200), channel_id=1, source_target_pairs={{0,8},{1,9},{2,0},{3,1},{4,12},{5,13},{6,4},{7,5},{8,16},{9,17},{1... | collective-permute-start | bytes 1769480 | tf_op jit(solution)/shard_map/ppermute | solution.py:125
  382.2 13.8 %collective-permute-start.24 = (bf16[128,2304]{1,0:T(8,128)(2,1)S(1)}, bf16[128,2304]{1,0:T(8,128)(2,1)}, u32[]{:S(2)}, u32[]{:S(2)}) collective-permute-start(bf16[128,2304]{1,0:T(8,128)(2,1)S(1)} %get-tuple-element.200), channel_id=1, source_target_pairs={{0,2},{1,3},{2,10},{3,11},{4,6},{5,7},{6,14},{7,15},{8,0},{9,1},{1... | collective-permute-start | bytes 1769480 | tf_op jit(solution)/shard_map/ppermute | solution.py:125
  396.0 13.2 %collective-permute-start.25 = (bf16[128,2304]{1,0:T(8,128)(2,1)S(1)}, bf16[128,2304]{1,0:T(8,128)(2,1)S(1)}, u32[]{:S(2)}, u32[]{:S(2)}) collective-permute-start(bf16[128,2304]{1,0:T(8,128)(2,1)S(1)} %collective-permute-done.23), channel_id=1, source_target_pairs={{0,8},{1,9},{2,0},{3,1},{4,12},{5,13},{6,4},{7,5},{8,16},{9,17},{1... | collective-permute-start | bytes 1769480 | tf_op jit(solution)/shard_map/ppermute | solution.py:125
  397.6 14.1 %collective-permute-start.26 = (bf16[128,2304]{1,0:T(8,128)(2,1)}, bf16[128,2304]{1,0:T(8,128)(2,1)S(1)}, u32[]{:S(2)}, u32[]{:S(2)}) collective-permute-start(bf16[128,2304]{1,0:T(8,128)(2,1)} %collective-permute-done.24), channel_id=1, source_target_pairs={{0,2},{1,3},{2,10},{3,11},{4,6},{5,7},{6,14},{7,15},{8,0},{9,1},{1... | collective-permute-start | bytes 1769480 | tf_op jit(solution)/shard_map/ppermute | solution.py:125
  411.7 13.1 %collective-permute-start.27 = (bf16[128,2304]{1,0:T(8,128)(2,1)S(1)}, bf16[128,2304]{1,0:T(8,128)(2,1)S(1)}, u32[]{:S(2)}, u32[]{:S(2)}) collective-permute-start(bf16[128,2304]{1,0:T(8,128)(2,1)S(1)} %collective-permute-done.25), channel_id=1, source_target_pairs={{0,8},{1,9},{2,0},{3,1},{4,12},{5,13},{6,4},{7,5},{8,16},{9,17},{1... | collective-permute-start | bytes 1769480 | tf_op jit(solution)/shard_map/ppermute | solution.py:125
  413.5 12.5 %collective-permute-start.28 = (bf16[128,2304]{1,0:T(8,128)(2,1)S(1)}, bf16[128,2304]{1,0:T(8,128)(2,1)S(1)}, u32[]{:S(2)}, u32[]{:S(2)}) collective-permute-start(bf16[128,2304]{1,0:T(8,128)(2,1)S(1)} %collective-permute-done.26), channel_id=1, source_target_pairs={{0,2},{1,3},{2,10},{3,11},{4,6},{5,7},{6,14},{7,15},{8,0},{9,1},{1... | collective-permute-start | bytes 1769480 | tf_op jit(solution)/shard_map/ppermute | solution.py:125
  453.4 9.9 %collective-permute-start.31 = (bf16[64,2304]{1,0:T(8,128)(2,1)S(1)}, bf16[64,2304]{1,0:T(8,128)(2,1)S(1)}, u32[]{:S(2)}, u32[]{:S(2)}) collective-permute-start(bf16[64,2304]{1,0:T(8,128)(2,1)S(1)} %get-tuple-element.285), channel_id=1, source_target_pairs={{0,8},{1,9},{2,0},{3,1},{4,12},{5,13},{6,4},{7,5},{8,16},{9,17},{1... | collective-permute-start | bytes 884744 | tf_op jit(solution)/shard_map/ppermute | solution.py:125
  465.1 16.0 %collective-permute-start.33 = (bf16[128,2304]{1,0:T(8,128)(2,1)S(1)}, bf16[128,2304]{1,0:T(8,128)(2,1)S(1)}, u32[]{:S(2)}, u32[]{:S(2)}) collective-permute-start(bf16[128,2304]{1,0:T(8,128)(2,1)S(1)} %pad_maximum_fusion.4), channel_id=1, source_target_pairs={{0,8},{1,9},{2,0},{3,1},{4,12},{5,13},{6,4},{7,5},{8,16},{9,17},{1... | collective-permute-start | bytes 1769480 | tf_op jit(solution)/shard_map/ppermute | solution.py:125
  466.1 16.2 %collective-permute-start.34 = (bf16[128,2304]{1,0:T(8,128)(2,1)S(1)}, bf16[128,2304]{1,0:T(8,128)(2,1)S(1)}, u32[]{:S(2)}, u32[]{:S(2)}) collective-permute-start(bf16[128,2304]{1,0:T(8,128)(2,1)S(1)} %pad_maximum_fusion.5), channel_id=1, source_target_pairs={{0,2},{1,3},{2,10},{3,11},{4,6},{5,7},{6,14},{7,15},{8,0},{9,1},{1... | collective-permute-start | bytes 1769480 | tf_op jit(solution)/shard_map/ppermute | solution.py:125
  482.6 9.9 %collective-permute-start.35 = (bf16[128,2304]{1,0:T(8,128)(2,1)S(1)}, bf16[128,2304]{1,0:T(8,128)(2,1)S(1)}, u32[]{:S(2)}, u32[]{:S(2)}) collective-permute-start(bf16[128,2304]{1,0:T(8,128)(2,1)S(1)} %get-tuple-element.223), channel_id=1, source_target_pairs={{0,8},{1,9},{2,0},{3,1},{4,12},{5,13},{6,4},{7,5},{8,16},{9,17},{1... | collective-permute-start | bytes 1769480 | tf_op jit(solution)/shard_map/ppermute | solution.py:125
  491.5 35.4 %collective-permute-start.77 = (bf16[2,2,288,1152]{3,2,0,1:T(8,128)(2,1)S(1)}, bf16[2,2,288,1152]{3,2,0,1:T(8,128)(2,1)S(1)}, u32[]{:S(2)}, u32[]{:S(2)}) collective-permute-start(bf16[2,2,288,1152]{3,2,0,1:T(8,128)(2,1)S(1)} %copy_bitcast_fusion), channel_id=1, source_target_pairs={{0,1},{1,0},{2,3},{3,2},{4,5},{5,4},{6,7},{7,6},{8,9},{9,8},{10,11... | collective-permute-start | bytes 7962632 | tf_op jit(solution)/shard_map/ppermute | solution.py:125
  493.1 14.5 %collective-permute-start.37 = (bf16[128,2304]{1,0:T(8,128)(2,1)S(1)}, bf16[128,2304]{1,0:T(8,128)(2,1)S(1)}, u32[]{:S(2)}, u32[]{:S(2)}) collective-permute-start(bf16[128,2304]{1,0:T(8,128)(2,1)S(1)} %get-tuple-element.221), channel_id=1, source_target_pairs={{0,8},{1,9},{2,0},{3,1},{4,12},{5,13},{6,4},{7,5},{8,16},{9,17},{1... | collective-permute-start | bytes 1769480 | tf_op jit(solution)/shard_map/ppermute | solution.py:125
  493.2 14.6 %collective-permute-start.38 = (bf16[128,2304]{1,0:T(8,128)(2,1)S(1)}, bf16[128,2304]{1,0:T(8,128)(2,1)S(1)}, u32[]{:S(2)}, u32[]{:S(2)}) collective-permute-start(bf16[128,2304]{1,0:T(8,128)(2,1)S(1)} %get-tuple-element.220), channel_id=1, source_target_pairs={{0,2},{1,3},{2,10},{3,11},{4,6},{5,7},{6,14},{7,15},{8,0},{9,1},{1... | collective-permute-start | bytes 1769480 | tf_op jit(solution)/shard_map/ppermute | solution.py:125
  506.5 65.0 %collective-permute-start.69 = (bf16[2,2,288,1152]{3,2,0,1:T(8,128)(2,1)}, bf16[2,2,288,1152]{3,2,0,1:T(8,128)(2,1)}, u32[]{:S(2)}, u32[]{:S(2)}) collective-permute-start(bf16[2,2,288,1152]{3,2,0,1:T(8,128)(2,1)} %copy_bitcast_fusion.2), channel_id=1, source_target_pairs={{0,1},{1,0},{2,3},{3,2},{4,5},{5,4},{6,7},{7,6},{8,9},{9,8},{10,11... | collective-permute-start | bytes 7962632 | tf_op jit(solution)/shard_map/ppermute | solution.py:125
  511.0 15.8 %collective-permute-start.39 = (bf16[128,2304]{1,0:T(8,128)(2,1)S(1)}, bf16[128,2304]{1,0:T(8,128)(2,1)S(1)}, u32[]{:S(2)}, u32[]{:S(2)}) collective-permute-start(bf16[128,2304]{1,0:T(8,128)(2,1)S(1)} %get-tuple-element.204), channel_id=1, source_target_pairs={{0,1},{1,0},{2,3},{3,2},{4,5},{5,4},{6,7},{7,6},{8,9},{9,8},{10,11... | collective-permute-start | bytes 1769480 | tf_op jit(solution)/shard_map/ppermute | solution.py:125
  511.1 15.7 %collective-permute-start.40 = (bf16[128,2304]{1,0:T(8,128)(2,1)S(1)}, bf16[128,2304]{1,0:T(8,128)(2,1)S(1)}, u32[]{:S(2)}, u32[]{:S(2)}) collective-permute-start(bf16[128,2304]{1,0:T(8,128)(2,1)S(1)} %get-tuple-element.204), channel_id=1, source_target_pairs={{0,2},{1,3},{2,0},{3,1},{4,6},{5,7},{6,4},{7,5},{8,10},{9,11},{10,... | collective-permute-start | bytes 1769480 | tf_op jit(solution)/shard_map/ppermute | solution.py:125
  522.0 102.5 %collective-permute-start.73 = (bf16[2,2,288,1152]{3,2,0,1:T(8,128)(2,1)}, bf16[2,2,288,1152]{3,2,0,1:T(8,128)(2,1)}, u32[]{:S(2)}, u32[]{:S(2)}) collective-permute-start(bf16[2,2,288,1152]{3,2,0,1:T(8,128)(2,1)} %copy_bitcast_fusion.1), channel_id=1, source_target_pairs={{0,1},{1,0},{2,3},{3,2},{4,5},{5,4},{6,7},{7,6},{8,9},{9,8},{10,11... | collective-permute-start | bytes 7962632 | tf_op jit(solution)/shard_map/ppermute | solution.py:125
  529.6 55.4 %collective-permute-start.78 = (bf16[576,1152]{1,0:T(8,128)(2,1)}, bf16[576,1152]{1,0:T(8,128)(2,1)}, u32[]{:S(2)}, u32[]{:S(2)}) collective-permute-start(bf16[576,1152]{1,0:T(8,128)(2,1)} %bitcast.82), channel_id=1, source_target_pairs={{0,4},{1,5},{2,6},{3,7},{4,0},{5,1},{6,2},{7,3},{8,12},{9,13},{10,... | collective-permute-start | bytes 3981320 | tf_op jit(solution)/shard_map/ppermute | solution.py:125
  552.3 15.4 %collective-permute-start.42 = (bf16[256,512]{1,0:T(8,128)(2,1)S(1)}, bf16[256,512]{1,0:T(8,128)(2,1)S(1)}, u32[]{:S(2)}, u32[]{:S(2)}) collective-permute-start(bf16[256,512]{1,0:T(8,128)(2,1)S(1)} %get-tuple-element.239), channel_id=1, source_target_pairs={{0,8},{1,9},{2,10},{3,11},{4,0},{5,1},{6,2},{7,3},{8,16},{9,17},{1... | collective-permute-start | bytes 786440 | tf_op jit(solution)/shard_map/ppermute | solution.py:125
  552.8 15.0 %collective-permute-start.43 = (bf16[256,512]{1,0:T(8,128)(2,1)S(1)}, bf16[256,512]{1,0:T(8,128)(2,1)S(1)}, u32[]{:S(2)}, u32[]{:S(2)}) collective-permute-start(bf16[256,512]{1,0:T(8,128)(2,1)S(1)} %get-tuple-element.240), channel_id=1, source_target_pairs={{0,4},{1,5},{2,6},{3,7},{4,12},{5,13},{6,14},{7,15},{8,0},{9,1},{1... | collective-permute-start | bytes 786440 | tf_op jit(solution)/shard_map/ppermute | solution.py:125
  567.9 13.5 %collective-permute-start.44 = (bf16[512,512]{1,0:T(8,128)(2,1)S(1)}, bf16[512,512]{1,0:T(8,128)(2,1)S(1)}, u32[]{:S(2)}, u32[]{:S(2)}) collective-permute-start(bf16[512,512]{1,0:T(8,128)(2,1)S(1)} %pad_maximum_fusion.10), channel_id=1, source_target_pairs={{0,8},{1,9},{2,10},{3,11},{4,0},{5,1},{6,2},{7,3},{8,16},{9,17},{1... | collective-permute-start | bytes 1572872 | tf_op jit(solution)/shard_map/ppermute | solution.py:125
  568.0 13.5 %collective-permute-start.45 = (bf16[512,512]{1,0:T(8,128)(2,1)S(1)}, bf16[512,512]{1,0:T(8,128)(2,1)S(1)}, u32[]{:S(2)}, u32[]{:S(2)}) collective-permute-start(bf16[512,512]{1,0:T(8,128)(2,1)S(1)} %pad_maximum_fusion.11), channel_id=1, source_target_pairs={{0,4},{1,5},{2,6},{3,7},{4,12},{5,13},{6,14},{7,15},{8,0},{9,1},{1... | collective-permute-start | bytes 1572872 | tf_op jit(solution)/shard_map/ppermute | solution.py:125
  573.8 55.0 %collective-permute-start.70 = (bf16[576,1152]{1,0:T(8,128)(2,1)S(1)}, bf16[576,1152]{1,0:T(8,128)(2,1)S(1)}, u32[]{:S(2)}, u32[]{:S(2)}) collective-permute-start(bf16[576,1152]{1,0:T(8,128)(2,1)S(1)} %bitcast.334), channel_id=1, source_target_pairs={{0,4},{1,5},{2,6},{3,7},{4,0},{5,1},{6,2},{7,3},{8,12},{9,13},{10,... | collective-permute-start | bytes 3981320 | tf_op jit(solution)/shard_map/ppermute | solution.py:125
  581.8 16.8 %collective-permute-start.46 = (bf16[512,512]{1,0:T(8,128)(2,1)S(1)}, bf16[512,512]{1,0:T(8,128)(2,1)S(1)}, u32[]{:S(2)}, u32[]{:S(2)}) collective-permute-start(bf16[512,512]{1,0:T(8,128)(2,1)S(1)} %get-tuple-element.237), channel_id=1, source_target_pairs={{0,8},{1,9},{2,10},{3,11},{4,0},{5,1},{6,2},{7,3},{8,16},{9,17},{1... | collective-permute-start | bytes 1572872 | tf_op jit(solution)/shard_map/ppermute | solution.py:125
  582.6 16.7 %collective-permute-start.47 = (bf16[512,512]{1,0:T(8,128)(2,1)S(1)}, bf16[512,512]{1,0:T(8,128)(2,1)S(1)}, u32[]{:S(2)}, u32[]{:S(2)}) collective-permute-start(bf16[512,512]{1,0:T(8,128)(2,1)S(1)} %get-tuple-element.236), channel_id=1, source_target_pairs={{0,4},{1,5},{2,6},{3,7},{4,12},{5,13},{6,14},{7,15},{8,0},{9,1},{1... | collective-permute-start | bytes 1572872 | tf_op jit(solution)/shard_map/ppermute | solution.py:125
  587.1 43.5 %collective-permute-start.79 = (bf16[288,1152]{1,0:T(8,128)(2,1)S(1)}, bf16[288,1152]{1,0:T(8,128)(2,1)S(1)}, u32[]{:S(2)}, u32[]{:S(2)}) collective-permute-start(bf16[288,1152]{1,0:T(8,128)(2,1)S(1)} %get-tuple-element.293), channel_id=1, source_target_pairs={{8,0},{24,1},{10,2},{26,3},{12,4},{28,5},{14,6},{30,7},{0,8},{16,9... | collective-permute-start | bytes 1990664 | tf_op jit(solution)/shard_map/ppermute | solution.py:125
  598.6 34.0 %collective-permute-start.80 = (bf16[288,1152]{1,0:T(8,128)(2,1)S(1)}, bf16[288,1152]{1,0:T(8,128)(2,1)S(1)}, u32[]{:S(2)}, u32[]{:S(2)}) collective-permute-start(bf16[288,1152]{1,0:T(8,128)(2,1)S(1)} %get-tuple-element.292), channel_id=1, source_target_pairs={{0,0},{16,1},{2,2},{18,3},{4,4},{20,5},{6,6},{22,7},{8,8},{24,9},{... | collective-permute-start | bytes 1990664 | tf_op jit(solution)/shard_map/ppermute | solution.py:125
  599.6 42.3 %collective-permute-start.48 = (bf16[512,512]{1,0:T(8,128)(2,1)S(1)}, bf16[512,512]{1,0:T(8,128)(2,1)S(1)}, u32[]{:S(2)}, u32[]{:S(2)}) collective-permute-start(bf16[512,512]{1,0:T(8,128)(2,1)S(1)} %get-tuple-element.235), channel_id=1, source_target_pairs={{0,8},{1,9},{2,10},{3,11},{4,0},{5,1},{6,2},{7,3},{8,16},{9,17},{1... | collective-permute-start | bytes 1572872 | tf_op jit(solution)/shard_map/ppermute | solution.py:125
  624.5 39.9 %collective-permute-start.49 = (bf16[512,512]{1,0:T(8,128)(2,1)S(1)}, bf16[512,512]{1,0:T(8,128)(2,1)S(1)}, u32[]{:S(2)}, u32[]{:S(2)}) collective-permute-start(bf16[512,512]{1,0:T(8,128)(2,1)S(1)} %get-tuple-element.234), channel_id=1, source_target_pairs={{0,4},{1,5},{2,6},{3,7},{4,12},{5,13},{6,14},{7,15},{8,0},{9,1},{1... | collective-permute-start | bytes 1572872 | tf_op jit(solution)/shard_map/ppermute | solution.py:125
  628.8 118.7 %collective-permute-start.74 = (bf16[576,1152]{1,0:T(8,128)(2,1)}, bf16[576,1152]{1,0:T(8,128)(2,1)}, u32[]{:S(2)}, u32[]{:S(2)}) collective-permute-start(bf16[576,1152]{1,0:T(8,128)(2,1)} %bitcast.73), channel_id=1, source_target_pairs={{0,4},{1,5},{2,6},{3,7},{4,0},{5,1},{6,2},{7,3},{8,12},{9,13},{10,... | collective-permute-start | bytes 3981320 | tf_op jit(solution)/shard_map/ppermute | solution.py:125
  630.6 92.0 %collective-permute-start.71 = (bf16[288,1152]{1,0:T(8,128)(2,1)}, bf16[288,1152]{1,0:T(8,128)(2,1)}, u32[]{:S(2)}, u32[]{:S(2)}) collective-permute-start(bf16[288,1152]{1,0:T(8,128)(2,1)} %get-tuple-element.301), channel_id=1, source_target_pairs={{8,0},{24,1},{10,2},{26,3},{12,4},{28,5},{14,6},{30,7},{0,8},{16,9... | collective-permute-start | bytes 1990664 | tf_op jit(solution)/shard_map/ppermute | solution.py:125
  632.6 90.9 %collective-permute-start.72 = (bf16[288,1152]{1,0:T(8,128)(2,1)}, bf16[288,1152]{1,0:T(8,128)(2,1)}, u32[]{:S(2)}, u32[]{:S(2)}) collective-permute-start(bf16[288,1152]{1,0:T(8,128)(2,1)} %get-tuple-element.300), channel_id=1, source_target_pairs={{0,0},{16,1},{2,2},{18,3},{4,4},{20,5},{6,6},{22,7},{8,8},{24,9},{... | collective-permute-start | bytes 1990664 | tf_op jit(solution)/shard_map/ppermute | solution.py:125
  721.2 23.7 %collective-permute-start.55 = (bf16[288,1024]{1,0:T(8,128)(2,1)S(1)}, bf16[288,1024]{1,0:T(8,128)(2,1)S(1)}, u32[]{:S(2)}, u32[]{:S(2)}) collective-permute-start(bf16[288,1024]{1,0:T(8,128)(2,1)S(1)} %fusion.76), channel_id=1, source_target_pairs={{0,8},{1,9},{2,10},{3,11},{4,0},{5,1},{6,2},{7,3},{8,16},{9,17},{1... | collective-permute-start | bytes 1769480 | tf_op jit(solution)/shard_map/ppermute | solution.py:125
  722.6 23.6 %collective-permute-start.56 = (bf16[288,1024]{1,0:T(8,128)(2,1)S(1)}, bf16[288,1024]{1,0:T(8,128)(2,1)S(1)}, u32[]{:S(2)}, u32[]{:S(2)}) collective-permute-start(bf16[288,1024]{1,0:T(8,128)(2,1)S(1)} %pad_maximum_fusion.6), channel_id=1, source_target_pairs={{0,4},{1,5},{2,6},{3,7},{4,12},{5,13},{6,14},{7,15},{8,0},{9,1},{1... | collective-permute-start | bytes 1769480 | tf_op jit(solution)/shard_map/ppermute | solution.py:125
  723.5 18.4 %collective-permute-start.65 = (bf16[288,512]{1,0:T(8,128)(2,1)S(1)}, bf16[288,512]{1,0:T(8,128)(2,1)S(1)}, u32[]{:S(2)}, u32[]{:S(2)}) collective-permute-start(bf16[288,512]{1,0:T(8,128)(2,1)S(1)} %get-tuple-element.269), channel_id=1, source_target_pairs={{0,8},{1,9},{2,10},{3,11},{4,0},{5,1},{6,2},{7,3},{8,16},{9,17},{1... | collective-permute-start | bytes 884744 | tf_op jit(solution)/shard_map/ppermute | solution.py:125
  727.8 15.4 %collective-permute-start.66 = (bf16[288,512]{1,0:T(8,128)(2,1)S(1)}, bf16[288,512]{1,0:T(8,128)(2,1)S(1)}, u32[]{:S(2)}, u32[]{:S(2)}) collective-permute-start(bf16[288,512]{1,0:T(8,128)(2,1)S(1)} %get-tuple-element.268), channel_id=1, source_target_pairs={{0,4},{1,5},{2,6},{3,7},{4,12},{5,13},{6,14},{7,15},{8,0},{9,1},{1... | collective-permute-start | bytes 884744 | tf_op jit(solution)/shard_map/ppermute | solution.py:125
  741.8 14.7 %collective-permute-start.50 = (bf16[128,2304]{1,0:T(8,128)(2,1)S(1)}, bf16[128,2304]{1,0:T(8,128)(2,1)S(1)}, u32[]{:S(2)}, u32[]{:S(2)}) collective-permute-start(bf16[128,2304]{1,0:T(8,128)(2,1)S(1)} %copy-done.45), channel_id=1, source_target_pairs={{0,1},{1,0},{2,3},{3,2},{4,5},{5,4},{6,7},{7,6},{8,9},{9,8},{10,11... | collective-permute-start | bytes 1769480 | tf_op jit(solution)/shard_map/ppermute | solution.py:125
  743.2 20.2 %collective-permute-start.52 = (bf16[128,2304]{1,0:T(8,128)(2,1)S(1)}, bf16[128,2304]{1,0:T(8,128)(2,1)S(1)}, u32[]{:S(2)}, u32[]{:S(2)}) collective-permute-start(bf16[128,2304]{1,0:T(8,128)(2,1)S(1)} %fusion.59), channel_id=1, source_target_pairs={{0,2},{1,3},{2,0},{3,1},{4,6},{5,7},{6,4},{7,5},{8,10},{9,11},{10,... | collective-permute-start | bytes 1769480 | tf_op jit(solution)/shard_map/ppermute | solution.py:125
  745.0 9.9 %collective-permute-start.67 = (bf16[288,512]{1,0:T(8,128)(2,1)S(1)}, bf16[288,512]{1,0:T(8,128)(2,1)S(1)}, u32[]{:S(2)}, u32[]{:S(2)}) collective-permute-start(bf16[288,512]{1,0:T(8,128)(2,1)S(1)} %get-tuple-element.267), channel_id=1, source_target_pairs={{0,8},{1,9},{2,10},{3,11},{4,0},{5,1},{6,2},{7,3},{8,16},{9,17},{1... | collective-permute-start | bytes 884744 | tf_op jit(solution)/shard_map/ppermute | solution.py:125
  747.5 22.4 %collective-permute-start.57 = (bf16[288,1024]{1,0:T(8,128)(2,1)S(1)}, bf16[288,1024]{1,0:T(8,128)(2,1)S(1)}, u32[]{:S(2)}, u32[]{:S(2)}) collective-permute-start(bf16[288,1024]{1,0:T(8,128)(2,1)S(1)} %add_convert_fusion.3), channel_id=1, source_target_pairs={{0,8},{1,9},{2,10},{3,11},{4,0},{5,1},{6,2},{7,3},{8,16},{9,17},{1... | collective-permute-start | bytes 1769480 | tf_op jit(solution)/shard_map/ppermute | solution.py:125
  754.9 14.9 %collective-permute-start.58 = (bf16[288,1024]{1,0:T(8,128)(2,1)S(1)}, bf16[288,1024]{1,0:T(8,128)(2,1)S(1)}, u32[]{:S(2)}, u32[]{:S(2)}) collective-permute-start(bf16[288,1024]{1,0:T(8,128)(2,1)S(1)} %add_convert_fusion.2), channel_id=1, source_target_pairs={{0,4},{1,5},{2,6},{3,7},{4,12},{5,13},{6,14},{7,15},{8,0},{9,1},{1... | collective-permute-start | bytes 1769480 | tf_op jit(solution)/shard_map/ppermute | solution.py:125
  755.5 56.9 %collective-permute-start.75 = (bf16[288,1152]{1,0:T(8,128)(2,1)}, bf16[288,1152]{1,0:T(8,128)(2,1)}, u32[]{:S(2)}, u32[]{:S(2)}) collective-permute-start(bf16[288,1152]{1,0:T(8,128)(2,1)} %get-tuple-element.297), channel_id=1, source_target_pairs={{8,0},{24,1},{10,2},{26,3},{12,4},{28,5},{14,6},{30,7},{0,8},{16,9... | collective-permute-start | bytes 1990664 | tf_op jit(solution)/shard_map/ppermute | solution.py:125
  756.6 55.8 %collective-permute-start.76 = (bf16[288,1152]{1,0:T(8,128)(2,1)}, bf16[288,1152]{1,0:T(8,128)(2,1)}, u32[]{:S(2)}, u32[]{:S(2)}) collective-permute-start(bf16[288,1152]{1,0:T(8,128)(2,1)} %get-tuple-element.296), channel_id=1, source_target_pairs={{0,0},{16,1},{2,2},{18,3},{4,4},{20,5},{6,6},{22,7},{8,8},{24,9},{... | collective-permute-start | bytes 1990664 | tf_op jit(solution)/shard_map/ppermute | solution.py:125
  770.0 25.0 %collective-permute-start.59 = (bf16[288,1024]{1,0:T(8,128)(2,1)S(1)}, bf16[288,1024]{1,0:T(8,128)(2,1)S(1)}, u32[]{:S(2)}, u32[]{:S(2)}) collective-permute-start(bf16[288,1024]{1,0:T(8,128)(2,1)S(1)} %add_convert_fusion.1), channel_id=1, source_target_pairs={{0,8},{1,9},{2,10},{3,11},{4,0},{5,1},{6,2},{7,3},{8,16},{9,17},{1... | collective-permute-start | bytes 1769480 | tf_op jit(solution)/shard_map/ppermute | solution.py:125
  773.3 34.4 %collective-permute-start.60 = (bf16[288,1024]{1,0:T(8,128)(2,1)S(1)}, bf16[288,1024]{1,0:T(8,128)(2,1)S(1)}, u32[]{:S(2)}, u32[]{:S(2)}) collective-permute-start(bf16[288,1024]{1,0:T(8,128)(2,1)S(1)} %add_convert_fusion), channel_id=1, source_target_pairs={{0,4},{1,5},{2,6},{3,7},{4,12},{5,13},{6,14},{7,15},{8,0},{9,1},{1... | collective-permute-start | bytes 1769480 | tf_op jit(solution)/shard_map/ppermute | solution.py:125
  808.9 13.0 %all-to-all-start = ((bf16[4,72,1024]{2,1,0:T(8,128)(2,1)}), bf16[4,72,1024]{2,1,0:T(8,128)(2,1)S(1)}, u32[]{:S(2)}, u32[]{:S(2)}) async-start(bf16[4,72,1024]{2,1,0:T(8,128)(2,1)} %pad_maximum_fusion.7), calls=%async_computation | async-start | bytes 1179648 | tf_op jit(solution)/shard_map/all_to_all | solution.py:924
  (141 other events, 1888.8 us)

commit v2 on v1

--- a/solution.py
+++ b/solution.py
@@ -453,6 +453,163 @@
     )(kv, w_up)
 
 
+def grads_kernel(plan, q_in, kv_in, out_in, rows_in, gain_in, *refs):
+    parts = (q_in, kv_in, out_in)
+    lows = (0, q_in.shape[2], q_in.shape[2] + kv_in.shape[2])
+    query_out, key_out, value_out, out_out, rows_out, gain_out = refs[:6]
+    main_send, main_recv, gain_send, gain_recv, turn_send, turn_recv, gain_last, gain_turn = refs[6:14]
+    core_recv, row_send, row_recv, send, recv = refs[14:]
+    link = Sender(plan, send, recv)
+    count, ulysses, cores = plan.contexts, plan.ulysses, plan.cores
+    middle = count // 2
+    ctx, uly = link.ctx, link.uly
+    ahead = {"ctx": link.spot((link.here + 1) % count), "uly": uly}
+    behind = {"ctx": link.spot((link.here + count - 1) % count), "uly": uly}
+    link.meet()
+
+    half = max(ulysses // 2, 1)
+    lanes = [range(half), range(half, ulysses)]
+
+    def pass_on(step, way, lane):
+        left = middle - step
+        there = link.spot((link.here + (left if way == 0 else count - left)) % count)
+        received = step > 1 or (step == 1 and lane == way)
+        for m in lanes[lane]:
+            place = there * ulysses + m
+            gain = gain_in[place]
+            for array, low in zip(parts, lows, strict=True):
+                high = low + array.shape[2]
+                block = array[place]
+                if received:
+                    block = block.astype(f32) + main_recv[step - 1, way, m, :, low:high].astype(f32)
+                main_send[step, way, m, :, low:high] = block.astype(bf16)
+            gain_send[step, way, m] = gain + gain_recv[step - 1, way, m] if received else gain
+        device = ahead if way == 0 else behind
+        rows = pl.ds(lanes[lane][0], len(lanes[lane]))
+        return [
+            link.push(main_send.at[step, way, rows], main_recv.at[step, way, rows], device),
+            link.push(gain_send.at[step, way, rows], gain_recv.at[step, way, rows], device),
+        ]
+
+    last = {}
+    core_copies, row_copies = [], []
+    for step in range(middle):
+        sent = {}
+        for lane in range(2):
+            for way in range(2):
+                for copy in last.get((lane, way), ()):
+                    copy.wait_recv()
+                if step or lane == way:
+                    sent[lane, way] = pass_on(step, way, lane)
+        last = sent
+        if step == 0:
+            for dc in range(1, cores):
+                core = (link.core + dc) % cores
+                for r in range(plan.rows):
+                    device = link.at(link.layer, link.side, link.row, core)
+                    source = rows_in.at[r * cores + core]
+                    core_copies.append(link.push(source, core_recv.at[dc - 1, r], device))
+        if step == min(1, middle - 1):
+            for copy in core_copies:
+                copy.wait_recv()
+
+            def total(r):
+                found = rows_in[r * cores + link.core].astype(f32)
+                for dc in range(1, cores):
+                    found = found + core_recv[dc - 1, r].astype(f32)
+                return found
+
+            for dr in range(1, plan.rows):
+                row_send[dr - 1] = total((link.row + dr) % plan.rows).astype(bf16)
+            rows_out[...] = total(link.row)
+            for dr in range(1, plan.rows):
+                device = link.at(link.layer, link.side, (link.row + dr) % plan.rows, link.core)
+                row_copies.append(link.push(row_send.at[dr - 1], row_recv.at[dr - 1], device))
+    for copies in last.values():
+        for copy in copies:
+            copy.wait_recv()
+    place = ctx * ulysses
+
+    def finish(m, array, received, low):
+        high = low + array.shape[2]
+        found = array[place + m].astype(f32)
+        if middle > 1:
+            return found + received[middle - 1, 0, m, :, low:high].astype(f32) + received[
+                middle - 1, 1, m, :, low:high
+            ].astype(f32)
+        way = 0 if m < ulysses // 2 else 1
+        return found + received[0, way, m, :, low:high].astype(f32)
+
+    for m in range(ulysses):
+        turn_send[m, :, : lows[1]] = finish(m, q_in, main_recv, 0).astype(bf16)
+        turn_send[m, :, lows[1] :] = finish(m, kv_in, main_recv, lows[1]).astype(bf16)
+        gain_last[m] = finish(m, gain_in, gain_recv, 0)
+    turn_recv[uly] = turn_send[uly]
+    gain_turn[uly] = gain_last[uly]
+    turned = []
+    for friend, u in link.group():
+        turned.append(link.push(turn_send.at[u], turn_recv.at[uly], friend))
+        turned.append(link.push(gain_last.at[u], gain_turn.at[uly], friend))
+    for m in range(ulysses):
+        out_out[m] = finish(m, out_in, main_recv, lows[2])
+    for dr, copy in enumerate(row_copies):
+        copy.wait_recv()
+        rows_out[...] += row_recv[dr].astype(f32)
+    for copy in turned:
+        copy.wait_recv()
+    q_cols, k_cols = query_out.shape[1] // ulysses, key_out.shape[1] // ulysses
+    for u in range(ulysses):
+        query_out[:, u * q_cols : (u + 1) * q_cols] = turn_recv[u, :, :q_cols].astype(f32)
+        cols = slice(u * k_cols, (u + 1) * k_cols)
+        key_out[:, cols] = turn_recv[u, :, q_cols : q_cols + k_cols].astype(f32)
+        value_out[:, cols] = turn_recv[u, :, q_cols + k_cols :].astype(f32)
+    gain_out[...] = gain_turn[0]
+    for u in range(1, ulysses):
+        gain_out[...] += gain_turn[u]
+    link.finish()
+
+
+def sum_grads(plan, q, kv, out, rows, gains, q_width, k_width):
+    contexts, ulysses = plan.contexts, plan.ulysses
+    shard = q.shape[1]
+    turned = (ulysses, shard, q.shape[2] + kv.shape[2])
+    middle, tail = contexts // 2, gains.shape[1:]
+    wide = (shard, turned[2] + out.shape[2])
+    block = rows.shape[1:]
+    results = [
+        jax.ShapeDtypeStruct((shard, q_width), f32),
+        jax.ShapeDtypeStruct((shard, k_width), f32),
+        jax.ShapeDtypeStruct((shard, k_width), f32),
+        jax.ShapeDtypeStruct((ulysses, *out.shape[1:]), f32),
+        jax.ShapeDtypeStruct(block, f32),
+        jax.ShapeDtypeStruct(tail, f32),
+    ]
+    copies = 8 * middle + (plan.cores - 1) * plan.rows + plan.rows - 1 + 2 * (ulysses - 1)
+    local = pl.BlockSpec(memory_space=pltpu.VMEM)
+    return pl.pallas_call(
+        functools.partial(grads_kernel, plan),
+        out_shape=results,
+        in_specs=[local] * 5,
+        out_specs=[local] * len(results),
+        scratch_shapes=[
+            pltpu.VMEM((middle, 2, ulysses, *wide), bf16),
+            pltpu.VMEM((middle, 2, ulysses, *wide), bf16),
+            pltpu.VMEM((middle, 2, ulysses, *tail), f32),
+            pltpu.VMEM((middle, 2, ulysses, *tail), f32),
+            pltpu.VMEM(turned, bf16),
+            pltpu.VMEM(turned, bf16),
+            pltpu.VMEM((ulysses, *tail), f32),
+            pltpu.VMEM((ulysses, *tail), f32),
+            pltpu.VMEM((max(plan.cores - 1, 1), plan.rows, *block), bf16),
+            pltpu.VMEM((max(plan.rows - 1, 1), *block), bf16),
+            pltpu.VMEM((max(plan.rows - 1, 1), *block), bf16),
+            pltpu.SemaphoreType.DMA((copies,)),
+            pltpu.SemaphoreType.DMA((copies,)),
+        ],
+        compiler_params=pltpu.CompilerParams(collective_id=3, has_side_effects=True),
+    )(q, kv, out, rows, gains)
+
+
 def visible(q_first, k_first, boundary, span):
     q_pos = q_first + lax.broadcasted_iota(jnp.int32, (span, span), 0)
     k_pos = k_first + lax.broadcasted_iota(jnp.int32, (span, span), 1)
@@ -706,29 +863,6 @@
         return ring_scatter([part(k) for k in range(contexts)], ctx_ring, bf16)
 
     shard = gain_attn_in.shape[0]
-    places = (ctx_place, row, core)
-    tiny_rings = (ctx_ring, row_ring, core_ring)
-    ring_order = [inn * sides + out for out, inn in ctx_ring.cells]
-
-    def turn(values, axis, back):
-        count, place = values.shape[axis], places[axis]
-        start = place if back else (count - place) % count
-        twice = jnp.concatenate([values, values], axis=axis)
-        return lax.dynamic_slice_in_dim(twice, start, count, axis)
-
-    def sum_gains(parts):
-        count = parts.shape[0]
-        found = jnp.transpose(parts.reshape(count, contexts * ulysses, shard), (1, 0, 2))
-        found = jnp.pad(found, ((0, 0), (0, -count % 8), (0, -shard % 128)))
-        found = found.reshape(contexts, plan.rows, cores, *found.shape[1:])
-        found = jnp.stack([found[c] for c in ring_order])
-        for axis in range(3):
-            found = turn(found, axis, True)
-        for axis in (2, 1, 0):
-            entries = [lax.index_in_dim(found, k, axis, False) for k in range(found.shape[axis])]
-            found = ring_scatter(entries, tiny_rings[axis], f32)
-        return found[:count, :shard]
-
     packed = jnp.stack([gain_attn_in, gain_attn_out, gain_ffn_in, gain_ffn_out])
     packed = jnp.pad(packed, ((0, 4), (0, -shard % 128)))
     tok_group, col_qkv, col_out, gains, ffn_gate = fetch_weights(
@@ -790,22 +924,20 @@
                     where.append(origin * sides + (side + k) % sides)
         return place_rows(blocks, where, contexts).reshape(width, slice_cols)
 
-    def slice_start(grad):
-        parts = grad.reshape(cores, halves, sides, -1, slice_cols)
-        size = parts.shape[3]
+    def slice_start(lefts, right, earlier):
         others = []
         for m in range(1, cores):
-            at = ((core + m) % cores, 0, 0, 0, 0)
-            piece = lax.dynamic_slice(parts, at, (1, *parts.shape[1:]))[0]
+            piece = dot(after(lefts[m], earlier), right, 0, 0).astype(bf16)
             perm = plan.perm(lambda l, s, r, c, m=m: (l, s, r, (c + m) % cores))
             others.append(move(piece, perm))
+        own = dot(after(lefts[0], earlier), right, 0, 0).astype(bf16)
+        arrays = [x.reshape(halves, sides, -1, slice_cols) for x in (own, *others)]
+        size = arrays[0].shape[2]
 
         def side_part(k):
-            here = (side + k) % sides
+            at = (0, (side + k) % sides, 0, 0)
             shape = (halves, 1, size, slice_cols)
-            found = lax.dynamic_slice(parts, (core, 0, here, 0, 0), (1, *shape))[0].astype(f32)
-            for other in others:
-                found = found + lax.dynamic_slice(other, (0, here, 0, 0), shape).astype(f32)
+            found = sum(lax.dynamic_slice(x, at, shape).astype(f32) for x in arrays)
             return found.reshape(halves * size, slice_cols)
 
         sent = [side_part(k).astype(bf16) for k in range(1, sides)]
@@ -856,7 +988,7 @@
 
     def down_part(n, far):
         rows_in = hidden[n] if far is None else after(hidden[n], far)
-        return dot(rows_in, ffn_down, 1, 1)
+        return dot(rows_in, ffn_down, 1, 1).astype(bf16)
 
     ffn_out, _ = ffn_scatter(down_part)
     block_out = (hidden_in + norm_apply(ffn_out, weight_four)).astype(bf16)
@@ -873,20 +1005,22 @@
         left, right = d_gate[n], d_upper[n]
         if far is not None:
             left, right = after(left, far), after(right, far)
-        return dot(left, ffn_gate, 1, 1) + dot(right, ffn_up, 1, 1)
+        first = lax.optimization_barrier(dot(left, ffn_gate, 1, 1).astype(bf16))
+        return (first.astype(f32) + dot(right, ffn_up, 1, 1)).astype(bf16)
 
     d_mid, landed = ffn_scatter(mid_part)
     grad_hidden = cot_own + norm_grad(hidden_in, weight_three, d_mid)
-    joined = [jnp.concatenate(x, axis=0) for x in (d_ffn, hidden, normed_mid, d_gate, d_upper)]
-
-    def weight_grad(left, right, earlier):
-        left = after(left, earlier)
-        grad = dot(left, right, 0, 0).astype(bf16)
-        return slice_start(grad)
-
-    sum_down = weight_grad(joined[0], joined[1], landed[0])
-    sum_gate = weight_grad(joined[2], joined[3], landed[min(1, len(landed) - 1)])
-    sum_up = weight_grad(joined[2], joined[4], d_mid)
+
+    def by_core(pieces):
+        cols = width // cores
+        cut = lambda x, m: lax.dynamic_slice_in_dim(x, (core + m) % cores * cols, cols, 1)
+        return [jnp.concatenate([cut(x, m) for x in pieces], axis=0) for m in range(cores)]
+
+    d_ffn, normed_mid = by_core(d_ffn), by_core(normed_mid)
+    hidden, d_gate, d_upper = (jnp.concatenate(x, axis=0) for x in (hidden, d_gate, d_upper))
+    sum_down = slice_start(d_ffn, hidden, landed[0])
+    sum_gate = slice_start(normed_mid, d_gate, landed[min(1, len(landed) - 1)])
+    sum_up = slice_start(normed_mid, d_upper, d_mid)
     grad_down = slice_end(after(sum_down, d_mid))
     grad_gate = slice_end(after(sum_gate, d_mid))
 
@@ -909,39 +1043,36 @@
     grad_kv = ctx_scatter([grad_kv])
     grad_up = slice_end(after(sum_up, grad_q))
     grad_q = (rotary(grad_q, cosines, sines, -1.0) * q_scale).astype(bf16)
-    grad_k = rotary(grad_kv[:, :k_cols], cosines, sines, -1.0).astype(bf16)
+    k_cosines, k_sines = after(cosines, grad_kv), after(sines, grad_kv)
+    grad_k = rotary(grad_kv[:, :k_cols], k_cosines, k_sines, -1.0).astype(bf16)
     grad_v = grad_kv[:, k_cols:].astype(bf16)
     grad_kv = jnp.concatenate([grad_k, grad_v], axis=1)
     q_part = dot(normed_in, grad_q, 0, 0).astype(bf16)
     kv_part = dot(normed_in, grad_kv, 0, 0).astype(bf16)
-    d_in_part = dot(grad_q, col_qkv[:, :q_cols], 1, 1) + dot(grad_kv, col_qkv[:, q_cols:], 1, 1)
-    d_in = group_scatter(d_in_part)
+    d_in_part = dot(grad_q, col_qkv[:, :q_cols], 1, 1)
+    d_in_part = (d_in_part + dot(grad_kv, col_qkv[:, q_cols:], 1, 1)).astype(bf16)
+
+    gain_parts = jnp.stack(
+        [
+            gain_part(attn_out, after(grad_hidden, grad_q)),
+            gain_part(hidden_in, after(d_mid, grad_q)),
+            gain_part(ffn_out, after(cot_own, grad_q)),
+        ]
+    ).reshape(3, contexts * ulysses, shard)
+    gain_parts = jnp.pad(jnp.transpose(gain_parts, (1, 0, 2)), ((0, 0), (0, 5), (0, -shard % 128)))
+    grad_query, grad_key, grad_value, grad_outproj, d_in, gain_grads = sum_grads(
+        plan,
+        q_part.reshape(contexts * ulysses, shard, -1),
+        kv_part.reshape(contexts * ulysses, shard, -1),
+        out_part.reshape(contexts * ulysses, shard, -1),
+        d_in_part.reshape(ulysses, rows, width),
+        gain_parts,
+        w_query.shape[1],
+        w_key.shape[1],
+    )
+    grad_outproj = grad_outproj.reshape(w_out.shape)
+    gain_grads = gain_grads[:, :shard]
     grad_tokens = grad_hidden + norm_grad(tok_own, weight_one, d_in)
-    first_grad = ctx_scatter([q_part, out_part])
-    second_grad = ctx_scatter([kv_part])
-    grad_outproj = first_grad[:, q_cols:]
-    mixed_grad = jnp.concatenate([first_grad[:, :q_cols], second_grad], axis=1).astype(bf16)
-    mixed_grad = lax.all_to_all(
-        mixed_grad.reshape(ulysses, -1, mixed_grad.shape[1]),
-        "uly",
-        split_axis=0,
-        concat_axis=0,
-        tiled=True,
-    )
-    mixed_grad = jnp.transpose(mixed_grad, (1, 0, 2)).astype(f32)
-    grad_query = mixed_grad[:, :, :q_cols].reshape(w_query.shape)
-    grad_key = mixed_grad[:, :, q_cols : q_cols + k_cols].reshape(w_key.shape)
-    grad_value = mixed_grad[:, :, q_cols + k_cols :].reshape(w_value.shape)
-
-    gain_grads = sum_gains(
-        jnp.stack(
-            [
-                gain_part(attn_out, after(grad_hidden, grad_q)),
-                gain_part(hidden_in, after(d_mid, grad_q)),
-                gain_part(ffn_out, after(cot_own, grad_q)),
-            ]
-        )
-    )
     products = [
         jnp.sum(w.astype(f32) * g, axis=1)
         for w, g in ((w_query, grad_query), (w_key, grad_key), (w_value, grad_value))

time: 835 us -> 813 us (0.974)
  the two profiles are of different devices: /device:TPU:8 before, /device:TPU:3 now
where the time goes in v2:
time: 813 us; the launch traced here: 803 us
  Pallas kernels  312 us (38%)
  waiting for transfers between devices  191 us (23%)
  starting transfers between devices  101 us (12%)
  matrix products  99.3 us (12%)
  other arithmetic  66.2 us (8%)
  local copies, waits for them, and re-layouts  24.7 us (3%)
    ppermute x62, waiting for transfers between devices, move(): return lax.ppermute(values, AXES, perm)  191 us
    pallas_call x1, Pallas kernels, fetch_weights(): pl.pallas_call(functools.partial(weights_kernel, plan), out_shape=results...  109 us
    ppermute x62, starting transfers between devices, move(): return lax.ppermute(values, AXES, perm)  101 us
    pallas_call x1, Pallas kernels, sum_grads(): pl.pallas_call(functools.partial(grads_kernel, plan), out_shape=results,...  101 us
    dot_general x26, matrix products, dot(): lax.dot_general(left, right, (((left_dim,), (right_dim,)), ((), ())), pre...  99.3 us
    pallas_call x1, Pallas kernels, fetch_keys(): pl.pallas_call(functools.partial(keys_kernel, plan), out_shape=[jax.Shape...  76.8 us
  transfers between devices with their start and end apart: 62, of which 29 were waited for; matrix products, arithmetic and copies ran while one was open for 17% of the time, Pallas kernels for 14%

profile of v2, /device:TPU:3, one launch (start us, length us, event | category | flops | bytes accessed | tf_op | source)
XLA Modules:
  0.0 803.0 jit_solution(356252686824558030)
XLA Ops:
  2.0 109.2 %shard_map.255 = (bf16[4,128,2304]{2,1,0:T(8,128)(2,1)}, bf16[32,72,1024]{2,1,0:T(8,128)(2,1)}, bf16[8,288,512]{2,1,0:T(8,128)(2,1)}, f32[32,8,128]{2,1,0:T(8,128)}, bf16[8,288,1152]{2,1,0:T(8,128)(2,1)}) custom-call(bf16[128,2304]{1,0:T(8,128)(2,1)} %refs_0_.1, bf16[72,2048]{1,0:T(8,128)(2,1)} %refs_1_.1, bf16[72,1024]{1,0:T(8,128)(2,1)} %refs_2_.1, ...), custom_call_target="tpu_custom_call" | custom-call | tf_op jit(solution)/shard_map/pallas_call | solution.py:404
  119.0 2.6 fusion.103
  124.4 76.8 %shard_map.256 = (bf16[8,512,512]{2,1,0:T(8,128)(2,1)}, bf16[8,288,1152]{2,1,0:T(8,128)(2,1)}) custom-call(bf16[512,512]{1,0:T(8,128)(2,1)} %pad_maximum_fusion.19.kv_in, bf16[288,2304]{1,0:T(8,128)(2,1)} %up_in.1), custom_call_target="tpu_custom_call" | custom-call | tf_op jit(solution)/shard_map/pallas_call | solution.py:438
  202.0 10.5 %shard_map.257 = (bf16[512,512]{1,0:T(8,128)(2,1)}, f32[512,256]{1,0:T(8,128)}) custom-call(s32[2]{0:T(128)} %copy-done.67, s32[16]{0:T(128)} %broadcast_multiply_fusion.4.kp, s32[1]{0:T(128)} %bitcast.bd, bf16[512,512]{1,0:T(8,128)(2,1)} %fusion.31.q_ref, bf16[4096,512]{1,0:T(8,128)(2,1)} %bitcast.233), custom_call_target="tpu_custom_call" | custom-call | flops 2147483648 | bytes 8388608 | tf_op jit(solution)/shard_map/pallas_call | solution.py:711
  222.0 4.4 collective-permute-start.12
  228.4 10.2 %collective-permute-done.11 = bf16[288,1152]{1,0:T(8,128)(2,1)S(1)} collective-permute-done((bf16[288,1152]{1,0:T(8,128)(2,1)}, bf16[288,1152]{1,0:T(8,128)(2,1)S(1)}, u32[]{:S(2)}, u32[]{:S(2)}) %collective-permute-start.11) | collective-permute-done | bytes 663584 | tf_op jit(solution)/shard_map/ppermute | solution.py:125
  238.6 9.6 %collective-permute-done.12 = bf16[288,1152]{1,0:T(8,128)(2,1)S(1)} collective-permute-done((bf16[288,1152]{1,0:T(8,128)(2,1)S(1)}, bf16[288,1152]{1,0:T(8,128)(2,1)S(1)}, u32[]{:S(2)}, u32[]{:S(2)}) %collective-permute-start.12) | collective-permute-done | bytes 663584 | tf_op jit(solution)/shard_map/ppermute | solution.py:125
  254.5 7.7 collective-permute-start.3
  262.8 7.2 collective-permute-done.3
  270.0 6.6 collective-permute-done.4
  281.3 10.4 %collective-permute-done.5 = bf16[128,2304]{1,0:T(8,128)(2,1)S(1)} collective-permute-done((bf16[128,2304]{1,0:T(8,128)(2,1)S(1)}, bf16[128,2304]{1,0:T(8,128)(2,1)S(1)}, u32[]{:S(2)}, u32[]{:S(2)}) %collective-permute-start.5) | collective-permute-done | bytes 589856 | tf_op jit(solution)/shard_map/ppermute | solution.py:125
  293.5 4.0 fusion.105
  297.5 9.3 %collective-permute-done.7 = bf16[128,2304]{1,0:T(8,128)(2,1)S(1)} collective-permute-done((bf16[128,2304]{1,0:T(8,128)(2,1)S(1)}, bf16[128,2304]{1,0:T(8,128)(2,1)S(1)}, u32[]{:S(2)}, u32[]{:S(2)}) %collective-permute-start.7) | collective-permute-done | bytes 589856 | tf_op jit(solution)/shard_map/ppermute | solution.py:125
  308.6 4.9 collective-permute-done.9
  316.1 3.8 multiply_convert_fusion.4
  320.8 2.5 convolution_convert_fusion.12
  325.1 5.8 multiply_convert_fusion.2
  332.7 4.2 convolution_convert_fusion.7
  337.0 5.4 collective-permute-done.18
  345.2 10.0 %collective-permute-done.19 = bf16[128,2304]{1,0:T(8,128)(2,1)S(1)} collective-permute-done((bf16[128,2304]{1,0:T(8,128)(2,1)S(1)}, bf16[128,2304]{1,0:T(8,128)(2,1)S(1)}, u32[]{:S(2)}, u32[]{:S(2)}) %collective-permute-start.19) | collective-permute-done | bytes 589856 | tf_op jit(solution)/shard_map/ppermute | solution.py:125
  371.3 2.7 constant_dynamic-update-slice_fusion.13
  376.0 6.7 collective-permute-done.23
  384.6 12.3 %collective-permute-done.25 = bf16[128,2304]{1,0:T(8,128)(2,1)S(1)} collective-permute-done((bf16[128,2304]{1,0:T(8,128)(2,1)S(1)}, bf16[128,2304]{1,0:T(8,128)(2,1)S(1)}, u32[]{:S(2)}, u32[]{:S(2)}) %collective-permute-start.25) | collective-permute-done | bytes 589856 | tf_op jit(solution)/shard_map/ppermute | solution.py:125
  399.0 6.2 multiply_convert_fusion.1
  405.4 7.3 collective-permute-done.27
  414.8 5.6 collective-permute-done.29
  422.3 3.1 fusion.23
  425.6 2.5 convolution_convert_fusion.11
  428.1 5.1 fusion.3
  433.2 4.4 convolution_convert_fusion.6
  439.3 7.0 add_convert_fusion
  448.7 3.3 convolution_convert_fusion
  452.0 13.4 %collective-permute-start.58 = (bf16[1152,1152]{1,0:T(8,128)(2,1)S(1)}, bf16[1152,1152]{1,0:T(8,128)(2,1)S(1)}, u32[]{:S(2)}, u32[]{:S(2)}) collective-permute-start(bf16[1152,1152]{1,0:T(8,128)(2,1)S(1)} %convolution_convert_fusion), channel_id=1, source_target_pairs={{0,1},{1,0},{2,3},{3,2},{4,5},{5,4},{6,7},{7,6},{8,9},{9,8},{10,11... | collective-permute-start | bytes 7962632 | tf_op jit(solution)/shard_map/ppermute | solution.py:125
  465.4 3.3 convolution_convert_fusion.1
  470.5 4.8 convolution_convert_fusion.4
  475.3 3.2 collective-permute-start.50
  478.5 2.8 collective-permute-done.35
  484.9 4.8 convolution_convert_fusion.5
  489.7 5.1 collective-permute-done.37
  499.3 3.8 collective-permute-start.39
  503.2 4.8 convolution_convert_fusion.2
  509.2 4.7 convolution_convert_fusion.3
  513.9 4.1 collective-permute-done.40
  521.6 2.6 convert_multiply_fusion.3
  525.5 15.2 %shard_map.258 = (f32[512,512]{1,0:T(8,128)}, bf16[4096,512]{1,0:T(8,128)(2,1)}) custom-call(s32[2]{0:T(128)} %copy-done.67, s32[16]{0:T(128)} %broadcast_multiply_fusion.4.kp, s32[1]{0:T(128)} %bitcast.bd, bf16[512,512]{1,0:T(8,128)(2,1)} %fusion.31.q_ref, bf16[512,512]{1,0:T(8,128)(2,1)} %get-tuple-element.299.g_ref, ...), custom_call_target="tpu_custom_call" | custom-call | flops 5368709120 | bytes 8388608 | tf_op jit(solution)/shard_map/pallas_call | solution.py:773
  540.7 3.2 multiply_cosine_fusion
  545.2 9.4 %collective-permute-start.42 = (bf16[256,512]{1,0:T(8,128)(2,1)S(1)}, bf16[256,512]{1,0:T(8,128)(2,1)S(1)}, u32[]{:S(2)}, u32[]{:S(2)}) collective-permute-start(bf16[256,512]{1,0:T(8,128)(2,1)S(1)} %get-tuple-element.202), channel_id=1, source_target_pairs={{0,8},{1,9},{2,10},{3,11},{4,0},{5,1},{6,2},{7,3},{8,16},{9,17},{1... | collective-permute-start | bytes 786440 | tf_op jit(solution)/shard_map/ppermute | solution.py:125
  554.7 2.9 convolution_convert_fusion.8
  557.7 3.1 multiply_reduce_fusion.1
  560.8 3.6 fusion.15
  564.4 2.9 convolution_convert_fusion.10
  572.2 3.2 add_convert_fusion.3
  577.0 4.7 collective-permute-done.45
  587.7 2.6 collective-permute-start.60
  590.4 30.9 %collective-permute-done.46 = bf16[512,512]{1,0:T(8,128)(2,1)S(1)} collective-permute-done((bf16[512,512]{1,0:T(8,128)(2,1)S(1)}, bf16[512,512]{1,0:T(8,128)(2,1)S(1)}, u32[]{:S(2)}, u32[]{:S(2)}) %collective-permute-start.46) | collective-permute-done | bytes 524320 | tf_op jit(solution)/shard_map/ppermute | solution.py:125
  625.9 4.4 add_convert_fusion.2
  633.2 3.0 collective-permute-start.52
  636.2 6.1 collective-permute-done.61
  647.8 2.8 convolution_convert_fusion.9
  650.7 2.9 fusion.2
  653.6 100.7 %shard_map.259 = (f32[72,2048]{1,0:T(8,128)}, f32[72,1024]{1,0:T(8,128)}, f32[72,1024]{1,0:T(8,128)}, f32[4,72,512]{2,1,0:T(8,128)}, f32[128,2304]{1,0:T(8,128)}, /*index=5*/f32[8,128]{1,0:T(8,128)}) custom-call(bf16[32,72,512]{2,1,0:T(8,128)(2,1)} %bitcast.208, bf16[32,72,512]{2,1,0:T(8,128)(2,1)} %bitcast.209, bf16[32,72,512]{2,1,0:T(8,128)(2,1)} %bitcast.207, ...), custom_call_target="tpu_custom_call" | custom-call | tf_op jit(solution)/shard_map/pallas_call | solution.py:589
  765.7 5.0 collective-permute-start.57
  773.9 7.8 collective-permute-done.56
  781.7 16.1 %collective-permute-done.57 = bf16[288,1152]{1,0:T(8,128)(2,1)S(1)} collective-permute-done((bf16[288,1152]{1,0:T(8,128)(2,1)S(1)}, bf16[288,1152]{1,0:T(8,128)(2,1)S(1)}, u32[]{:S(2)}, u32[]{:S(2)}) %collective-permute-start.57) | collective-permute-done | bytes 663584 | tf_op jit(solution)/shard_map/ppermute | solution.py:125
  (442 shorter events, 136.0 us)
Async XLA Ops:
  0.7 121.5 %copy-start.65 = (f32[128]{0:T(128)}, f32[128]{0:T(128)S(1)}, u32[]{:S(2)}) copy-start(f32[128]{0:T(128)S(1)} %multiply_power_fusion) | copy-start | bytes 1540
  2.0 113.9 %copy-start.69 = (s32[16]{0:T(128)S(1)}, s32[16]{0:T(128)}, u32[]{:S(2)}) copy-start(s32[16]{0:T(128)} %param.20) | copy-start | bytes 196
  218.2 8.2 %collective-permute-start.1 = (bf16[128,2304]{1,0:T(8,128)(2,1)}, bf16[128,2304]{1,0:T(8,128)(2,1)}, u32[]{:S(2)}, u32[]{:S(2)}) collective-permute-start(bf16[128,2304]{1,0:T(8,128)(2,1)} %get-tuple-element.196), channel_id=1, source_target_pairs={{0,1},{1,0},{2,3},{3,2},{4,5},{5,4},{6,7},{7,6},{8,9},{9,8},{10,11... | collective-permute-start | bytes 1769480 | tf_op jit(solution)/shard_map/ppermute | solution.py:125
  219.1 31.7 %collective-permute-start = (bf16[128,2304]{1,0:T(8,128)(2,1)}, bf16[128,2304]{1,0:T(8,128)(2,1)}, u32[]{:S(2)}, u32[]{:S(2)}) collective-permute-start(bf16[128,2304]{1,0:T(8,128)(2,1)} %get-tuple-element.195), channel_id=1, source_target_pairs={{0,1},{1,0},{2,3},{3,2},{4,5},{5,4},{6,7},{7,6},{8,9},{9,8},{10,11... | collective-permute-start | bytes 1769480 | tf_op jit(solution)/shard_map/ppermute | solution.py:125
  220.1 18.6 %collective-permute-start.11 = (bf16[288,1152]{1,0:T(8,128)(2,1)}, bf16[288,1152]{1,0:T(8,128)(2,1)S(1)}, u32[]{:S(2)}, u32[]{:S(2)}) collective-permute-start(bf16[288,1152]{1,0:T(8,128)(2,1)} %get-tuple-element.260), channel_id=1, source_target_pairs={{0,0},{1,16},{2,2},{3,18},{4,4},{5,20},{6,6},{7,22},{8,8},{9,24},{... | collective-permute-start | bytes 1990664 | tf_op jit(solution)/shard_map/ppermute | solution.py:125
  222.0 26.3 %collective-permute-start.12 = (bf16[288,1152]{1,0:T(8,128)(2,1)S(1)}, bf16[288,1152]{1,0:T(8,128)(2,1)S(1)}, u32[]{:S(2)}, u32[]{:S(2)}) collective-permute-start(bf16[288,1152]{1,0:T(8,128)(2,1)S(1)} %get-tuple-element.259), channel_id=1, source_target_pairs={{0,8},{1,24},{2,10},{3,26},{4,12},{5,28},{6,14},{7,30},{8,0},{9,16... | collective-permute-start | bytes 1990664 | tf_op jit(solution)/shard_map/ppermute | solution.py:125
  228.0 22.8 %collective-permute-start.2 = (bf16[128,2304]{1,0:T(8,128)(2,1)S(1)}, bf16[128,2304]{1,0:T(8,128)(2,1)}, u32[]{:S(2)}, u32[]{:S(2)}) collective-permute-start(bf16[128,2304]{1,0:T(8,128)(2,1)S(1)} %fusion.29), channel_id=1, source_target_pairs={{0,2},{1,3},{2,0},{3,1},{4,6},{5,7},{6,4},{7,5},{8,10},{9,11},{10,... | collective-permute-start | bytes 1769480 | tf_op jit(solution)/shard_map/ppermute | solution.py:125
  248.4 30.1 %collective-permute-start.13 = (bf16[576,1152]{1,0:T(8,128)(2,1)S(1)}, bf16[576,1152]{1,0:T(8,128)(2,1)S(1)}, u32[]{:S(2)}, u32[]{:S(2)}) collective-permute-start(bf16[576,1152]{1,0:T(8,128)(2,1)S(1)} %pad_maximum_fusion.14), channel_id=1, source_target_pairs={{0,4},{1,5},{2,6},{3,7},{4,0},{5,1},{6,2},{7,3},{8,12},{9,13},{10,... | collective-permute-start | bytes 3981320 | tf_op jit(solution)/shard_map/ppermute | solution.py:125
  254.5 15.5 %collective-permute-start.3 = (bf16[128,2304]{1,0:T(8,128)(2,1)S(1)}, bf16[128,2304]{1,0:T(8,128)(2,1)S(1)}, u32[]{:S(2)}, u32[]{:S(2)}) collective-permute-start(bf16[128,2304]{1,0:T(8,128)(2,1)S(1)} %get-tuple-element.182), channel_id=1, source_target_pairs={{0,8},{1,9},{2,0},{3,1},{4,12},{5,13},{6,4},{7,5},{8,16},{9,17},{1... | collective-permute-start | bytes 1769480 | tf_op jit(solution)/shard_map/ppermute | solution.py:125
  262.2 14.3 %collective-permute-start.4 = (bf16[128,2304]{1,0:T(8,128)(2,1)S(1)}, bf16[128,2304]{1,0:T(8,128)(2,1)S(1)}, u32[]{:S(2)}, u32[]{:S(2)}) collective-permute-start(bf16[128,2304]{1,0:T(8,128)(2,1)S(1)} %get-tuple-element.182), channel_id=1, source_target_pairs={{0,2},{1,3},{2,10},{3,11},{4,6},{5,7},{6,14},{7,15},{8,0},{9,1},{1... | collective-permute-start | bytes 1769480 | tf_op jit(solution)/shard_map/ppermute | solution.py:125
  276.5 15.2 %collective-permute-start.5 = (bf16[128,2304]{1,0:T(8,128)(2,1)S(1)}, bf16[128,2304]{1,0:T(8,128)(2,1)S(1)}, u32[]{:S(2)}, u32[]{:S(2)}) collective-permute-start(bf16[128,2304]{1,0:T(8,128)(2,1)S(1)} %collective-permute-done.3), channel_id=1, source_target_pairs={{0,8},{1,9},{2,0},{3,1},{4,12},{5,13},{6,4},{7,5},{8,16},{9,17},{1... | collective-permute-start | bytes 1769480 | tf_op jit(solution)/shard_map/ppermute | solution.py:125
  277.0 14.7 %collective-permute-start.6 = (bf16[128,2304]{1,0:T(8,128)(2,1)S(1)}, bf16[128,2304]{1,0:T(8,128)(2,1)S(1)}, u32[]{:S(2)}, u32[]{:S(2)}) collective-permute-start(bf16[128,2304]{1,0:T(8,128)(2,1)S(1)} %collective-permute-done.4), channel_id=1, source_target_pairs={{0,2},{1,3},{2,10},{3,11},{4,6},{5,7},{6,14},{7,15},{8,0},{9,1},{1... | collective-permute-start | bytes 1769480 | tf_op jit(solution)/shard_map/ppermute | solution.py:125
  278.7 41.2 %collective-permute-start.14 = (bf16[1152,1152]{1,0:T(8,128)(2,1)S(1)}, bf16[1152,1152]{1,0:T(8,128)(2,1)S(1)}, u32[]{:S(2)}, u32[]{:S(2)}) collective-permute-start(bf16[1152,1152]{1,0:T(8,128)(2,1)S(1)} %pad_maximum_fusion), channel_id=1, source_target_pairs={{0,1},{1,0},{2,3},{3,2},{4,5},{5,4},{6,7},{7,6},{8,9},{9,8},{10,11... | collective-permute-start | bytes 7962632 | tf_op jit(solution)/shard_map/ppermute | solution.py:125
  291.7 15.2 %collective-permute-start.8 = (bf16[128,2304]{1,0:T(8,128)(2,1)S(1)}, bf16[128,2304]{1,0:T(8,128)(2,1)S(1)}, u32[]{:S(2)}, u32[]{:S(2)}) collective-permute-start(bf16[128,2304]{1,0:T(8,128)(2,1)S(1)} %collective-permute-done.6), channel_id=1, source_target_pairs={{0,2},{1,3},{2,10},{3,11},{4,6},{5,7},{6,14},{7,15},{8,0},{9,1},{1... | collective-permute-start | bytes 1769480 | tf_op jit(solution)/shard_map/ppermute | solution.py:125
  292.9 14.0 %collective-permute-start.7 = (bf16[128,2304]{1,0:T(8,128)(2,1)S(1)}, bf16[128,2304]{1,0:T(8,128)(2,1)S(1)}, u32[]{:S(2)}, u32[]{:S(2)}) collective-permute-start(bf16[128,2304]{1,0:T(8,128)(2,1)S(1)} %collective-permute-done.5), channel_id=1, source_target_pairs={{0,8},{1,9},{2,0},{3,1},{4,12},{5,13},{6,4},{7,5},{8,16},{9,17},{1... | collective-permute-start | bytes 1769480 | tf_op jit(solution)/shard_map/ppermute | solution.py:125
  306.9 6.6 collective-permute-start.9
  307.2 6.4 collective-permute-start.10
  323.4 7.5 collective-permute-start.15
  323.5 7.4 collective-permute-start.16
  331.1 11.3 %collective-permute-start.18 = (bf16[128,2304]{1,0:T(8,128)(2,1)S(1)}, bf16[128,2304]{1,0:T(8,128)(2,1)S(1)}, u32[]{:S(2)}, u32[]{:S(2)}) collective-permute-start(bf16[128,2304]{1,0:T(8,128)(2,1)S(1)} %pad_maximum_fusion.16), channel_id=1, source_target_pairs={{0,2},{1,3},{2,10},{3,11},{4,6},{5,7},{6,14},{7,15},{8,0},{9,1},{1... | collective-permute-start | bytes 1769480 | tf_op jit(solution)/shard_map/ppermute | solution.py:125
  332.4 11.0 %collective-permute-start.17 = (bf16[128,2304]{1,0:T(8,128)(2,1)S(1)}, bf16[128,2304]{1,0:T(8,128)(2,1)S(1)}, u32[]{:S(2)}, u32[]{:S(2)}) collective-permute-start(bf16[128,2304]{1,0:T(8,128)(2,1)S(1)} %pad_maximum_fusion.15), channel_id=1, source_target_pairs={{0,8},{1,9},{2,0},{3,1},{4,12},{5,13},{6,4},{7,5},{8,16},{9,17},{1... | collective-permute-start | bytes 1769480 | tf_op jit(solution)/shard_map/ppermute | solution.py:125
  343.7 11.5 %collective-permute-start.19 = (bf16[128,2304]{1,0:T(8,128)(2,1)S(1)}, bf16[128,2304]{1,0:T(8,128)(2,1)S(1)}, u32[]{:S(2)}, u32[]{:S(2)}) collective-permute-start(bf16[128,2304]{1,0:T(8,128)(2,1)S(1)} %get-tuple-element.222), channel_id=1, source_target_pairs={{0,8},{1,9},{2,0},{3,1},{4,12},{5,13},{6,4},{7,5},{8,16},{9,17},{1... | collective-permute-start | bytes 1769480 | tf_op jit(solution)/shard_map/ppermute | solution.py:125
  344.0 11.2 %collective-permute-start.20 = (bf16[128,2304]{1,0:T(8,128)(2,1)S(1)}, bf16[128,2304]{1,0:T(8,128)(2,1)S(1)}, u32[]{:S(2)}, u32[]{:S(2)}) collective-permute-start(bf16[128,2304]{1,0:T(8,128)(2,1)S(1)} %get-tuple-element.221), channel_id=1, source_target_pairs={{0,2},{1,3},{2,10},{3,11},{4,6},{5,7},{6,14},{7,15},{8,0},{9,1},{1... | collective-permute-start | bytes 1769480 | tf_op jit(solution)/shard_map/ppermute | solution.py:125
  356.5 12.7 %collective-permute-start.21 = (bf16[128,2304]{1,0:T(8,128)(2,1)}, bf16[128,2304]{1,0:T(8,128)(2,1)S(1)}, u32[]{:S(2)}, u32[]{:S(2)}) collective-permute-start(bf16[128,2304]{1,0:T(8,128)(2,1)} %get-tuple-element.220), channel_id=1, source_target_pairs={{0,8},{1,9},{2,0},{3,1},{4,12},{5,13},{6,4},{7,5},{8,16},{9,17},{1... | collective-permute-start | bytes 1769480 | tf_op jit(solution)/shard_map/ppermute | solution.py:125
  356.8 12.5 %collective-permute-start.22 = (bf16[128,2304]{1,0:T(8,128)(2,1)}, bf16[128,2304]{1,0:T(8,128)(2,1)S(1)}, u32[]{:S(2)}, u32[]{:S(2)}) collective-permute-start(bf16[128,2304]{1,0:T(8,128)(2,1)} %get-tuple-element.219), channel_id=1, source_target_pairs={{0,2},{1,3},{2,10},{3,11},{4,6},{5,7},{6,14},{7,15},{8,0},{9,1},{1... | collective-permute-start | bytes 1769480 | tf_op jit(solution)/shard_map/ppermute | solution.py:125
  374.0 8.8 %collective-permute-start.23 = (bf16[128,2304]{1,0:T(8,128)(2,1)S(1)}, bf16[128,2304]{1,0:T(8,128)(2,1)S(1)}, u32[]{:S(2)}, u32[]{:S(2)}) collective-permute-start(bf16[128,2304]{1,0:T(8,128)(2,1)S(1)} %get-tuple-element.180), channel_id=1, source_target_pairs={{0,8},{1,9},{2,0},{3,1},{4,12},{5,13},{6,4},{7,5},{8,16},{9,17},{1... | collective-permute-start | bytes 1769480 | tf_op jit(solution)/shard_map/ppermute | solution.py:125
  374.3 8.7 %collective-permute-start.24 = (bf16[128,2304]{1,0:T(8,128)(2,1)S(1)}, bf16[128,2304]{1,0:T(8,128)(2,1)S(1)}, u32[]{:S(2)}, u32[]{:S(2)}) collective-permute-start(bf16[128,2304]{1,0:T(8,128)(2,1)S(1)} %get-tuple-element.180), channel_id=1, source_target_pairs={{0,2},{1,3},{2,10},{3,11},{4,6},{5,7},{6,14},{7,15},{8,0},{9,1},{1... | collective-permute-start | bytes 1769480 | tf_op jit(solution)/shard_map/ppermute | solution.py:125
  383.0 13.8 %collective-permute-start.25 = (bf16[128,2304]{1,0:T(8,128)(2,1)S(1)}, bf16[128,2304]{1,0:T(8,128)(2,1)S(1)}, u32[]{:S(2)}, u32[]{:S(2)}) collective-permute-start(bf16[128,2304]{1,0:T(8,128)(2,1)S(1)} %collective-permute-done.23), channel_id=1, source_target_pairs={{0,8},{1,9},{2,0},{3,1},{4,12},{5,13},{6,4},{7,5},{8,16},{9,17},{1... | collective-permute-start | bytes 1769480 | tf_op jit(solution)/shard_map/ppermute | solution.py:125
  383.2 14.2 %collective-permute-start.26 = (bf16[128,2304]{1,0:T(8,128)(2,1)S(1)}, bf16[128,2304]{1,0:T(8,128)(2,1)S(1)}, u32[]{:S(2)}, u32[]{:S(2)}) collective-permute-start(bf16[128,2304]{1,0:T(8,128)(2,1)S(1)} %collective-permute-done.24), channel_id=1, source_target_pairs={{0,2},{1,3},{2,10},{3,11},{4,6},{5,7},{6,14},{7,15},{8,0},{9,1},{1... | collective-permute-start | bytes 1769480 | tf_op jit(solution)/shard_map/ppermute | solution.py:125
  397.4 15.4 %collective-permute-start.28 = (bf16[128,2304]{1,0:T(8,128)(2,1)S(1)}, bf16[128,2304]{1,0:T(8,128)(2,1)S(1)}, u32[]{:S(2)}, u32[]{:S(2)}) collective-permute-start(bf16[128,2304]{1,0:T(8,128)(2,1)S(1)} %collective-permute-done.26), channel_id=1, source_target_pairs={{0,2},{1,3},{2,10},{3,11},{4,6},{5,7},{6,14},{7,15},{8,0},{9,1},{1... | collective-permute-start | bytes 1769480 | tf_op jit(solution)/shard_map/ppermute | solution.py:125
  398.7 14.0 %collective-permute-start.27 = (bf16[128,2304]{1,0:T(8,128)(2,1)S(1)}, bf16[128,2304]{1,0:T(8,128)(2,1)S(1)}, u32[]{:S(2)}, u32[]{:S(2)}) collective-permute-start(bf16[128,2304]{1,0:T(8,128)(2,1)S(1)} %collective-permute-done.25), channel_id=1, source_target_pairs={{0,8},{1,9},{2,0},{3,1},{4,12},{5,13},{6,4},{7,5},{8,16},{9,17},{1... | collective-permute-start | bytes 1769480 | tf_op jit(solution)/shard_map/ppermute | solution.py:125
  412.8 7.6 collective-permute-start.29
  413.3 8.9 %collective-permute-start.30 = (bf16[64,2304]{1,0:T(8,128)(2,1)S(1)}, bf16[64,2304]{1,0:T(8,128)(2,1)S(1)}, u32[]{:S(2)}, u32[]{:S(2)}) collective-permute-start(bf16[64,2304]{1,0:T(8,128)(2,1)S(1)} %slice.297), channel_id=1, source_target_pairs={{0,2},{1,3},{2,10},{3,11},{4,6},{5,7},{6,14},{7,15},{8,0},{9,1},{1... | collective-permute-start | bytes 884744 | tf_op jit(solution)/shard_map/ppermute | solution.py:125
  437.6 9.0 %collective-permute-start.31 = (bf16[64,2304]{1,0:T(8,128)(2,1)S(1)}, bf16[64,2304]{1,0:T(8,128)(2,1)S(1)}, u32[]{:S(2)}, u32[]{:S(2)}) collective-permute-start(bf16[64,2304]{1,0:T(8,128)(2,1)S(1)} %get-tuple-element.236), channel_id=1, source_target_pairs={{0,8},{1,9},{2,0},{3,1},{4,12},{5,13},{6,4},{7,5},{8,16},{9,17},{1... | collective-permute-start | bytes 884744 | tf_op jit(solution)/shard_map/ppermute | solution.py:125
  438.0 8.7 %collective-permute-start.32 = (bf16[64,2304]{1,0:T(8,128)(2,1)S(1)}, bf16[64,2304]{1,0:T(8,128)(2,1)S(1)}, u32[]{:S(2)}, u32[]{:S(2)}) collective-permute-start(bf16[64,2304]{1,0:T(8,128)(2,1)S(1)} %get-tuple-element.235), channel_id=1, source_target_pairs={{0,2},{1,3},{2,10},{3,11},{4,6},{5,7},{6,14},{7,15},{8,0},{9,1},{1... | collective-permute-start | bytes 884744 | tf_op jit(solution)/shard_map/ppermute | solution.py:125
  446.9 21.8 %collective-permute-start.34 = (bf16[128,2304]{1,0:T(8,128)(2,1)S(1)}, bf16[128,2304]{1,0:T(8,128)(2,1)S(1)}, u32[]{:S(2)}, u32[]{:S(2)}) collective-permute-start(bf16[128,2304]{1,0:T(8,128)(2,1)S(1)} %pad_maximum_fusion.18), channel_id=1, source_target_pairs={{0,2},{1,3},{2,10},{3,11},{4,6},{5,7},{6,14},{7,15},{8,0},{9,1},{1... | collective-permute-start | bytes 1769480 | tf_op jit(solution)/shard_map/ppermute | solution.py:125
  448.4 20.3 %collective-permute-start.33 = (bf16[128,2304]{1,0:T(8,128)(2,1)S(1)}, bf16[128,2304]{1,0:T(8,128)(2,1)S(1)}, u32[]{:S(2)}, u32[]{:S(2)}) collective-permute-start(bf16[128,2304]{1,0:T(8,128)(2,1)S(1)} %pad_maximum_fusion.17), channel_id=1, source_target_pairs={{0,8},{1,9},{2,0},{3,1},{4,12},{5,13},{6,4},{7,5},{8,16},{9,17},{1... | collective-permute-start | bytes 1769480 | tf_op jit(solution)/shard_map/ppermute | solution.py:125
  452.0 67.0 %collective-permute-start.58 = (bf16[1152,1152]{1,0:T(8,128)(2,1)S(1)}, bf16[1152,1152]{1,0:T(8,128)(2,1)S(1)}, u32[]{:S(2)}, u32[]{:S(2)}) collective-permute-start(bf16[1152,1152]{1,0:T(8,128)(2,1)S(1)} %convolution_convert_fusion), channel_id=1, source_target_pairs={{0,1},{1,0},{2,3},{3,2},{4,5},{5,4},{6,7},{7,6},{8,9},{9,8},{10,11... | collective-permute-start | bytes 7962632 | tf_op jit(solution)/shard_map/ppermute | solution.py:125
  469.0 12.3 %collective-permute-start.35 = (bf16[128,2304]{1,0:T(8,128)(2,1)S(1)}, bf16[128,2304]{1,0:T(8,128)(2,1)S(1)}, u32[]{:S(2)}, u32[]{:S(2)}) collective-permute-start(bf16[128,2304]{1,0:T(8,128)(2,1)S(1)} %get-tuple-element.218), channel_id=1, source_target_pairs={{0,8},{1,9},{2,0},{3,1},{4,12},{5,13},{6,4},{7,5},{8,16},{9,17},{1... | collective-permute-start | bytes 1769480 | tf_op jit(solution)/shard_map/ppermute | solution.py:125
  469.8 12.4 %collective-permute-start.36 = (bf16[128,2304]{1,0:T(8,128)(2,1)S(1)}, bf16[128,2304]{1,0:T(8,128)(2,1)S(1)}, u32[]{:S(2)}, u32[]{:S(2)}) collective-permute-start(bf16[128,2304]{1,0:T(8,128)(2,1)S(1)} %get-tuple-element.217), channel_id=1, source_target_pairs={{0,2},{1,3},{2,10},{3,11},{4,6},{5,7},{6,14},{7,15},{8,0},{9,1},{1... | collective-permute-start | bytes 1769480 | tf_op jit(solution)/shard_map/ppermute | solution.py:125
  475.3 96.9 %collective-permute-start.50 = (bf16[1152,1152]{1,0:T(8,128)(2,1)}, bf16[1152,1152]{1,0:T(8,128)(2,1)}, u32[]{:S(2)}, u32[]{:S(2)}) collective-permute-start(bf16[1152,1152]{1,0:T(8,128)(2,1)} %convolution_convert_fusion.4), channel_id=1, source_target_pairs={{0,1},{1,0},{2,3},{3,2},{4,5},{5,4},{6,7},{7,6},{8,9},{9,8},{10,11... | collective-permute-start | bytes 7962632 | tf_op jit(solution)/shard_map/ppermute | solution.py:125
  482.5 12.3 %collective-permute-start.37 = (bf16[128,2304]{1,0:T(8,128)(2,1)S(1)}, bf16[128,2304]{1,0:T(8,128)(2,1)S(1)}, u32[]{:S(2)}, u32[]{:S(2)}) collective-permute-start(bf16[128,2304]{1,0:T(8,128)(2,1)S(1)} %get-tuple-element.216), channel_id=1, source_target_pairs={{0,8},{1,9},{2,0},{3,1},{4,12},{5,13},{6,4},{7,5},{8,16},{9,17},{1... | collective-permute-start | bytes 1769480 | tf_op jit(solution)/shard_map/ppermute | solution.py:125
  484.7 12.2 %collective-permute-start.38 = (bf16[128,2304]{1,0:T(8,128)(2,1)S(1)}, bf16[128,2304]{1,0:T(8,128)(2,1)S(1)}, u32[]{:S(2)}, u32[]{:S(2)}) collective-permute-start(bf16[128,2304]{1,0:T(8,128)(2,1)S(1)} %get-tuple-element.215), channel_id=1, source_target_pairs={{0,2},{1,3},{2,10},{3,11},{4,6},{5,7},{6,14},{7,15},{8,0},{9,1},{1... | collective-permute-start | bytes 1769480 | tf_op jit(solution)/shard_map/ppermute | solution.py:125
  499.3 19.6 %collective-permute-start.39 = (bf16[128,2304]{1,0:T(8,128)(2,1)S(1)}, bf16[128,2304]{1,0:T(8,128)(2,1)S(1)}, u32[]{:S(2)}, u32[]{:S(2)}) collective-permute-start(bf16[128,2304]{1,0:T(8,128)(2,1)S(1)} %get-tuple-element.174), channel_id=1, source_target_pairs={{0,1},{1,0},{2,3},{3,2},{4,5},{5,4},{6,7},{7,6},{8,9},{9,8},{10,11... | collective-permute-start | bytes 1769480 | tf_op jit(solution)/shard_map/ppermute | solution.py:125
  503.2 14.8 %collective-permute-start.40 = (bf16[128,2304]{1,0:T(8,128)(2,1)S(1)}, bf16[128,2304]{1,0:T(8,128)(2,1)S(1)}, u32[]{:S(2)}, u32[]{:S(2)}) collective-permute-start(bf16[128,2304]{1,0:T(8,128)(2,1)S(1)} %get-tuple-element.174), channel_id=1, source_target_pairs={{0,2},{1,3},{2,0},{3,1},{4,6},{5,7},{6,4},{7,5},{8,10},{9,11},{10,... | collective-permute-start | bytes 1769480 | tf_op jit(solution)/shard_map/ppermute | solution.py:125
  507.9 117.8 %collective-permute-start.54 = (bf16[1152,1152]{1,0:T(8,128)(2,1)}, bf16[1152,1152]{1,0:T(8,128)(2,1)}, u32[]{:S(2)}, u32[]{:S(2)}) collective-permute-start(bf16[1152,1152]{1,0:T(8,128)(2,1)} %convolution_convert_fusion.2), channel_id=1, source_target_pairs={{0,1},{1,0},{2,3},{3,2},{4,5},{5,4},{6,7},{7,6},{8,9},{9,8},{10,11... | collective-permute-start | bytes 7962632 | tf_op jit(solution)/shard_map/ppermute | solution.py:125
  518.0 3.6 collective-permute-start.41
  521.5 64.2 %collective-permute-start.59 = (bf16[576,1152]{1,0:T(8,128)(2,1)}, bf16[576,1152]{1,0:T(8,128)(2,1)}, u32[]{:S(2)}, u32[]{:S(2)}) collective-permute-start(bf16[576,1152]{1,0:T(8,128)(2,1)} %bitcast.66), channel_id=1, source_target_pairs={{0,4},{1,5},{2,6},{3,7},{4,0},{5,1},{6,2},{7,3},{8,12},{9,13},{10,... | collective-permute-start | bytes 3981320 | tf_op jit(solution)/shard_map/ppermute | solution.py:125
  545.2 22.1 %collective-permute-start.42 = (bf16[256,512]{1,0:T(8,128)(2,1)S(1)}, bf16[256,512]{1,0:T(8,128)(2,1)S(1)}, u32[]{:S(2)}, u32[]{:S(2)}) collective-permute-start(bf16[256,512]{1,0:T(8,128)(2,1)S(1)} %get-tuple-element.202), channel_id=1, source_target_pairs={{0,8},{1,9},{2,10},{3,11},{4,0},{5,1},{6,2},{7,3},{8,16},{9,17},{1... | collective-permute-start | bytes 786440 | tf_op jit(solution)/shard_map/ppermute | solution.py:125
  554.6 12.7 %collective-permute-start.43 = (bf16[256,512]{1,0:T(8,128)(2,1)S(1)}, bf16[256,512]{1,0:T(8,128)(2,1)S(1)}, u32[]{:S(2)}, u32[]{:S(2)}) collective-permute-start(bf16[256,512]{1,0:T(8,128)(2,1)S(1)} %get-tuple-element.203), channel_id=1, source_target_pairs={{0,4},{1,5},{2,6},{3,7},{4,12},{5,13},{6,14},{7,15},{8,0},{9,1},{1... | collective-permute-start | bytes 786440 | tf_op jit(solution)/shard_map/ppermute | solution.py:125
  568.6 13.1 %collective-permute-start.45 = (bf16[512,512]{1,0:T(8,128)(2,1)S(1)}, bf16[512,512]{1,0:T(8,128)(2,1)}, u32[]{:S(2)}, u32[]{:S(2)}) collective-permute-start(bf16[512,512]{1,0:T(8,128)(2,1)S(1)} %pad_maximum_fusion.22), channel_id=1, source_target_pairs={{0,4},{1,5},{2,6},{3,7},{4,12},{5,13},{6,14},{7,15},{8,0},{9,1},{1... | collective-permute-start | bytes 1572872 | tf_op jit(solution)/shard_map/ppermute | solution.py:125
  569.5 13.2 %collective-permute-start.44 = (bf16[512,512]{1,0:T(8,128)(2,1)}, bf16[512,512]{1,0:T(8,128)(2,1)}, u32[]{:S(2)}, u32[]{:S(2)}) collective-permute-start(bf16[512,512]{1,0:T(8,128)(2,1)} %pad_maximum_fusion.21), channel_id=1, source_target_pairs={{0,8},{1,9},{2,10},{3,11},{4,0},{5,1},{6,2},{7,3},{8,16},{9,17},{1... | collective-permute-start | bytes 1572872 | tf_op jit(solution)/shard_map/ppermute | solution.py:125
  575.5 54.8 %collective-permute-start.51 = (bf16[576,1152]{1,0:T(8,128)(2,1)S(1)}, bf16[576,1152]{1,0:T(8,128)(2,1)S(1)}, u32[]{:S(2)}, u32[]{:S(2)}) collective-permute-start(bf16[576,1152]{1,0:T(8,128)(2,1)S(1)} %bitcast.210), channel_id=1, source_target_pairs={{0,4},{1,5},{2,6},{3,7},{4,0},{5,1},{6,2},{7,3},{8,12},{9,13},{10,... | collective-permute-start | bytes 3981320 | tf_op jit(solution)/shard_map/ppermute | solution.py:125
  584.2 37.0 %collective-permute-start.46 = (bf16[512,512]{1,0:T(8,128)(2,1)S(1)}, bf16[512,512]{1,0:T(8,128)(2,1)S(1)}, u32[]{:S(2)}, u32[]{:S(2)}) collective-permute-start(bf16[512,512]{1,0:T(8,128)(2,1)S(1)} %get-tuple-element.200), channel_id=1, source_target_pairs={{0,8},{1,9},{2,10},{3,11},{4,0},{5,1},{6,2},{7,3},{8,16},{9,17},{1... | collective-permute-start | bytes 1572872 | tf_op jit(solution)/shard_map/ppermute | solution.py:125
  585.4 37.7 %collective-permute-start.47 = (bf16[512,512]{1,0:T(8,128)(2,1)S(1)}, bf16[512,512]{1,0:T(8,128)(2,1)S(1)}, u32[]{:S(2)}, u32[]{:S(2)}) collective-permute-start(bf16[512,512]{1,0:T(8,128)(2,1)S(1)} %get-tuple-element.199), channel_id=1, source_target_pairs={{0,4},{1,5},{2,6},{3,7},{4,12},{5,13},{6,14},{7,15},{8,0},{9,1},{1... | collective-permute-start | bytes 1572872 | tf_op jit(solution)/shard_map/ppermute | solution.py:125
  587.7 45.4 %collective-permute-start.60 = (bf16[288,1152]{1,0:T(8,128)(2,1)S(1)}, bf16[288,1152]{1,0:T(8,128)(2,1)S(1)}, u32[]{:S(2)}, u32[]{:S(2)}) collective-permute-start(bf16[288,1152]{1,0:T(8,128)(2,1)S(1)} %get-tuple-element.250), channel_id=1, source_target_pairs={{8,0},{24,1},{10,2},{26,3},{12,4},{28,5},{14,6},{30,7},{0,8},{16,9... | collective-permute-start | bytes 1990664 | tf_op jit(solution)/shard_map/ppermute | solution.py:125
  621.2 21.1 %collective-permute-start.61 = (bf16[288,1152]{1,0:T(8,128)(2,1)S(1)}, bf16[288,1152]{1,0:T(8,128)(2,1)S(1)}, u32[]{:S(2)}, u32[]{:S(2)}) collective-permute-start(bf16[288,1152]{1,0:T(8,128)(2,1)S(1)} %get-tuple-element.249), channel_id=1, source_target_pairs={{0,0},{16,1},{2,2},{18,3},{4,4},{20,5},{6,6},{22,7},{8,8},{24,9},{... | collective-permute-start | bytes 1990664 | tf_op jit(solution)/shard_map/ppermute | solution.py:125
  623.5 22.6 %collective-permute-start.48 = (bf16[512,512]{1,0:T(8,128)(2,1)S(1)}, bf16[512,512]{1,0:T(8,128)(2,1)S(1)}, u32[]{:S(2)}, u32[]{:S(2)}) collective-permute-start(bf16[512,512]{1,0:T(8,128)(2,1)S(1)} %get-tuple-element.198), channel_id=1, source_target_pairs={{0,8},{1,9},{2,10},{3,11},{4,0},{5,1},{6,2},{7,3},{8,16},{9,17},{1... | collective-permute-start | bytes 1572872 | tf_op jit(solution)/shard_map/ppermute | solution.py:125
  625.7 20.3 %collective-permute-start.49 = (bf16[512,512]{1,0:T(8,128)(2,1)S(1)}, bf16[512,512]{1,0:T(8,128)(2,1)S(1)}, u32[]{:S(2)}, u32[]{:S(2)}) collective-permute-start(bf16[512,512]{1,0:T(8,128)(2,1)S(1)} %get-tuple-element.197), channel_id=1, source_target_pairs={{0,4},{1,5},{2,6},{3,7},{4,12},{5,13},{6,14},{7,15},{8,0},{9,1},{1... | collective-permute-start | bytes 1572872 | tf_op jit(solution)/shard_map/ppermute | solution.py:125
  630.3 131.6 %collective-permute-start.55 = (bf16[576,1152]{1,0:T(8,128)(2,1)}, bf16[576,1152]{1,0:T(8,128)(2,1)}, u32[]{:S(2)}, u32[]{:S(2)}) collective-permute-start(bf16[576,1152]{1,0:T(8,128)(2,1)} %bitcast.59), channel_id=1, source_target_pairs={{0,4},{1,5},{2,6},{3,7},{4,0},{5,1},{6,2},{7,3},{8,12},{9,13},{10,... | collective-permute-start | bytes 3981320 | tf_op jit(solution)/shard_map/ppermute | solution.py:125
  633.2 137.6 %collective-permute-start.52 = (bf16[288,1152]{1,0:T(8,128)(2,1)}, bf16[288,1152]{1,0:T(8,128)(2,1)}, u32[]{:S(2)}, u32[]{:S(2)}) collective-permute-start(bf16[288,1152]{1,0:T(8,128)(2,1)} %get-tuple-element.258), channel_id=1, source_target_pairs={{8,0},{24,1},{10,2},{26,3},{12,4},{28,5},{14,6},{30,7},{0,8},{16,9... | collective-permute-start | bytes 1990664 | tf_op jit(solution)/shard_map/ppermute | solution.py:125
  642.3 128.5 %collective-permute-start.53 = (bf16[288,1152]{1,0:T(8,128)(2,1)}, bf16[288,1152]{1,0:T(8,128)(2,1)}, u32[]{:S(2)}, u32[]{:S(2)}) collective-permute-start(bf16[288,1152]{1,0:T(8,128)(2,1)} %get-tuple-element.257), channel_id=1, source_target_pairs={{0,0},{16,1},{2,2},{18,3},{4,4},{20,5},{6,6},{22,7},{8,8},{24,9},{... | collective-permute-start | bytes 1990664 | tf_op jit(solution)/shard_map/ppermute | solution.py:125
  763.9 17.8 %collective-permute-start.56 = (bf16[288,1152]{1,0:T(8,128)(2,1)S(1)}, bf16[288,1152]{1,0:T(8,128)(2,1)S(1)}, u32[]{:S(2)}, u32[]{:S(2)}) collective-permute-start(bf16[288,1152]{1,0:T(8,128)(2,1)S(1)} %get-tuple-element.254), channel_id=1, source_target_pairs={{8,0},{24,1},{10,2},{26,3},{12,4},{28,5},{14,6},{30,7},{0,8},{16,9... | collective-permute-start | bytes 1990664 | tf_op jit(solution)/shard_map/ppermute | solution.py:125
  765.7 32.2 %collective-permute-start.57 = (bf16[288,1152]{1,0:T(8,128)(2,1)S(1)}, bf16[288,1152]{1,0:T(8,128)(2,1)S(1)}, u32[]{:S(2)}, u32[]{:S(2)}) collective-permute-start(bf16[288,1152]{1,0:T(8,128)(2,1)S(1)} %get-tuple-element.253), channel_id=1, source_target_pairs={{0,0},{16,1},{2,2},{18,3},{4,4},{20,5},{6,6},{22,7},{8,8},{24,9},{... | collective-permute-start | bytes 1990664 | tf_op jit(solution)/shard_map/ppermute | solution.py:125
  (99 other events, 937.5 us)

commit v3 on v2

--- a/solution.py
+++ b/solution.py
@@ -897,7 +897,10 @@
     slice_cols = w_gate.shape[1] // halves
 
     def slice_perm(p):
-        return plan.perm(lambda l, s, r, c: (c * halves + (l + p) % halves, s, r, l // halves))
+        def target(l, s, r, c):
+            return c * halves + (l + p) % halves, s, r, (l // halves + 1) % cores
+
+        return plan.perm(target)
 
     def slice_back(p):
         return [(b, a) for a, b in slice_perm(p)]
@@ -920,7 +923,7 @@
                 for p in range(halves):
                     n = k * halves + p
                     blocks.append(found[n * size : (n + 1) * size])
-                    origin = (core + m) % cores * halves + (layer - p) % halves
+                    origin = (core + m + cores - 1) % cores * halves + (layer - p) % halves
                     where.append(origin * sides + (side + k) % sides)
         return place_rows(blocks, where, contexts).reshape(width, slice_cols)
 
@@ -954,7 +957,7 @@
 
     ffn_down = slice_fetch(after(w_down, kv))
     head_o, lse = attend(queries, kv, own_spans, key_spans, boundary, span)
-    attn_out = group_scatter(dot(head_o, col_out, 1, 1))
+    attn_out = group_scatter(dot(head_o, col_out, 1, 1).astype(bf16))
     tok_own = tokens.astype(f32)
     hidden_in = tok_own + norm_apply(attn_out, weight_two)
     normed_own = norm_apply(hidden_in, weight_three).astype(bf16)
@@ -1013,7 +1016,8 @@
 
     def by_core(pieces):
         cols = width // cores
-        cut = lambda x, m: lax.dynamic_slice_in_dim(x, (core + m) % cores * cols, cols, 1)
+        place = lambda m: (core + m + cores - 1) % cores * cols
+        cut = lambda x, m: lax.dynamic_slice_in_dim(x, place(m), cols, 1)
         return [jnp.concatenate([cut(x, m) for x in pieces], axis=0) for m in range(cores)]
 
     d_ffn, normed_mid = by_core(d_ffn), by_core(normed_mid)

time: 813 us -> 806 us (level)
  the two profiles are of different devices: /device:TPU:3 before, /device:TPU:1 now
where the time goes in v3:
time: 806 us; the launch traced here: 797 us
  Pallas kernels  319 us (40%)
  waiting for transfers between devices  209 us (26%)
  matrix products  100 us (12%)
  starting transfers between devices  70.9 us (9%)
  other arithmetic  67.2 us (8%)
  local copies, waits for them, and re-layouts  22.4 us (3%)
    ppermute x62, waiting for transfers between devices, move(): return lax.ppermute(values, AXES, perm)  209 us
    pallas_call x1, Pallas kernels, fetch_weights(): pl.pallas_call(functools.partial(weights_kernel, plan), out_shape=results...  111 us
    dot_general x26, matrix products, dot(): lax.dot_general(left, right, (((left_dim,), (right_dim,)), ((), ())), pre...  100 us
    pallas_call x1, Pallas kernels, sum_grads(): pl.pallas_call(functools.partial(grads_kernel, plan), out_shape=results,...  93.9 us
    pallas_call x1, Pallas kernels, fetch_keys(): pl.pallas_call(functools.partial(keys_kernel, plan), out_shape=[jax.Shape...  75.8 us
    ppermute x62, starting transfers between devices, move(): return lax.ppermute(values, AXES, perm)  70.9 us
    pallas_call x1, Pallas kernels, attend_back(): pl.pallas_call(functools.partial(attend_back_kernel, span, repeat, chunk)...  23 us
  transfers between devices with their start and end apart: 62, of which 30 were waited for; matrix products, arithmetic and copies ran while one was open for 17% of the time, Pallas kernels for 15%

profile of v3, /device:TPU:1, one launch (start us, length us, event | category | flops | bytes accessed | tf_op | source)
XLA Modules:
  0.0 796.5 jit_solution(28435641977107829)
XLA Ops:
  2.0 110.9 %shard_map.255 = (bf16[4,128,2304]{2,1,0:T(8,128)(2,1)}, bf16[32,72,1024]{2,1,0:T(8,128)(2,1)}, bf16[8,288,512]{2,1,0:T(8,128)(2,1)}, f32[32,8,128]{2,1,0:T(8,128)}, bf16[8,288,1152]{2,1,0:T(8,128)(2,1)}) custom-call(bf16[128,2304]{1,0:T(8,128)(2,1)} %refs_0_.1, bf16[72,2048]{1,0:T(8,128)(2,1)} %refs_1_.1, bf16[72,1024]{1,0:T(8,128)(2,1)} %refs_2_.1, ...), custom_call_target="tpu_custom_call" | custom-call | tf_op jit(solution)/shard_map/pallas_call | solution.py:404
  120.7 2.6 fusion.101
  126.1 75.8 %shard_map.256 = (bf16[8,512,512]{2,1,0:T(8,128)(2,1)}, bf16[8,288,1152]{2,1,0:T(8,128)(2,1)}) custom-call(bf16[512,512]{1,0:T(8,128)(2,1)} %pad_maximum_fusion.19.kv_in, bf16[288,2304]{1,0:T(8,128)(2,1)} %up_in.1), custom_call_target="tpu_custom_call" | custom-call | tf_op jit(solution)/shard_map/pallas_call | solution.py:438
  202.8 15.2 %shard_map.257 = (bf16[512,512]{1,0:T(8,128)(2,1)}, f32[512,256]{1,0:T(8,128)}) custom-call(s32[2]{0:T(128)} %copy-done.63, s32[16]{0:T(128)} %broadcast_multiply_fusion.4.kp, s32[1]{0:T(128)} %bitcast.bd, bf16[512,512]{1,0:T(8,128)(2,1)} %fusion.31.q_ref, bf16[4096,512]{1,0:T(8,128)(2,1)} %bitcast.227), custom_call_target="tpu_custom_call" | custom-call | flops 2147483648 | bytes 8388608 | tf_op jit(solution)/shard_map/pallas_call | solution.py:711
  218.1 3.3 convolution_convert_fusion.11
  228.9 11.4 %collective-permute-done.11 = bf16[288,1152]{1,0:T(8,128)(2,1)S(1)} collective-permute-done((bf16[288,1152]{1,0:T(8,128)(2,1)}, bf16[288,1152]{1,0:T(8,128)(2,1)S(1)}, u32[]{:S(2)}, u32[]{:S(2)}) %collective-permute-start.11) | collective-permute-done | bytes 663584 | tf_op jit(solution)/shard_map/ppermute | solution.py:125
  240.3 10.2 %collective-permute-done.12 = bf16[288,1152]{1,0:T(8,128)(2,1)S(1)} collective-permute-done((bf16[288,1152]{1,0:T(8,128)(2,1)}, bf16[288,1152]{1,0:T(8,128)(2,1)S(1)}, u32[]{:S(2)}, u32[]{:S(2)}) %collective-permute-start.12) | collective-permute-done | bytes 663584 | tf_op jit(solution)/shard_map/ppermute | solution.py:125
  254.7 4.1 collective-permute-start.3
  259.3 10.7 %collective-permute-done.3 = bf16[128,2304]{1,0:T(8,128)(2,1)S(1)} collective-permute-done((bf16[128,2304]{1,0:T(8,128)(2,1)S(1)}, bf16[128,2304]{1,0:T(8,128)(2,1)S(1)}, u32[]{:S(2)}, u32[]{:S(2)}) %collective-permute-start.3) | collective-permute-done | bytes 589856 | tf_op jit(solution)/shard_map/ppermute | solution.py:125
  270.1 2.6 collective-permute-done.4
  272.6 3.1 collective-permute-start.5
  275.9 4.2 collective-permute-done.13
  280.6 7.4 collective-permute-done.5
  291.7 4.0 fusion.102
  295.7 7.4 collective-permute-done.7
  304.9 3.9 collective-permute-done.9
  313.2 3.8 multiply_convert_fusion.4
  322.2 5.8 multiply_convert_fusion.2
  329.8 4.2 convolution_convert_fusion.7
  334.1 5.6 collective-permute-done.18
  341.5 10.0 %collective-permute-done.19 = bf16[128,2304]{1,0:T(8,128)(2,1)S(1)} collective-permute-done((bf16[128,2304]{1,0:T(8,128)(2,1)S(1)}, bf16[128,2304]{1,0:T(8,128)(2,1)S(1)}, u32[]{:S(2)}, u32[]{:S(2)}) %collective-permute-start.19) | collective-permute-done | bytes 589856 | tf_op jit(solution)/shard_map/ppermute | solution.py:125
  367.6 2.7 constant_dynamic-update-slice_fusion.13
  372.5 6.6 collective-permute-done.23
  381.3 13.5 %collective-permute-done.25 = bf16[128,2304]{1,0:T(8,128)(2,1)S(1)} collective-permute-done((bf16[128,2304]{1,0:T(8,128)(2,1)S(1)}, bf16[128,2304]{1,0:T(8,128)(2,1)S(1)}, u32[]{:S(2)}, u32[]{:S(2)}) %collective-permute-start.25) | collective-permute-done | bytes 589856 | tf_op jit(solution)/shard_map/ppermute | solution.py:125
  396.6 6.2 multiply_convert_fusion.1
  403.2 7.6 collective-permute-done.27
  412.9 5.6 collective-permute-done.29
  420.7 3.1 fusion.23
  423.9 2.5 convolution_convert_fusion.12
  426.5 5.1 fusion.3
  431.6 4.4 convolution_convert_fusion.6
  437.6 7.0 add_convert_fusion
  446.9 3.3 convolution_convert_fusion
  450.2 13.4 %collective-permute-start.58 = (bf16[1152,1152]{1,0:T(8,128)(2,1)S(1)}, bf16[1152,1152]{1,0:T(8,128)(2,1)S(1)}, u32[]{:S(2)}, u32[]{:S(2)}) collective-permute-start(bf16[1152,1152]{1,0:T(8,128)(2,1)S(1)} %convolution_convert_fusion), channel_id=1, source_target_pairs={{0,1},{1,0},{2,3},{3,2},{4,5},{5,4},{6,7},{7,6},{8,9},{9,8},{10,11... | collective-permute-start | bytes 7962632 | tf_op jit(solution)/shard_map/ppermute | solution.py:125
  463.7 3.3 convolution_convert_fusion.1
  468.8 4.8 convolution_convert_fusion.4
  473.5 3.1 collective-permute-start.50
  476.6 3.1 collective-permute-done.35
  483.3 4.8 convolution_convert_fusion.5
  488.1 5.1 collective-permute-done.37
  497.8 3.8 collective-permute-start.39
  501.6 4.8 convolution_convert_fusion.2
  507.6 4.7 convolution_convert_fusion.3
  512.3 4.1 collective-permute-done.40
  520.0 2.6 convert_multiply_fusion.3
  523.9 23.0 %shard_map.258 = (f32[512,512]{1,0:T(8,128)}, bf16[4096,512]{1,0:T(8,128)(2,1)}) custom-call(s32[2]{0:T(128)} %copy-done.63, s32[16]{0:T(128)} %broadcast_multiply_fusion.4.kp, s32[1]{0:T(128)} %bitcast.bd, bf16[512,512]{1,0:T(8,128)(2,1)} %fusion.31.q_ref, bf16[512,512]{1,0:T(8,128)(2,1)} %get-tuple-element.299.g_ref, ...), custom_call_target="tpu_custom_call" | custom-call | flops 5368709120 | bytes 8388608 | tf_op jit(solution)/shard_map/pallas_call | solution.py:773
  547.0 3.2 multiply_cosine_fusion
  553.1 2.9 convolution_convert_fusion.8
  556.1 3.1 multiply_reduce_fusion.1
  559.2 3.6 fusion.15
  562.8 2.9 convolution_convert_fusion.10
  570.6 3.2 add_convert_fusion.3
  573.9 6.1 collective-permute-done.45
  586.1 3.4 collective-permute-start.60
  589.5 31.2 %collective-permute-done.46 = bf16[512,512]{1,0:T(8,128)(2,1)S(1)} collective-permute-done((bf16[512,512]{1,0:T(8,128)(2,1)S(1)}, bf16[512,512]{1,0:T(8,128)(2,1)S(1)}, u32[]{:S(2)}, u32[]{:S(2)}) %collective-permute-start.46) | collective-permute-done | bytes 524320 | tf_op jit(solution)/shard_map/ppermute | solution.py:125
  624.1 4.3 add_convert_fusion.2
  630.2 2.7 collective-permute-done.61
  632.9 4.3 collective-permute-start.53
  639.1 11.1 %collective-permute-done.49 = bf16[512,512]{1,0:T(8,128)(2,1)S(1)} collective-permute-done((bf16[512,512]{1,0:T(8,128)(2,1)S(1)}, bf16[512,512]{1,0:T(8,128)(2,1)S(1)}, u32[]{:S(2)}, u32[]{:S(2)}) %collective-permute-start.49) | collective-permute-done | bytes 524320 | tf_op jit(solution)/shard_map/ppermute | solution.py:125
  650.6 2.8 convolution_convert_fusion.9
  653.4 2.9 fusion.2
  656.4 93.9 %shard_map.259 = (f32[72,2048]{1,0:T(8,128)}, f32[72,1024]{1,0:T(8,128)}, f32[72,1024]{1,0:T(8,128)}, f32[4,72,512]{2,1,0:T(8,128)}, f32[128,2304]{1,0:T(8,128)}, /*index=5*/f32[8,128]{1,0:T(8,128)}) custom-call(bf16[32,72,512]{2,1,0:T(8,128)(2,1)} %bitcast.203, bf16[32,72,512]{2,1,0:T(8,128)(2,1)} %bitcast.204, bf16[32,72,512]{2,1,0:T(8,128)(2,1)} %bitcast.202, ...), custom_call_target="tpu_custom_call" | custom-call | tf_op jit(solution)/shard_map/pallas_call | solution.py:589
  763.1 14.6 %collective-permute-done.56 = bf16[288,1152]{1,0:T(8,128)(2,1)S(1)} collective-permute-done((bf16[288,1152]{1,0:T(8,128)(2,1)S(1)}, bf16[288,1152]{1,0:T(8,128)(2,1)S(1)}, u32[]{:S(2)}, u32[]{:S(2)}) %collective-permute-start.56) | collective-permute-done | bytes 663584 | tf_op jit(solution)/shard_map/ppermute | solution.py:125
  777.7 13.7 %collective-permute-done.57 = bf16[288,1152]{1,0:T(8,128)(2,1)S(1)} collective-permute-done((bf16[288,1152]{1,0:T(8,128)(2,1)S(1)}, bf16[288,1152]{1,0:T(8,128)(2,1)S(1)}, u32[]{:S(2)}, u32[]{:S(2)}) %collective-permute-start.57) | collective-permute-done | bytes 663584 | tf_op jit(solution)/shard_map/ppermute | solution.py:125
  (440 shorter events, 124.3 us)
Async XLA Ops:
  0.7 123.3 %copy-start.61 = (f32[128]{0:T(128)}, f32[128]{0:T(128)S(1)}, u32[]{:S(2)}) copy-start(f32[128]{0:T(128)S(1)} %multiply_power_fusion) | copy-start | bytes 1540
  2.0 115.7 %copy-start.66 = (s32[16]{0:T(128)S(1)}, s32[16]{0:T(128)}, u32[]{:S(2)}) copy-start(s32[16]{0:T(128)} %param.20) | copy-start | bytes 196
  222.6 3.4 collective-permute-start.1
  223.4 27.2 %collective-permute-start = (bf16[128,2304]{1,0:T(8,128)(2,1)}, bf16[128,2304]{1,0:T(8,128)(2,1)}, u32[]{:S(2)}, u32[]{:S(2)}) collective-permute-start(bf16[128,2304]{1,0:T(8,128)(2,1)} %get-tuple-element.221), channel_id=1, source_target_pairs={{0,1},{1,0},{2,3},{3,2},{4,5},{5,4},{6,7},{7,6},{8,9},{9,8},{10,11... | collective-permute-start | bytes 1769480 | tf_op jit(solution)/shard_map/ppermute | solution.py:125
  225.9 14.4 %collective-permute-start.11 = (bf16[288,1152]{1,0:T(8,128)(2,1)}, bf16[288,1152]{1,0:T(8,128)(2,1)S(1)}, u32[]{:S(2)}, u32[]{:S(2)}) collective-permute-start(bf16[288,1152]{1,0:T(8,128)(2,1)} %get-tuple-element.260), channel_id=1, source_target_pairs={{0,1},{1,17},{2,3},{3,19},{4,5},{5,21},{6,7},{7,23},{8,9},{9,25},{... | collective-permute-start | bytes 1990664 | tf_op jit(solution)/shard_map/ppermute | solution.py:125
  225.9 24.5 %collective-permute-start.12 = (bf16[288,1152]{1,0:T(8,128)(2,1)}, bf16[288,1152]{1,0:T(8,128)(2,1)S(1)}, u32[]{:S(2)}, u32[]{:S(2)}) collective-permute-start(bf16[288,1152]{1,0:T(8,128)(2,1)} %get-tuple-element.259), channel_id=1, source_target_pairs={{0,9},{1,25},{2,11},{3,27},{4,13},{5,29},{6,15},{7,31},{8,1},{9,17... | collective-permute-start | bytes 1990664 | tf_op jit(solution)/shard_map/ppermute | solution.py:125
  227.4 23.9 %collective-permute-start.2 = (bf16[128,2304]{1,0:T(8,128)(2,1)S(1)}, bf16[128,2304]{1,0:T(8,128)(2,1)S(1)}, u32[]{:S(2)}, u32[]{:S(2)}) collective-permute-start(bf16[128,2304]{1,0:T(8,128)(2,1)S(1)} %fusion.29), channel_id=1, source_target_pairs={{0,2},{1,3},{2,0},{3,1},{4,6},{5,7},{6,4},{7,5},{8,10},{9,11},{10,... | collective-permute-start | bytes 1769480 | tf_op jit(solution)/shard_map/ppermute | solution.py:125
  250.6 29.6 %collective-permute-start.13 = (bf16[576,1152]{1,0:T(8,128)(2,1)S(1)}, bf16[576,1152]{1,0:T(8,128)(2,1)S(1)}, u32[]{:S(2)}, u32[]{:S(2)}) collective-permute-start(bf16[576,1152]{1,0:T(8,128)(2,1)S(1)} %pad_maximum_fusion.14), channel_id=1, source_target_pairs={{0,4},{1,5},{2,6},{3,7},{4,0},{5,1},{6,2},{7,3},{8,12},{9,13},{10,... | collective-permute-start | bytes 3981320 | tf_op jit(solution)/shard_map/ppermute | solution.py:125
  254.7 15.4 %collective-permute-start.3 = (bf16[128,2304]{1,0:T(8,128)(2,1)S(1)}, bf16[128,2304]{1,0:T(8,128)(2,1)S(1)}, u32[]{:S(2)}, u32[]{:S(2)}) collective-permute-start(bf16[128,2304]{1,0:T(8,128)(2,1)S(1)} %get-tuple-element.182), channel_id=1, source_target_pairs={{0,8},{1,9},{2,0},{3,1},{4,12},{5,13},{6,4},{7,5},{8,16},{9,17},{1... | collective-permute-start | bytes 1769480 | tf_op jit(solution)/shard_map/ppermute | solution.py:125
  258.8 13.9 %collective-permute-start.4 = (bf16[128,2304]{1,0:T(8,128)(2,1)S(1)}, bf16[128,2304]{1,0:T(8,128)(2,1)S(1)}, u32[]{:S(2)}, u32[]{:S(2)}) collective-permute-start(bf16[128,2304]{1,0:T(8,128)(2,1)S(1)} %get-tuple-element.182), channel_id=1, source_target_pairs={{0,2},{1,3},{2,10},{3,11},{4,6},{5,7},{6,14},{7,15},{8,0},{9,1},{1... | collective-permute-start | bytes 1769480 | tf_op jit(solution)/shard_map/ppermute | solution.py:125
  272.6 15.3 %collective-permute-start.5 = (bf16[128,2304]{1,0:T(8,128)(2,1)S(1)}, bf16[128,2304]{1,0:T(8,128)(2,1)S(1)}, u32[]{:S(2)}, u32[]{:S(2)}) collective-permute-start(bf16[128,2304]{1,0:T(8,128)(2,1)S(1)} %collective-permute-done.3), channel_id=1, source_target_pairs={{0,8},{1,9},{2,0},{3,1},{4,12},{5,13},{6,4},{7,5},{8,16},{9,17},{1... | collective-permute-start | bytes 1769480 | tf_op jit(solution)/shard_map/ppermute | solution.py:125
  275.8 14.1 %collective-permute-start.6 = (bf16[128,2304]{1,0:T(8,128)(2,1)S(1)}, bf16[128,2304]{1,0:T(8,128)(2,1)S(1)}, u32[]{:S(2)}, u32[]{:S(2)}) collective-permute-start(bf16[128,2304]{1,0:T(8,128)(2,1)S(1)} %collective-permute-done.4), channel_id=1, source_target_pairs={{0,2},{1,3},{2,10},{3,11},{4,6},{5,7},{6,14},{7,15},{8,0},{9,1},{1... | collective-permute-start | bytes 1769480 | tf_op jit(solution)/shard_map/ppermute | solution.py:125
  280.3 36.6 %collective-permute-start.14 = (bf16[1152,1152]{1,0:T(8,128)(2,1)S(1)}, bf16[1152,1152]{1,0:T(8,128)(2,1)S(1)}, u32[]{:S(2)}, u32[]{:S(2)}) collective-permute-start(bf16[1152,1152]{1,0:T(8,128)(2,1)S(1)} %pad_maximum_fusion), channel_id=1, source_target_pairs={{0,1},{1,0},{2,3},{3,2},{4,5},{5,4},{6,7},{7,6},{8,9},{9,8},{10,11... | collective-permute-start | bytes 7962632 | tf_op jit(solution)/shard_map/ppermute | solution.py:125
  289.9 13.2 %collective-permute-start.8 = (bf16[128,2304]{1,0:T(8,128)(2,1)S(1)}, bf16[128,2304]{1,0:T(8,128)(2,1)S(1)}, u32[]{:S(2)}, u32[]{:S(2)}) collective-permute-start(bf16[128,2304]{1,0:T(8,128)(2,1)S(1)} %collective-permute-done.6), channel_id=1, source_target_pairs={{0,2},{1,3},{2,10},{3,11},{4,6},{5,7},{6,14},{7,15},{8,0},{9,1},{1... | collective-permute-start | bytes 1769480 | tf_op jit(solution)/shard_map/ppermute | solution.py:125
  289.9 13.2 %collective-permute-start.7 = (bf16[128,2304]{1,0:T(8,128)(2,1)S(1)}, bf16[128,2304]{1,0:T(8,128)(2,1)S(1)}, u32[]{:S(2)}, u32[]{:S(2)}) collective-permute-start(bf16[128,2304]{1,0:T(8,128)(2,1)S(1)} %collective-permute-done.5), channel_id=1, source_target_pairs={{0,8},{1,9},{2,0},{3,1},{4,12},{5,13},{6,4},{7,5},{8,16},{9,17},{1... | collective-permute-start | bytes 1769480 | tf_op jit(solution)/shard_map/ppermute | solution.py:125
  303.2 5.6 collective-permute-start.9
  304.7 5.9 collective-permute-start.10
  320.5 7.5 collective-permute-start.15
  321.1 6.9 collective-permute-start.16
  328.2 11.5 %collective-permute-start.18 = (bf16[128,2304]{1,0:T(8,128)(2,1)S(1)}, bf16[128,2304]{1,0:T(8,128)(2,1)S(1)}, u32[]{:S(2)}, u32[]{:S(2)}) collective-permute-start(bf16[128,2304]{1,0:T(8,128)(2,1)S(1)} %pad_maximum_fusion.16), channel_id=1, source_target_pairs={{0,2},{1,3},{2,10},{3,11},{4,6},{5,7},{6,14},{7,15},{8,0},{9,1},{1... | collective-permute-start | bytes 1769480 | tf_op jit(solution)/shard_map/ppermute | solution.py:125
  328.3 11.3 %collective-permute-start.17 = (bf16[128,2304]{1,0:T(8,128)(2,1)S(1)}, bf16[128,2304]{1,0:T(8,128)(2,1)S(1)}, u32[]{:S(2)}, u32[]{:S(2)}) collective-permute-start(bf16[128,2304]{1,0:T(8,128)(2,1)S(1)} %pad_maximum_fusion.15), channel_id=1, source_target_pairs={{0,8},{1,9},{2,0},{3,1},{4,12},{5,13},{6,4},{7,5},{8,16},{9,17},{1... | collective-permute-start | bytes 1769480 | tf_op jit(solution)/shard_map/ppermute | solution.py:125
  340.0 11.5 %collective-permute-start.19 = (bf16[128,2304]{1,0:T(8,128)(2,1)S(1)}, bf16[128,2304]{1,0:T(8,128)(2,1)S(1)}, u32[]{:S(2)}, u32[]{:S(2)}) collective-permute-start(bf16[128,2304]{1,0:T(8,128)(2,1)S(1)} %get-tuple-element.220), channel_id=1, source_target_pairs={{0,8},{1,9},{2,0},{3,1},{4,12},{5,13},{6,4},{7,5},{8,16},{9,17},{1... | collective-permute-start | bytes 1769480 | tf_op jit(solution)/shard_map/ppermute | solution.py:125
  340.7 10.8 %collective-permute-start.20 = (bf16[128,2304]{1,0:T(8,128)(2,1)S(1)}, bf16[128,2304]{1,0:T(8,128)(2,1)S(1)}, u32[]{:S(2)}, u32[]{:S(2)}) collective-permute-start(bf16[128,2304]{1,0:T(8,128)(2,1)S(1)} %get-tuple-element.219), channel_id=1, source_target_pairs={{0,2},{1,3},{2,10},{3,11},{4,6},{5,7},{6,14},{7,15},{8,0},{9,1},{1... | collective-permute-start | bytes 1769480 | tf_op jit(solution)/shard_map/ppermute | solution.py:125
  352.8 12.8 %collective-permute-start.21 = (bf16[128,2304]{1,0:T(8,128)(2,1)}, bf16[128,2304]{1,0:T(8,128)(2,1)S(1)}, u32[]{:S(2)}, u32[]{:S(2)}) collective-permute-start(bf16[128,2304]{1,0:T(8,128)(2,1)} %get-tuple-element.218), channel_id=1, source_target_pairs={{0,8},{1,9},{2,0},{3,1},{4,12},{5,13},{6,4},{7,5},{8,16},{9,17},{1... | collective-permute-start | bytes 1769480 | tf_op jit(solution)/shard_map/ppermute | solution.py:125
  353.5 12.1 %collective-permute-start.22 = (bf16[128,2304]{1,0:T(8,128)(2,1)}, bf16[128,2304]{1,0:T(8,128)(2,1)S(1)}, u32[]{:S(2)}, u32[]{:S(2)}) collective-permute-start(bf16[128,2304]{1,0:T(8,128)(2,1)} %get-tuple-element.217), channel_id=1, source_target_pairs={{0,2},{1,3},{2,10},{3,11},{4,6},{5,7},{6,14},{7,15},{8,0},{9,1},{1... | collective-permute-start | bytes 1769480 | tf_op jit(solution)/shard_map/ppermute | solution.py:125
  370.3 8.8 %collective-permute-start.23 = (bf16[128,2304]{1,0:T(8,128)(2,1)S(1)}, bf16[128,2304]{1,0:T(8,128)(2,1)S(1)}, u32[]{:S(2)}, u32[]{:S(2)}) collective-permute-start(bf16[128,2304]{1,0:T(8,128)(2,1)S(1)} %get-tuple-element.180), channel_id=1, source_target_pairs={{0,8},{1,9},{2,0},{3,1},{4,12},{5,13},{6,4},{7,5},{8,16},{9,17},{1... | collective-permute-start | bytes 1769480 | tf_op jit(solution)/shard_map/ppermute | solution.py:125
  371.0 8.7 %collective-permute-start.24 = (bf16[128,2304]{1,0:T(8,128)(2,1)S(1)}, bf16[128,2304]{1,0:T(8,128)(2,1)S(1)}, u32[]{:S(2)}, u32[]{:S(2)}) collective-permute-start(bf16[128,2304]{1,0:T(8,128)(2,1)S(1)} %get-tuple-element.180), channel_id=1, source_target_pairs={{0,2},{1,3},{2,10},{3,11},{4,6},{5,7},{6,14},{7,15},{8,0},{9,1},{1... | collective-permute-start | bytes 1769480 | tf_op jit(solution)/shard_map/ppermute | solution.py:125
  379.8 15.1 %collective-permute-start.25 = (bf16[128,2304]{1,0:T(8,128)(2,1)S(1)}, bf16[128,2304]{1,0:T(8,128)(2,1)S(1)}, u32[]{:S(2)}, u32[]{:S(2)}) collective-permute-start(bf16[128,2304]{1,0:T(8,128)(2,1)S(1)} %collective-permute-done.23), channel_id=1, source_target_pairs={{0,8},{1,9},{2,0},{3,1},{4,12},{5,13},{6,4},{7,5},{8,16},{9,17},{1... | collective-permute-start | bytes 1769480 | tf_op jit(solution)/shard_map/ppermute | solution.py:125
  380.5 14.4 %collective-permute-start.26 = (bf16[128,2304]{1,0:T(8,128)(2,1)S(1)}, bf16[128,2304]{1,0:T(8,128)(2,1)S(1)}, u32[]{:S(2)}, u32[]{:S(2)}) collective-permute-start(bf16[128,2304]{1,0:T(8,128)(2,1)S(1)} %collective-permute-done.24), channel_id=1, source_target_pairs={{0,2},{1,3},{2,10},{3,11},{4,6},{5,7},{6,14},{7,15},{8,0},{9,1},{1... | collective-permute-start | bytes 1769480 | tf_op jit(solution)/shard_map/ppermute | solution.py:125
  394.9 15.9 %collective-permute-start.28 = (bf16[128,2304]{1,0:T(8,128)(2,1)S(1)}, bf16[128,2304]{1,0:T(8,128)(2,1)S(1)}, u32[]{:S(2)}, u32[]{:S(2)}) collective-permute-start(bf16[128,2304]{1,0:T(8,128)(2,1)S(1)} %collective-permute-done.26), channel_id=1, source_target_pairs={{0,2},{1,3},{2,10},{3,11},{4,6},{5,7},{6,14},{7,15},{8,0},{9,1},{1... | collective-permute-start | bytes 1769480 | tf_op jit(solution)/shard_map/ppermute | solution.py:125
  396.5 14.3 %collective-permute-start.27 = (bf16[128,2304]{1,0:T(8,128)(2,1)S(1)}, bf16[128,2304]{1,0:T(8,128)(2,1)S(1)}, u32[]{:S(2)}, u32[]{:S(2)}) collective-permute-start(bf16[128,2304]{1,0:T(8,128)(2,1)S(1)} %collective-permute-done.25), channel_id=1, source_target_pairs={{0,8},{1,9},{2,0},{3,1},{4,12},{5,13},{6,4},{7,5},{8,16},{9,17},{1... | collective-permute-start | bytes 1769480 | tf_op jit(solution)/shard_map/ppermute | solution.py:125
  410.9 7.6 collective-permute-start.29
  411.4 9.1 %collective-permute-start.30 = (bf16[64,2304]{1,0:T(8,128)(2,1)S(1)}, bf16[64,2304]{1,0:T(8,128)(2,1)S(1)}, u32[]{:S(2)}, u32[]{:S(2)}) collective-permute-start(bf16[64,2304]{1,0:T(8,128)(2,1)S(1)} %slice.297), channel_id=1, source_target_pairs={{0,2},{1,3},{2,10},{3,11},{4,6},{5,7},{6,14},{7,15},{8,0},{9,1},{1... | collective-permute-start | bytes 884744 | tf_op jit(solution)/shard_map/ppermute | solution.py:125
  436.0 8.9 %collective-permute-start.31 = (bf16[64,2304]{1,0:T(8,128)(2,1)S(1)}, bf16[64,2304]{1,0:T(8,128)(2,1)S(1)}, u32[]{:S(2)}, u32[]{:S(2)}) collective-permute-start(bf16[64,2304]{1,0:T(8,128)(2,1)S(1)} %get-tuple-element.236), channel_id=1, source_target_pairs={{0,8},{1,9},{2,0},{3,1},{4,12},{5,13},{6,4},{7,5},{8,16},{9,17},{1... | collective-permute-start | bytes 884744 | tf_op jit(solution)/shard_map/ppermute | solution.py:125
  437.0 7.9 collective-permute-start.32
  445.1 21.8 %collective-permute-start.34 = (bf16[128,2304]{1,0:T(8,128)(2,1)S(1)}, bf16[128,2304]{1,0:T(8,128)(2,1)S(1)}, u32[]{:S(2)}, u32[]{:S(2)}) collective-permute-start(bf16[128,2304]{1,0:T(8,128)(2,1)S(1)} %pad_maximum_fusion.18), channel_id=1, source_target_pairs={{0,2},{1,3},{2,10},{3,11},{4,6},{5,7},{6,14},{7,15},{8,0},{9,1},{1... | collective-permute-start | bytes 1769480 | tf_op jit(solution)/shard_map/ppermute | solution.py:125
  446.6 20.4 %collective-permute-start.33 = (bf16[128,2304]{1,0:T(8,128)(2,1)S(1)}, bf16[128,2304]{1,0:T(8,128)(2,1)S(1)}, u32[]{:S(2)}, u32[]{:S(2)}) collective-permute-start(bf16[128,2304]{1,0:T(8,128)(2,1)S(1)} %pad_maximum_fusion.17), channel_id=1, source_target_pairs={{0,8},{1,9},{2,0},{3,1},{4,12},{5,13},{6,4},{7,5},{8,16},{9,17},{1... | collective-permute-start | bytes 1769480 | tf_op jit(solution)/shard_map/ppermute | solution.py:125
  450.2 67.2 %collective-permute-start.58 = (bf16[1152,1152]{1,0:T(8,128)(2,1)S(1)}, bf16[1152,1152]{1,0:T(8,128)(2,1)S(1)}, u32[]{:S(2)}, u32[]{:S(2)}) collective-permute-start(bf16[1152,1152]{1,0:T(8,128)(2,1)S(1)} %convolution_convert_fusion), channel_id=1, source_target_pairs={{0,1},{1,0},{2,3},{3,2},{4,5},{5,4},{6,7},{7,6},{8,9},{9,8},{10,11... | collective-permute-start | bytes 7962632 | tf_op jit(solution)/shard_map/ppermute | solution.py:125
  467.2 12.4 %collective-permute-start.35 = (bf16[128,2304]{1,0:T(8,128)(2,1)S(1)}, bf16[128,2304]{1,0:T(8,128)(2,1)S(1)}, u32[]{:S(2)}, u32[]{:S(2)}) collective-permute-start(bf16[128,2304]{1,0:T(8,128)(2,1)S(1)} %get-tuple-element.216), channel_id=1, source_target_pairs={{0,8},{1,9},{2,0},{3,1},{4,12},{5,13},{6,4},{7,5},{8,16},{9,17},{1... | collective-permute-start | bytes 1769480 | tf_op jit(solution)/shard_map/ppermute | solution.py:125
  468.2 12.6 %collective-permute-start.36 = (bf16[128,2304]{1,0:T(8,128)(2,1)S(1)}, bf16[128,2304]{1,0:T(8,128)(2,1)S(1)}, u32[]{:S(2)}, u32[]{:S(2)}) collective-permute-start(bf16[128,2304]{1,0:T(8,128)(2,1)S(1)} %get-tuple-element.215), channel_id=1, source_target_pairs={{0,2},{1,3},{2,10},{3,11},{4,6},{5,7},{6,14},{7,15},{8,0},{9,1},{1... | collective-permute-start | bytes 1769480 | tf_op jit(solution)/shard_map/ppermute | solution.py:125
  473.5 97.1 %collective-permute-start.50 = (bf16[1152,1152]{1,0:T(8,128)(2,1)}, bf16[1152,1152]{1,0:T(8,128)(2,1)}, u32[]{:S(2)}, u32[]{:S(2)}) collective-permute-start(bf16[1152,1152]{1,0:T(8,128)(2,1)} %convolution_convert_fusion.4), channel_id=1, source_target_pairs={{0,1},{1,0},{2,3},{3,2},{4,5},{5,4},{6,7},{7,6},{8,9},{9,8},{10,11... | collective-permute-start | bytes 7962632 | tf_op jit(solution)/shard_map/ppermute | solution.py:125
  481.1 12.1 %collective-permute-start.37 = (bf16[128,2304]{1,0:T(8,128)(2,1)S(1)}, bf16[128,2304]{1,0:T(8,128)(2,1)S(1)}, u32[]{:S(2)}, u32[]{:S(2)}) collective-permute-start(bf16[128,2304]{1,0:T(8,128)(2,1)S(1)} %get-tuple-element.214), channel_id=1, source_target_pairs={{0,8},{1,9},{2,0},{3,1},{4,12},{5,13},{6,4},{7,5},{8,16},{9,17},{1... | collective-permute-start | bytes 1769480 | tf_op jit(solution)/shard_map/ppermute | solution.py:125
  483.1 12.2 %collective-permute-start.38 = (bf16[128,2304]{1,0:T(8,128)(2,1)S(1)}, bf16[128,2304]{1,0:T(8,128)(2,1)S(1)}, u32[]{:S(2)}, u32[]{:S(2)}) collective-permute-start(bf16[128,2304]{1,0:T(8,128)(2,1)S(1)} %get-tuple-element.213), channel_id=1, source_target_pairs={{0,2},{1,3},{2,10},{3,11},{4,6},{5,7},{6,14},{7,15},{8,0},{9,1},{1... | collective-permute-start | bytes 1769480 | tf_op jit(solution)/shard_map/ppermute | solution.py:125
  497.8 19.6 %collective-permute-start.39 = (bf16[128,2304]{1,0:T(8,128)(2,1)S(1)}, bf16[128,2304]{1,0:T(8,128)(2,1)S(1)}, u32[]{:S(2)}, u32[]{:S(2)}) collective-permute-start(bf16[128,2304]{1,0:T(8,128)(2,1)S(1)} %get-tuple-element.174), channel_id=1, source_target_pairs={{0,1},{1,0},{2,3},{3,2},{4,5},{5,4},{6,7},{7,6},{8,9},{9,8},{10,11... | collective-permute-start | bytes 1769480 | tf_op jit(solution)/shard_map/ppermute | solution.py:125
  501.6 14.8 %collective-permute-start.40 = (bf16[128,2304]{1,0:T(8,128)(2,1)S(1)}, bf16[128,2304]{1,0:T(8,128)(2,1)S(1)}, u32[]{:S(2)}, u32[]{:S(2)}) collective-permute-start(bf16[128,2304]{1,0:T(8,128)(2,1)S(1)} %get-tuple-element.174), channel_id=1, source_target_pairs={{0,2},{1,3},{2,0},{3,1},{4,6},{5,7},{6,4},{7,5},{8,10},{9,11},{10,... | collective-permute-start | bytes 1769480 | tf_op jit(solution)/shard_map/ppermute | solution.py:125
  506.4 116.1 %collective-permute-start.54 = (bf16[1152,1152]{1,0:T(8,128)(2,1)}, bf16[1152,1152]{1,0:T(8,128)(2,1)}, u32[]{:S(2)}, u32[]{:S(2)}) collective-permute-start(bf16[1152,1152]{1,0:T(8,128)(2,1)} %convolution_convert_fusion.2), channel_id=1, source_target_pairs={{0,1},{1,0},{2,3},{3,2},{4,5},{5,4},{6,7},{7,6},{8,9},{9,8},{10,11... | collective-permute-start | bytes 7962632 | tf_op jit(solution)/shard_map/ppermute | solution.py:125
  516.4 3.5 collective-permute-start.41
  519.9 64.2 %collective-permute-start.59 = (bf16[576,1152]{1,0:T(8,128)(2,1)}, bf16[576,1152]{1,0:T(8,128)(2,1)}, u32[]{:S(2)}, u32[]{:S(2)}) collective-permute-start(bf16[576,1152]{1,0:T(8,128)(2,1)} %bitcast.64), channel_id=1, source_target_pairs={{0,4},{1,5},{2,6},{3,7},{4,0},{5,1},{6,2},{7,3},{8,12},{9,13},{10,... | collective-permute-start | bytes 3981320 | tf_op jit(solution)/shard_map/ppermute | solution.py:125
  551.5 14.2 %collective-permute-start.42 = (bf16[256,512]{1,0:T(8,128)(2,1)S(1)}, bf16[256,512]{1,0:T(8,128)(2,1)S(1)}, u32[]{:S(2)}, u32[]{:S(2)}) collective-permute-start(bf16[256,512]{1,0:T(8,128)(2,1)S(1)} %get-tuple-element.200), channel_id=1, source_target_pairs={{0,8},{1,9},{2,10},{3,11},{4,0},{5,1},{6,2},{7,3},{8,16},{9,17},{1... | collective-permute-start | bytes 786440 | tf_op jit(solution)/shard_map/ppermute | solution.py:125
  551.7 14.0 %collective-permute-start.43 = (bf16[256,512]{1,0:T(8,128)(2,1)S(1)}, bf16[256,512]{1,0:T(8,128)(2,1)S(1)}, u32[]{:S(2)}, u32[]{:S(2)}) collective-permute-start(bf16[256,512]{1,0:T(8,128)(2,1)S(1)} %get-tuple-element.201), channel_id=1, source_target_pairs={{0,4},{1,5},{2,6},{3,7},{4,12},{5,13},{6,14},{7,15},{8,0},{9,1},{1... | collective-permute-start | bytes 786440 | tf_op jit(solution)/shard_map/ppermute | solution.py:125
  567.0 13.1 %collective-permute-start.45 = (bf16[512,512]{1,0:T(8,128)(2,1)S(1)}, bf16[512,512]{1,0:T(8,128)(2,1)}, u32[]{:S(2)}, u32[]{:S(2)}) collective-permute-start(bf16[512,512]{1,0:T(8,128)(2,1)S(1)} %pad_maximum_fusion.22), channel_id=1, source_target_pairs={{0,4},{1,5},{2,6},{3,7},{4,12},{5,13},{6,14},{7,15},{8,0},{9,1},{1... | collective-permute-start | bytes 1572872 | tf_op jit(solution)/shard_map/ppermute | solution.py:125
  567.9 13.2 %collective-permute-start.44 = (bf16[512,512]{1,0:T(8,128)(2,1)}, bf16[512,512]{1,0:T(8,128)(2,1)}, u32[]{:S(2)}, u32[]{:S(2)}) collective-permute-start(bf16[512,512]{1,0:T(8,128)(2,1)} %pad_maximum_fusion.21), channel_id=1, source_target_pairs={{0,8},{1,9},{2,10},{3,11},{4,0},{5,1},{6,2},{7,3},{8,16},{9,17},{1... | collective-permute-start | bytes 1572872 | tf_op jit(solution)/shard_map/ppermute | solution.py:125
  573.9 54.6 %collective-permute-start.51 = (bf16[576,1152]{1,0:T(8,128)(2,1)S(1)}, bf16[576,1152]{1,0:T(8,128)(2,1)S(1)}, u32[]{:S(2)}, u32[]{:S(2)}) collective-permute-start(bf16[576,1152]{1,0:T(8,128)(2,1)S(1)} %bitcast.205), channel_id=1, source_target_pairs={{0,4},{1,5},{2,6},{3,7},{4,0},{5,1},{6,2},{7,3},{8,12},{9,13},{10,... | collective-permute-start | bytes 3981320 | tf_op jit(solution)/shard_map/ppermute | solution.py:125
  582.6 38.1 %collective-permute-start.46 = (bf16[512,512]{1,0:T(8,128)(2,1)S(1)}, bf16[512,512]{1,0:T(8,128)(2,1)S(1)}, u32[]{:S(2)}, u32[]{:S(2)}) collective-permute-start(bf16[512,512]{1,0:T(8,128)(2,1)S(1)} %get-tuple-element.198), channel_id=1, source_target_pairs={{0,8},{1,9},{2,10},{3,11},{4,0},{5,1},{6,2},{7,3},{8,16},{9,17},{1... | collective-permute-start | bytes 1572872 | tf_op jit(solution)/shard_map/ppermute | solution.py:125
  583.8 38.3 %collective-permute-start.47 = (bf16[512,512]{1,0:T(8,128)(2,1)S(1)}, bf16[512,512]{1,0:T(8,128)(2,1)S(1)}, u32[]{:S(2)}, u32[]{:S(2)}) collective-permute-start(bf16[512,512]{1,0:T(8,128)(2,1)S(1)} %get-tuple-element.197), channel_id=1, source_target_pairs={{0,4},{1,5},{2,6},{3,7},{4,12},{5,13},{6,14},{7,15},{8,0},{9,1},{1... | collective-permute-start | bytes 1572872 | tf_op jit(solution)/shard_map/ppermute | solution.py:125
  586.1 43.8 %collective-permute-start.60 = (bf16[288,1152]{1,0:T(8,128)(2,1)S(1)}, bf16[288,1152]{1,0:T(8,128)(2,1)S(1)}, u32[]{:S(2)}, u32[]{:S(2)}) collective-permute-start(bf16[288,1152]{1,0:T(8,128)(2,1)S(1)} %get-tuple-element.250), channel_id=1, source_target_pairs={{9,0},{25,1},{11,2},{27,3},{13,4},{29,5},{15,6},{31,7},{1,8},{17,9... | collective-permute-start | bytes 1990664 | tf_op jit(solution)/shard_map/ppermute | solution.py:125
  620.7 12.2 %collective-permute-start.61 = (bf16[288,1152]{1,0:T(8,128)(2,1)S(1)}, bf16[288,1152]{1,0:T(8,128)(2,1)S(1)}, u32[]{:S(2)}, u32[]{:S(2)}) collective-permute-start(bf16[288,1152]{1,0:T(8,128)(2,1)S(1)} %get-tuple-element.249), channel_id=1, source_target_pairs={{1,0},{17,1},{3,2},{19,3},{5,4},{21,5},{7,6},{23,7},{9,8},{25,9},{... | collective-permute-start | bytes 1990664 | tf_op jit(solution)/shard_map/ppermute | solution.py:125
  622.4 16.7 %collective-permute-start.48 = (bf16[512,512]{1,0:T(8,128)(2,1)S(1)}, bf16[512,512]{1,0:T(8,128)(2,1)S(1)}, u32[]{:S(2)}, u32[]{:S(2)}) collective-permute-start(bf16[512,512]{1,0:T(8,128)(2,1)S(1)} %get-tuple-element.196), channel_id=1, source_target_pairs={{0,8},{1,9},{2,10},{3,11},{4,0},{5,1},{6,2},{7,3},{8,16},{9,17},{1... | collective-permute-start | bytes 1572872 | tf_op jit(solution)/shard_map/ppermute | solution.py:125
  622.5 27.7 %collective-permute-start.49 = (bf16[512,512]{1,0:T(8,128)(2,1)S(1)}, bf16[512,512]{1,0:T(8,128)(2,1)S(1)}, u32[]{:S(2)}, u32[]{:S(2)}) collective-permute-start(bf16[512,512]{1,0:T(8,128)(2,1)S(1)} %get-tuple-element.195), channel_id=1, source_target_pairs={{0,4},{1,5},{2,6},{3,7},{4,12},{5,13},{6,14},{7,15},{8,0},{9,1},{1... | collective-permute-start | bytes 1572872 | tf_op jit(solution)/shard_map/ppermute | solution.py:125
  628.4 129.4 %collective-permute-start.55 = (bf16[576,1152]{1,0:T(8,128)(2,1)}, bf16[576,1152]{1,0:T(8,128)(2,1)}, u32[]{:S(2)}, u32[]{:S(2)}) collective-permute-start(bf16[576,1152]{1,0:T(8,128)(2,1)} %bitcast.57), channel_id=1, source_target_pairs={{0,4},{1,5},{2,6},{3,7},{4,0},{5,1},{6,2},{7,3},{8,12},{9,13},{10,... | collective-permute-start | bytes 3981320 | tf_op jit(solution)/shard_map/ppermute | solution.py:125
  629.9 130.0 %collective-permute-start.52 = (bf16[288,1152]{1,0:T(8,128)(2,1)}, bf16[288,1152]{1,0:T(8,128)(2,1)}, u32[]{:S(2)}, u32[]{:S(2)}) collective-permute-start(bf16[288,1152]{1,0:T(8,128)(2,1)} %get-tuple-element.258), channel_id=1, source_target_pairs={{9,0},{25,1},{11,2},{27,3},{13,4},{29,5},{15,6},{31,7},{1,8},{17,9... | collective-permute-start | bytes 1990664 | tf_op jit(solution)/shard_map/ppermute | solution.py:125
  632.9 127.1 %collective-permute-start.53 = (bf16[288,1152]{1,0:T(8,128)(2,1)}, bf16[288,1152]{1,0:T(8,128)(2,1)}, u32[]{:S(2)}, u32[]{:S(2)}) collective-permute-start(bf16[288,1152]{1,0:T(8,128)(2,1)} %get-tuple-element.257), channel_id=1, source_target_pairs={{1,0},{17,1},{3,2},{19,3},{5,4},{21,5},{7,6},{23,7},{9,8},{25,9},{... | collective-permute-start | bytes 1990664 | tf_op jit(solution)/shard_map/ppermute | solution.py:125
  759.8 17.9 %collective-permute-start.56 = (bf16[288,1152]{1,0:T(8,128)(2,1)S(1)}, bf16[288,1152]{1,0:T(8,128)(2,1)S(1)}, u32[]{:S(2)}, u32[]{:S(2)}) collective-permute-start(bf16[288,1152]{1,0:T(8,128)(2,1)S(1)} %get-tuple-element.254), channel_id=1, source_target_pairs={{9,0},{25,1},{11,2},{27,3},{13,4},{29,5},{15,6},{31,7},{1,8},{17,9... | collective-permute-start | bytes 1990664 | tf_op jit(solution)/shard_map/ppermute | solution.py:125
  759.9 31.5 %collective-permute-start.57 = (bf16[288,1152]{1,0:T(8,128)(2,1)S(1)}, bf16[288,1152]{1,0:T(8,128)(2,1)S(1)}, u32[]{:S(2)}, u32[]{:S(2)}) collective-permute-start(bf16[288,1152]{1,0:T(8,128)(2,1)S(1)} %get-tuple-element.253), channel_id=1, source_target_pairs={{1,0},{17,1},{3,2},{19,3},{5,4},{21,5},{7,6},{23,7},{9,8},{25,9},{... | collective-permute-start | bytes 1990664 | tf_op jit(solution)/shard_map/ppermute | solution.py:125
  (98 other events, 1065.2 us)
